TPU v7x, 8 devices: a whole 2x2x1 slice. The times are simulated.
8 devices in a mesh: replica: 1 (over z), data: 2 (over y), model: 4 (over x, core).
Axes of the slice: x: 2, y: 2, z: 1, core: 2. Of those that a mesh axis runs over, the one named last changes fastest.
Arguments:
- x_in: bfloat16 [16384, 512], P(('replica', 'data'))
- w_in: bfloat16 [512, 512], P(('replica', 'model'))
- w_mid: bfloat16 [512, 512], P(('replica', 'model'))
- w_out: bfloat16 [512, 512], P(('replica', 'model'))
- u_in: float32 [512], P(('replica', 'model'))
- u_mid: float32 [512], P(('replica', 'model'))
- u_out: float32 [512], P(('replica', 'model'))
- target: bfloat16 [16384, 512], P(('replica', 'data'), 'model')
Outputs:
- output 1: float32 [1], P('replica')
- output 2: bfloat16 [16384, 512], P(('replica', 'data'))
- output 3: float32 [512, 512], P(('replica', 'model'))
- output 4: float32 [512, 512], P(('replica', 'model'))
- output 5: float32 [512, 512], P(('replica', 'model'))
- output 6: float32 [512], P(('replica', 'model'))
- output 7: float32 [512], P(('replica', 'model'))
- output 8: float32 [512], P(('replica', 'model'))
- output 9: float32 [512], P('replica')
- output 10: float32 [512], P('replica')
- output 11: float32 [512], P('replica')
- output 12: float32 [3], P('replica')
All inputs are finite; a program needn't handle non-finite values.
Results may differ from a plain program's by a relative error of at most 0.0166482.
Values are sent between devices in bfloat16 or wider.
A program may use at most 1 GiB of HBM per device.

v0:
```python
import jax
import jax.numpy as jnp
from jax import lax
from jax.sharding import PartitionSpec as P

MATVEC_PRECISION = lax.Precision.HIGHEST


def solution(mesh):
    data_size = mesh.shape["data"]
    row_spec = P(("replica", "model"), None)
    vec_spec = P(("replica", "model"))
    batch_spec = P(("replica", "data"), None)
    target_spec = P(("replica", "data"), "model")
    part_spec = P("replica")

    def local_step(x_in, w_in, w_mid, w_out, u_in, u_mid, u_out, target):
        batch_total = x_in.shape[0] * data_size
        weights = [w_in, w_mid, w_out]
        u_vecs = [u_in, u_mid, u_out]
        saved_in = []
        saved_out = []
        layer_stats = []
        for layer_idx in range(3):
            weight = weights[layer_idx]
            partial_p = jnp.dot(u_vecs[layer_idx], weight, preferred_element_type=jnp.float32, precision=MATVEC_PRECISION)
            p_vec = lax.psum(partial_p, "model")
            v_vec = p_vec / jnp.maximum(jnp.sqrt(jnp.sum(p_vec * p_vec)), 1e-12)
            s_vec = jnp.dot(weight, v_vec, preferred_element_type=jnp.float32, precision=MATVEC_PRECISION)
            sigma_val = jnp.sqrt(lax.psum(jnp.sum(s_vec * s_vec), "model"))
            if layer_idx == 0:
                layer_in = x_in
            else:
                own_act = jax.nn.leaky_relu(saved_out[-1], 0.2).astype(jnp.bfloat16)
                layer_in = lax.all_gather(own_act, "model", axis=1, tiled=True)
            y_val = jnp.einsum("bi,oi->bo", layer_in, weight, preferred_element_type=jnp.float32) / sigma_val
            saved_in.append(layer_in)
            saved_out.append(y_val)
            layer_stats.append((s_vec / sigma_val, v_vec, sigma_val))
        residual = saved_out[2] - target.astype(jnp.float32)
        loss_val = 0.5 / batch_total * lax.psum(jnp.sum(residual * residual), ("data", "model"))
        grad_y = residual / batch_total
        grads_w = [None, None, None]
        for layer_idx in (2, 1, 0):
            weight = weights[layer_idx]
            u_next, v_vec, sigma_val = layer_stats[layer_idx]
            grad_b = grad_y.astype(jnp.bfloat16)
            corr_sum = lax.psum(jnp.sum(grad_y * saved_out[layer_idx]), ("data", "model"))
            g_part = jnp.einsum("bo,bi->oi", grad_b, saved_in[layer_idx], preferred_element_type=jnp.float32)
            g_mat = lax.psum(g_part, "data")
            grads_w[layer_idx] = g_mat / sigma_val - (corr_sum / sigma_val) * (u_next[:, None] * v_vec[None, :])
            x_part = (jnp.dot(grad_b, weight, preferred_element_type=jnp.float32) / sigma_val).astype(jnp.bfloat16)
            if layer_idx > 0:
                own_grad = lax.psum_scatter(x_part, "model", scatter_dimension=1, tiled=True)
                grad_y = own_grad.astype(jnp.float32) * jnp.where(saved_out[layer_idx - 1] > 0, 1.0, 0.2)
            else:
                grad_x = lax.psum(x_part, "model")
        return (loss_val.reshape(1), grad_x, grads_w[0], grads_w[1], grads_w[2],
                layer_stats[0][0], layer_stats[1][0], layer_stats[2][0],
                layer_stats[0][1], layer_stats[1][1], layer_stats[2][1],
                jnp.stack([layer_stats[0][2], layer_stats[1][2], layer_stats[2][2]]))

    in_specs = (batch_spec, row_spec, row_spec, row_spec, vec_spec, vec_spec, vec_spec, target_spec)
    out_specs = (part_spec, batch_spec, row_spec, row_spec, row_spec, vec_spec, vec_spec, vec_spec, part_spec, part_spec, part_spec, part_spec)
    return jax.shard_map(local_step, mesh=mesh, in_specs=in_specs, out_specs=out_specs, check_vma=False)
```

profile of v0, /device:TPU:0, one launch (start us, length us, event | category | flops | bytes accessed | tf_op | source)
XLA Modules:
  0.0 547.3 jit_solution(15682456121506623452)
XLA Ops:
  7.2 0.0 copy-start
  7.2 0.0 all-gather.3.cloned.1.call-start
  7.2 1.1 fusion.8
  8.3 0.0 copy-done
  8.3 0.8 fusion.6
  9.2 1.1 fusion.4
  10.3 8.9 %all-reduce.2 = (f32[512]{0:T(512)S(1)}, f32[512]{0:T(512)S(1)}, f32[512]{0:T(512)S(1)}) all-reduce(f32[512]{0:T(512)S(1)} %bitcast.57, f32[512]{0:T(512)S(1)} %bitcast.58, f32[512]{0:T(512)S(1)} %bitcast.59), channel_id=1, replica_groups=mesh['replica'=1,'data'=2,'model'=4] {'model'}, use_global_device_ids=true, to_apply=%region_0.0 | all-reduce | flops 1536 | bytes 12288 | tf_op jit(solution)/shard_map/psum | solution.py:27
  19.1 0.6 multiply_reduce_fusion.6
  20.4 0.0 copy-start.9
  20.4 1.7 multiply_reduce_fusion.9
  22.2 0.6 multiply_reduce_fusion.4
  24.2 0.0 copy-start.10
  24.2 0.0 copy-start.11
  24.2 1.7 multiply_reduce_fusion.7
  25.9 0.8 multiply_reduce_fusion.8
  26.8 6.4 %all-reduce.1 = (f32[]{:T(128)}, f32[]{:T(128)}, f32[]{:T(128)}) all-reduce(f32[]{:T(128)} %get-tuple-element.27, f32[]{:T(128)} %get-tuple-element.29, f32[]{:T(128)} %get-tuple-element.31), channel_id=1, replica_groups=mesh['replica'=1,'data'=2,'model'=4] {'model'}, use_global_device_ids=true, to_apply=%region_3.0 | all-reduce | flops 3 | bytes 24 | tf_op jit(solution)/shard_map/psum | solution.py:30
  33.8 8.4 %fusion = (bf16[8192,128]{1,0:T(8,128)(2,1)}, f32[8192,128]{1,0:T(8,128)}) fusion(f32[]{:T(128)} %sqrt.19, bf16[8192,512]{1,0:T(8,128)(2,1)} %param.8, bf16[128,512]{1,0:T(8,128)(2,1)} %param.9), kind=kOutput, calls=%fused_computation.8 | convolution fusion | flops 1078984704 | bytes 14811140 | tf_op jit(solution)/shard_map/bi,oi->bo/dot_general | solution.py:36
  42.3 0.0 all-gather.3.cloned.1.call-update
  42.3 0.0 all-gather.5.cloned.1.call-start
  43.0 0.0 copy-start.6
  43.0 0.0 copy-start.7
  43.0 56.4 %all-gather.3.cloned.1.call-done = bf16[8192,512]{1,0:T(8,128)(2,1)} async-done(((bf16[8192,128]{1,0:T(8,128)(2,1)}), bf16[8192,512]{1,0:T(8,128)(2,1)}) %all-gather.3.cloned.1.call-update) | async-done | bytes 8388624 | tf_op jit(solution)/shard_map/all_gather | solution.py:35
  99.4 8.4 %fusion.1 = (bf16[8192,128]{1,0:T(8,128)(2,1)}, f32[8192,128]{1,0:T(8,128)}) fusion(f32[]{:T(128)} %sqrt.21, bf16[8192,512]{1,0:T(8,128)(2,1)} %all-gather.3.cloned.1.call-done, bf16[128,512]{1,0:T(8,128)(2,1)S(1)} %copy-done), kind=kOutput, calls=%fused_computation.9 | convolution fusion | flops 1078984704 | bytes 14811140 | tf_op jit(solution)/shard_map/bi,oi->bo/dot_general | solution.py:36
  107.8 0.0 all-gather.5.cloned.1.call-update
  107.9 0.0 reduce-scatter.7.cloned.1.call-start
  108.6 56.3 %all-gather.5.cloned.1.call-done = bf16[8192,512]{1,0:T(8,128)(2,1)} async-done(((bf16[8192,128]{1,0:T(8,128)(2,1)}), bf16[8192,512]{1,0:T(8,128)(2,1)}) %all-gather.5.cloned.1.call-update) | async-done | bytes 8388624 | tf_op jit(solution)/shard_map/all_gather | solution.py:35
  164.9 0.0 copy-done.6
  164.9 0.0 copy-done.7
  164.9 6.3 %multiply_reduce_fusion = (f32[]{:T(128)}, f32[]{:T(128)}, f32[8192,128]{1,0:T(8,128)S(1)}) fusion(bf16[8192,128]{1,0:T(8,128)(2,1)S(1)} %copy-done.6, f32[]{:T(128)} %sqrt.23, bf16[8192,512]{1,0:T(8,128)(2,1)} %all-gather.5.cloned.1.call-done, bf16[128,512]{1,0:T(8,128)(2,1)S(1)} %copy-done.7), kind=kOutput, calls=%fused_computation.10 | convolution fusion | flops 1082130432 | bytes 14811148 | tf_op jit(solution)/shard_map/bi,oi->bo/dot_general | solution.py:36
  171.2 2.0 copy-done.5
  173.3 4.6 divide_convert_fusion.2
  177.9 11.3 %copy.20 = bf16[8192,512]{0,1:T(8,128)(2,1)} copy(bf16[8192,512]{1,0:T(8,128)(2,1)} %divide_convert_fusion.2) | data formatting | bytes 16777216
  189.2 0.0 reduce-scatter.7.cloned.1.call-update
  189.2 0.0 reduce-scatter.9.cloned.1.call-start
  189.2 65.2 %reduce-scatter.7.cloned.1.call-done = bf16[128,8192]{1,0:T(8,128)(2,1)} async-done(((bf16[512,8192]{1,0:T(8,128)(2,1)}), bf16[128,8192]{1,0:T(8,128)(2,1)}) %reduce-scatter.7.cloned.1.call-update) | async-done | bytes 2097168
  254.4 3.2 copy.21
  257.6 6.9 %divide_convert_fusion.1 = bf16[8192,512]{1,0:T(8,128)(2,1)} fusion(bf16[128,512]{1,0:T(8,128)(2,1)S(1)} %copy-done, f32[]{:T(128)} %sqrt.21, bf16[8192,128]{1,0:T(8,128)(2,1)S(1)} %copy.21, f32[8192,128]{1,0:T(8,128)} %get-tuple-element.36), kind=kOutput, calls=%fused_computation.1 | convolution fusion | flops 1087373312 | bytes 14811140 | tf_op jit(solution)/shard_map/dot_general | solution.py:52
  264.5 11.3 %copy.22 = bf16[8192,512]{0,1:T(8,128)(2,1)} copy(bf16[8192,512]{1,0:T(8,128)(2,1)} %divide_convert_fusion.1) | data formatting | bytes 16777216
  275.8 0.0 reduce-scatter.9.cloned.1.call-update
  275.8 0.2 all-reduce.9.cloned.1.call-start
  276.0 7.4 %fusion.10 = f32[128,512]{1,0:T(8,128)} fusion(bf16[8192,512]{1,0:T(8,128)(2,1)} %all-gather.5.cloned.1.call-done, f32[8192,128]{1,0:T(8,128)} %copy-done.5, bf16[8192,128]{1,0:T(8,128)(2,1)} %param.15), kind=kOutput, calls=%fused_computation.45 | convolution fusion | flops 1077936128 | bytes 14942208 | tf_op jit(solution)/shard_map/bo,bi->oi/dot_general | solution.py:49
  283.5 5.6 %fusion.11 = f32[128,512]{1,0:T(8,128)} fusion(bf16[8192,512]{1,0:T(8,128)(2,1)} %all-gather.3.cloned.1.call-done, bf16[8192,128]{1,0:T(8,128)(2,1)S(1)} %copy.21, f32[8192,128]{1,0:T(8,128)S(1)} %copy-done.4), kind=kOutput, calls=%fused_computation.46 | convolution fusion | flops 1078984704 | bytes 14942208 | tf_op jit(solution)/shard_map/bo,bi->oi/dot_general | solution.py:49
  289.1 52.0 %reduce-scatter.9.cloned.1.call-done = bf16[128,8192]{1,0:T(8,128)(2,1)} async-done(((bf16[512,8192]{1,0:T(8,128)(2,1)}), bf16[128,8192]{1,0:T(8,128)(2,1)}) %reduce-scatter.9.cloned.1.call-update) | async-done | bytes 2097168
  341.1 4.1 copy.23
  345.1 7.3 %fusion.14 = f32[128,512]{1,0:T(8,128)} fusion(bf16[8192,512]{1,0:T(8,128)(2,1)} %param.8, bf16[8192,128]{1,0:T(8,128)(2,1)} %copy.23, f32[8192,128]{1,0:T(8,128)} %get-tuple-element.34), kind=kOutput, calls=%fused_computation.47 | convolution fusion | flops 1078984704 | bytes 14942208 | tf_op jit(solution)/shard_map/bo,bi->oi/dot_general | solution.py:49
  352.5 0.0 all-reduce.9.cloned.1.call-update
  352.5 0.0 all-reduce.7.cloned.1.call-start
  352.6 7.5 %divide_convert_fusion = bf16[8192,512]{1,0:T(8,128)(2,1)} fusion(bf16[128,512]{1,0:T(8,128)(2,1)S(1)} %copy-done.8, f32[]{:T(128)} %sqrt.19, bf16[8192,128]{1,0:T(8,128)(2,1)} %copy.23, f32[8192,128]{1,0:T(8,128)} %get-tuple-element.34), kind=kOutput, calls=%fused_computation | convolution fusion | flops 1087373312 | bytes 14811140 | tf_op jit(solution)/shard_map/dot_general | solution.py:52
  360.1 0.0 all-reduce.7.cloned.1.call-update
  360.1 0.0 copy-start.2
  360.1 0.0 copy-start.3
  360.1 0.6 pad_maximum_fusion
  360.7 0.0 copy-start.13
  360.8 0.0 copy-start.14
  360.8 4.3 multiply_reduce_fusion.1
  365.0 1.8 multiply_reduce_fusion.2
  366.8 22.9 %all-reduce = (f32[]{:T(128)}, f32[]{:T(128)}, f32[]{:T(128)}, f32[]{:T(128)}) all-reduce(f32[]{:T(128)} %get-tuple-element.13, f32[]{:T(128)} %multiply_reduce_fusion.2, f32[]{:T(128)} %multiply_reduce_fusion.1, f32[]{:T(128)} %get-tuple-element.12), channel_id=1, replica_groups=mesh['replica'=1,'data'=2,'model'=4] {'data','model'}, use_global_device_ids=true, to_apply=%region_13.14 | all-reduce | flops 4 | bytes 32 | tf_op jit(solution)/shard_map/psum | solution.py:41
  392.2 0.0 all-reduce.9.cloned.1.call-done
  392.2 1.8 multiply_subtract_fusion.2
  394.0 1.8 multiply_subtract_fusion.1
  395.7 1.8 multiply_subtract_fusion
  397.5 134.4 %all-reduce.7.cloned.1.call-done = bf16[8192,512]{1,0:T(8,128)(2,1)} async-done(((bf16[8192,512]{1,0:T(8,128)(2,1)}), bf16[8192,512]{1,0:T(8,128)(2,1)}) %all-reduce.7.cloned.1.call-update) | async-done | bytes 8388624 | tf_op jit(solution)/shard_map/psum | solution.py:57
  531.9 7.4 %copy.28 = bf16[8192,512]{1,0:T(8,128)(2,1)} copy(bf16[8192,512]{1,0:T(8,128)(2,1)} %all-reduce.7.cloned.1.call-done) | data formatting | bytes 16777216
  539.3 0.0 copy-done.1
  (21 shorter events, 0.1 us)
Async XLA Ops:
  7.2 1.2 copy-start
  7.2 92.2 %all-gather.3.cloned.1.call-start = ((), (), s32[]{:S(2)}) async-start(), calls=%async_computation.2 | async-start | bytes 10485760 | tf_op jit(solution)/shard_map/all_gather | solution.py:35
  20.4 371.8 %copy-start.9 = (f32[512]{0:T(512)}, f32[512]{0:T(512)S(1)}, u32[]{:S(2)}) copy-start(f32[512]{0:T(512)S(1)} %broadcast_divide_fusion.2) | copy-start | bytes 6148
  24.2 371.6 %copy-start.10 = (f32[512]{0:T(512)}, f32[512]{0:T(512)S(1)}, u32[]{:S(2)}) copy-start(f32[512]{0:T(512)S(1)} %broadcast_divide_fusion) | copy-start | bytes 6148
  24.2 369.8 %copy-start.11 = (f32[512]{0:T(512)}, f32[512]{0:T(512)S(1)}, u32[]{:S(2)}) copy-start(f32[512]{0:T(512)S(1)} %broadcast_divide_fusion.1) | copy-start | bytes 6148
  42.3 122.6 %all-gather.5.cloned.1.call-start = ((), (), s32[]{:S(2)}) async-start(), calls=%async_computation.3 | async-start | bytes 10485760 | tf_op jit(solution)/shard_map/all_gather | solution.py:35
  43.0 121.8 %copy-start.6 = (bf16[8192,128]{1,0:T(8,128)(2,1)S(1)}, bf16[8192,128]{1,0:T(8,128)(2,1)}, u32[]{:S(2)}) copy-start(bf16[8192,128]{1,0:T(8,128)(2,1)} %param.15) | copy-start | bytes 6291460
  43.0 121.8 %copy-start.7 = (bf16[128,512]{1,0:T(8,128)(2,1)S(1)}, bf16[128,512]{1,0:T(8,128)(2,1)}, u32[]{:S(2)}) copy-start(bf16[128,512]{1,0:T(8,128)(2,1)} %param.11) | copy-start | bytes 393220
  107.9 146.6 %reduce-scatter.7.cloned.1.call-start = ((), (), s32[]{:S(2)}) async-start(), calls=%async_computation.5 | async-start | bytes 10485760
  171.2 2.0 copy-start.5
  189.2 151.9 %reduce-scatter.9.cloned.1.call-start = ((), (), s32[]{:S(2)}) async-start(), calls=%async_computation.6 | async-start | bytes 10485760
  275.8 116.4 %all-reduce.9.cloned.1.call-start = ((), (), s32[]{:S(2)}) async-start(), calls=%async_computation.7 | async-start | bytes 1572864 | tf_op jit(solution)/shard_map/psum | solution.py:50
  276.0 7.4 %copy-start.4 = (f32[8192,128]{1,0:T(8,128)S(1)}, f32[8192,128]{1,0:T(8,128)}, u32[]{:S(2)}) copy-start(f32[8192,128]{1,0:T(8,128)} %get-tuple-element.36) | copy-start | bytes 12582916
  345.1 7.4 %copy-start.8 = (bf16[128,512]{1,0:T(8,128)(2,1)S(1)}, bf16[128,512]{1,0:T(8,128)(2,1)}, u32[]{:S(2)}) copy-start(bf16[128,512]{1,0:T(8,128)(2,1)} %param.9) | copy-start | bytes 393220
  352.5 179.4 %all-reduce.7.cloned.1.call-start = ((), (), s32[]{:S(2)}) async-start(), calls=%async_computation.4 | async-start | bytes 16777216 | tf_op jit(solution)/shard_map/psum | solution.py:57
  360.1 4.9 copy-start.2
  360.1 4.9 copy-start.3
  360.7 31.5 %copy-start.12 = (f32[128]{0:T(128)}, f32[128]{0:T(128)S(1)}, u32[]{:S(2)}) copy-start(f32[128]{0:T(128)S(1)} %broadcast_divide_fusion.5) | copy-start | bytes 1540
  360.7 33.3 %copy-start.13 = (f32[128]{0:T(128)}, f32[128]{0:T(128)S(1)}, u32[]{:S(2)}) copy-start(f32[128]{0:T(128)S(1)} %broadcast_divide_fusion.4) | copy-start | bytes 1540
  360.8 35.0 %copy-start.14 = (f32[128]{0:T(128)}, f32[128]{0:T(128)S(1)}, u32[]{:S(2)}) copy-start(f32[128]{0:T(128)S(1)} %broadcast_divide_fusion.3) | copy-start | bytes 1540
  531.9 7.4 %copy-start.1 = (bf16[128,512]{1,0:T(8,128)(2,1)S(1)}, bf16[128,512]{1,0:T(8,128)(2,1)}, u32[]{:S(2)}) copy-start(bf16[128,512]{1,0:T(8,128)(2,1)} %param.10) | copy-start | bytes 393220
Sparse Core Ops, SparseCore 0:
  42.4 56.9 all-gather.2
  108.0 56.8 all-gather.4
  189.3 65.0 reduce-scatter.6
  275.9 65.0 reduce-scatter.8
  352.6 29.0 all-reduce.8
  384.6 147.2 all-reduce.6
where the time goes:
time: 549 us; the launch traced here: 547 us
  waiting for transfers between devices  364 us (66%)
  matrix products  69.9 us (13%)
  local copies, waits for them, and re-layouts  39.3 us (7%)
  blocking collectives  38.1 us (7%)
  between operations  22.1 us (4%)
  other arithmetic  13.1 us (2%)
    psum x1, waiting for transfers between devices, local_step(): grad_x = lax.psum(x_part, 'model')  134 us
    unnamed x8, waiting for transfers between devices  117 us
    all_gather x2, waiting for transfers between devices, local_step(): layer_in = lax.all_gather(own_act, 'model', axis=1, tiled=True)  113 us
    unnamed x35, local copies, waits for them, and re-layouts  39.3 us
    dot_general x3, matrix products, local_step(): jnp.einsum('bi,oi->bo', layer_in, weight, preferred_element_type=jnp.floa...  23.2 us
    psum x1, blocking collectives, local_step(): lax.psum(jnp.sum(residual * residual), ('data', 'model'))  22.9 us
    dot_general x3, matrix products, local_step(): jnp.einsum('bo,bi->oi', grad_b, saved_in[layer_idx], preferred_element_ty...  20.4 us
    dot_general x3, matrix products, local_step(): jnp.dot(grad_b, weight, preferred_element_type=jnp.float32) / sigma_val  19 us
  transfers between devices with their start and end apart: 6, of which 5 were waited for; matrix products, arithmetic and copies ran while one was open for 6% of the time, Pallas kernels for 0%

commit v1 on v0

v1 whole, which is shorter than its diff:
```python
import functools

import jax
import jax.numpy as jnp
from jax import lax
from jax.experimental import pallas as pl
from jax.experimental.pallas import tpu as pltpu
from jax.sharding import PartitionSpec as P

MESH = pl.DeviceIdType.MESH
F32 = jnp.float32
BF16 = jnp.bfloat16
NT = 16


def dot_nt(lhs, rhs):
    return lax.dot_general(lhs, rhs, (((1,), (1,)), ((), ())), preferred_element_type=F32)


def dot_nn(lhs, rhs):
    return lax.dot_general(lhs, rhs, (((1,), (0,)), ((), ())), preferred_element_type=F32)


def dot_tn(lhs, rhs):
    return lax.dot_general(lhs, rhs, (((0,), (0,)), ((), ())), preferred_element_type=F32)


def split_rows(vec):
    width = vec.shape[1]
    high = vec.astype(BF16).astype(F32)
    rest = vec - high
    mid = rest.astype(BF16).astype(F32)
    low = rest - mid
    row = lax.broadcasted_iota(jnp.int32, (16, width), 0)
    stacked = jnp.where(row == 0, high, jnp.where(row == 1, mid, jnp.where(row == 2, low, 0.0)))
    return stacked.astype(BF16)


def main_kernel(inv_batch, x_hbm, w0_hbm, w1_hbm, w2_hbm, u0_hbm, u1_hbm, u2_hbm, t_hbm,
                e_out, w_out, dw_out, v0_out, v1_out, v2_out, n0_out, n1_out, n2_out, sig_out,
                x0, x1, x2, y0, y1, y2, tbuf, wbuf, ubuf, ebuf, estage, acc, rbuf, stat, rstat, sstat, srow,
                w_send, w_recv, u_send, u_recv, t_send, t_recv, e_send, e_recv, d_send, d_recv,
                l_w, l_u, l_t, l_x, l_e, l_o):
    rep, dat, mod = lax.axis_index("replica"), lax.axis_index("data"), lax.axis_index("model")
    core = lax.rem(mod, 2)
    chip = mod // 2
    sib = mod + 1 - 2 * core
    cnt = lax.rem(mod + 2, 4)
    crs = lax.rem(sib + 2, 4)
    peers = [(rep, dat, sib), (rep, dat, cnt), (rep, dat, crs)]
    rows_own = x0.shape[0]
    chunk = rows_own // NT
    row_base = core * rows_own
    w_hbm = [w0_hbm, w1_hbm, w2_hbm]
    u_hbm = [u0_hbm, u1_hbm, u2_hbm]
    xs = [x0, x1, x2]
    ys = [y0, y1, y2]
    v_outs = [v0_out, v1_out, v2_out]
    n_outs = [n0_out, n1_out, n2_out]

    def remote(src, dst, ssem, rsem, peer):
        return pltpu.make_async_remote_copy(src_ref=src, dst_ref=dst, send_sem=ssem, recv_sem=rsem,
                                            device_id=peer, device_id_type=MESH)

    def wrow(idx):
        return pl.ds(pl.multiple_of(idx * 128, 128), 128)

    def w_copy(layer, kind):
        if kind == 2:
            src = wbuf.at[layer, wrow(cnt)]
            return remote(src, src, w_send.at[layer, 2], w_recv.at[layer, 2], peers[0])
        return remote(w_hbm[layer], wbuf.at[layer, wrow(mod)], w_send.at[layer, kind], w_recv.at[layer, kind], peers[kind])

    def u_copy(layer, kind):
        return remote(u_hbm[layer], ubuf.at[layer, mod], u_send.at[layer, kind], u_recv.at[layer, kind], peers[kind])

    def t_copy(kind, c):
        other_core = core if kind == 1 else 1 - core
        src = t_hbm.at[pl.ds(pl.multiple_of(other_core * rows_own + c * chunk, chunk), chunk)]
        dst = tbuf.at[mod, pl.ds(pl.multiple_of(c * chunk, chunk), chunk)]
        return remote(src, dst, t_send.at[kind, c], t_recv.at[kind, c], peers[kind])

    barrier = pltpu.get_barrier_semaphore()
    for peer in peers:
        pl.semaphore_signal(barrier, inc=1, device_id=peer, device_id_type=MESH)
    local_x = pltpu.make_async_copy(x_hbm.at[pl.ds(pl.multiple_of(row_base, rows_own), rows_own)], x0, l_x)
    local_x.start()
    local_w = [pltpu.make_async_copy(w_hbm[k], wbuf.at[k, wrow(mod)], l_w.at[k]) for k in range(3)]
    local_u = [pltpu.make_async_copy(u_hbm[k], ubuf.at[k, mod], l_u.at[k]) for k in range(3)]
    for k in range(3):
        local_w[k].start()
        local_u[k].start()
    local_t = pltpu.make_async_copy(t_hbm.at[pl.ds(pl.multiple_of(row_base, rows_own), rows_own)], tbuf.at[mod], l_t)
    local_t.start()
    pl.semaphore_wait(barrier, 3)

    for k in range(3):
        for kind in range(3):
            u_copy(k, kind).start()
    for k in range(3):
        w_copy(k, 1).start()
        w_copy(k, 0).start()

    def start_targets(c, carry):
        t_copy(1, c).start()
        t_copy(2, c).start()
        t_copy(0, c).start()
        return carry

    lax.fori_loop(0, NT, start_targets, 0)
    acc[...] = jnp.zeros_like(acc)
    stat[...] = jnp.zeros_like(stat)
    local_x.wait()

    inv_sigma = []
    w_full_copy = pltpu.make_async_copy(wbuf.at[0], w_out, l_o)
    for k in range(3):
        w_copy(k, 1).wait_recv()
        w_copy(k, 2).start()
        local_w[k].wait()
        local_u[k].wait()
        for kind in range(3):
            u_copy(k, kind).wait_recv()
        w_copy(k, 0).wait_recv()
        w_copy(k, 2).wait_recv()
        if k == 0:
            w_full_copy.start()
        u_row = jnp.concatenate([ubuf[k, j] for j in range(4)], axis=1)
        p_vec = jnp.sum(dot_nn(split_rows(u_row), wbuf[k]), axis=0, keepdims=True)
        norm = jnp.sqrt(jnp.sum(p_vec * p_vec, axis=1, keepdims=True))
        v_vec = p_vec / jnp.maximum(norm, 1e-12)
        s_vec = jnp.sum(dot_nt(split_rows(v_vec), wbuf[k]), axis=0, keepdims=True)
        sigma = jnp.sqrt(jnp.sum(s_vec * s_vec, axis=1, keepdims=True))
        v_outs[k][...] = v_vec
        srow[k] = jnp.broadcast_to(s_vec / sigma, srow.shape[1:])
        n_outs[k][...] = srow[k, 0:1, wrow(mod)]
        sig_out[k:k + 1, :] = jnp.broadcast_to(sigma, (1, 128))
        inv = 1.0 / sigma
        inv_sigma.append(inv)

        def forward(c, carry, k=k, inv=inv):
            rows = pl.ds(pl.multiple_of(c * chunk, chunk), chunk)
            y_val = dot_nt(xs[k][rows, :], wbuf[k]) * inv
            ys[k][rows, :] = y_val
            if k < 2:
                xs[k + 1][rows, :] = jnp.maximum(y_val, 0.2 * y_val).astype(BF16)
            return carry

        lax.fori_loop(0, NT, forward, 0)

    local_t.wait()
    own_cols = pl.ds(pl.multiple_of(chip * 256, 256), 256)

    def fold(val):
        return jnp.sum(val.reshape(val.shape[0] // 8, 8, val.shape[1]), axis=0)

    def add_grad(k, rows):
        part = dot_tn(ebuf[k, :, own_cols], xs[k][rows, :])
        acc[k, 0] += part[:128]
        acc[k, 1] += part[128:]

    def e_local(c):
        rows = pl.ds(pl.multiple_of(c * chunk, chunk), chunk)
        out_rows = pl.ds(pl.multiple_of(row_base + c * chunk, chunk), chunk)
        return pltpu.make_async_copy(estage.at[rows], e_out.at[out_rows], l_e.at[c])

    def e_remote(c):
        rows = pl.ds(pl.multiple_of(c * chunk, chunk), chunk)
        out_rows = pl.ds(pl.multiple_of(row_base + c * chunk, chunk), chunk)
        return remote(estage.at[rows], e_out.at[out_rows], e_send.at[c], e_recv.at[c], peers[0])

    def backward(c, carry):
        rows = pl.ds(pl.multiple_of(c * chunk, chunk), chunk)
        for kind in range(3):
            t_copy(kind, c).wait_recv()
        for j in range(4):
            cols = slice(128 * j, 128 * j + 128)
            y_val = y2[rows, cols]
            res = y_val - tbuf[j, rows, :].astype(F32)
            grad = res * inv_batch
            stat[0, :, cols] += fold(res * res)
            stat[1, :, cols] += fold(grad * y_val)
            ebuf[2, :, cols] = grad.astype(BF16)
        for k in (2, 1):
            back = (dot_nn(ebuf[k], wbuf[k]) * inv_sigma[k]).astype(BF16).astype(F32)
            y_val = ys[k - 1][rows, :]
            grad = back * jnp.where(y_val > 0, 1.0, 0.2)
            stat[4 - k] += fold(grad * y_val)
            e_val = grad.astype(BF16)
            ebuf[k - 1] = e_val
            if k == 1:
                estage[rows, :] = e_val
            add_grad(k, rows)
        add_grad(0, rows)
        e_local(c).start()
        e_remote(c).start()
        return carry

    lax.fori_loop(0, NT, backward, 0)

    row = lax.broadcasted_iota(jnp.int32, sstat.shape, 0)
    mine = jnp.zeros(sstat.shape, F32)
    for i in range(4):
        mine = jnp.where(row == i, jnp.sum(stat[i], axis=0, keepdims=True), mine)
    sstat[...] = mine
    d_copies = [remote(acc.at[k, 1 - core], rbuf.at[k], d_send.at[k], d_recv.at[k], peers[0]) for k in range(3)]
    d_copies.append(remote(sstat, rstat, d_send.at[3], d_recv.at[3], peers[0]))
    for copy in d_copies:
        copy.start()
    for k in range(3):
        d_copies[k].wait_recv()
        dw_out[128 * k:128 * k + 128, :] = acc[k, core] + rbuf[k]
    d_copies[3].wait_recv()
    dw_out[384:392, :] = sstat[...] + rstat[...]

    for copy in d_copies:
        copy.wait_send()

    def drain(c, carry):
        for kind in range(3):
            t_copy(kind, c).wait_send()
        e_local(c).wait()
        e_remote(c).wait_send()
        e_remote(c).wait_recv()
        return carry

    lax.fori_loop(0, NT, drain, 0)
    for k in range(3):
        for kind in range(3):
            w_copy(k, kind).wait_send()
            u_copy(k, kind).wait_send()
    w_full_copy.wait()


def solution(mesh):
    data_size = mesh.shape["data"]
    row_spec = P(("replica", "model"), None)
    vec_spec = P(("replica", "model"))
    batch_spec = P(("replica", "data"), None)
    target_spec = P(("replica", "data"), "model")
    part_spec = P("replica")

    def local_step(x_in, w_in, w_mid, w_out, u_in, u_mid, u_out, target):
        rows, width = x_in.shape
        half = rows // 2
        chunk = half // NT
        batch_total = rows * data_size
        any_spec = pl.BlockSpec(memory_space=pl.ANY)
        vmem_spec = pl.BlockSpec(memory_space=pltpu.VMEM)
        dma = pltpu.SemaphoreType.DMA
        outs = pl.pallas_call(
            functools.partial(main_kernel, 1.0 / batch_total),
            out_shape=[
                jax.ShapeDtypeStruct((rows, width), BF16),
                jax.ShapeDtypeStruct((width, width), BF16),
                jax.ShapeDtypeStruct((392, width), F32),
            ] + [jax.ShapeDtypeStruct((1, width), F32)] * 3 + [jax.ShapeDtypeStruct((1, 128), F32)] * 3 + [
                jax.ShapeDtypeStruct((8, 128), F32)],
            in_specs=[any_spec] * 8,
            out_specs=[any_spec] * 2 + [vmem_spec] * 8,
            scratch_shapes=[pltpu.VMEM((half, width), BF16)] * 3 + [pltpu.VMEM((half, width), F32)] * 3 + [
                pltpu.VMEM((4, half, 128), BF16),
                pltpu.VMEM((3, width, width), BF16),
                pltpu.VMEM((3, 4, 1, 128), F32),
                pltpu.VMEM((3, chunk, width), BF16),
                pltpu.VMEM((half, width), BF16),
                pltpu.VMEM((3, 2, 128, width), F32),
                pltpu.VMEM((3, 128, width), F32),
                pltpu.VMEM((4, 8, width), F32),
                pltpu.VMEM((8, width), F32),
                pltpu.VMEM((8, width), F32),
                pltpu.VMEM((3, 8, width), F32),
                dma((3, 3)), dma((3, 3)), dma((3, 3)), dma((3, 3)),
                dma((3, NT)), dma((3, NT)), dma((NT,)), dma((NT,)), dma((4,)), dma((4,)),
                dma((3,)), dma((3,)), dma(()), dma(()), dma((NT,)), dma(()),
            ],
            compiler_params=pltpu.CompilerParams(
                collective_id=0, has_side_effects=True, vmem_limit_bytes=63 * 2**20),
            name="fused_step",
        )(x_in, w_in, w_mid, w_out, u_in.reshape(1, 128), u_mid.reshape(1, 128), u_out.reshape(1, 128), target)
        e_all, w_full, dw_part = outs[:3]
        v_vecs, u_next, sig = outs[3:6], outs[6:9], outs[9][:3, 0]
        other = lax.ppermute(dw_part, "data", [(0, 1), (1, 0)])
        grad_x = (jnp.dot(e_all, w_full, preferred_element_type=F32) / sig[0]).astype(BF16)
        total = dw_part + other
        sums = jnp.sum(total[384:388], axis=1)
        loss_val = 0.5 / batch_total * sums[0]
        grads_w = []
        for k in range(3):
            corr = sums[3 - k]
            grads_w.append(total[128 * k:128 * k + 128] / sig[k] - (corr / sig[k]) * (u_next[k].reshape(128, 1) * v_vecs[k]))
        return (loss_val.reshape(1), grad_x, grads_w[0], grads_w[1], grads_w[2],
                u_next[0].reshape(128), u_next[1].reshape(128), u_next[2].reshape(128),
                v_vecs[0].reshape(width), v_vecs[1].reshape(width), v_vecs[2].reshape(width), sig)

    in_specs = (batch_spec, row_spec, row_spec, row_spec, vec_spec, vec_spec, vec_spec, target_spec)
    out_specs = (part_spec, batch_spec, row_spec, row_spec, row_spec, vec_spec, vec_spec, vec_spec, part_spec, part_spec, part_spec, part_spec)
    return jax.shard_map(local_step, mesh=mesh, in_specs=in_specs, out_specs=out_specs, check_vma=False)
```

time: 549 us -> 98.5 us (0.18)
  waiting for transfers between devices: 364 us -> 4.56 us
  Pallas kernels: 0 us -> 64.5 us
  matrix products: 69.9 us -> 12.1 us
  blocking collectives: 38.1 us -> 0 us
  local copies, waits for them, and re-layouts: 39.3 us -> 5.83 us
  between operations: 22.1 us -> 6.54 us
  other arithmetic: 13.1 us -> 3.19 us
    psum x2 -> x0, waiting for transfers between devices: 134 us -> none  [the longest x1 134 us: local_step(): grad_x = lax.psum(x_part, 'model')]
    unnamed x8 -> x0, waiting for transfers between devices: 117 us -> none
    all_gather x2 -> x0, waiting for transfers between devices: 113 us -> none  [local_step(): layer_in = lax.all_gather(own_act, 'model', axis=1, tiled=True)]
    pallas_call x0 -> x1, Pallas kernels: none -> 64.5 us  [local_step(): pl.pallas_call(functools.partial(main_kernel, 1.0 / batch_total), out_sha...]
    dot_general x15 -> x1, matrix products: 69.9 us -> 12.1 us  [local_step(): jnp.dot(e_all, w_full, preferred_element_type=F32) / sig[0]]
    psum x3 -> x0, blocking collectives: 38.1 us -> none  [the longest x1 22.9 us: local_step(): lax.psum(jnp.sum(residual * residual), ('data', 'model'))]
    unnamed x35 -> x22, local copies, waits for them, and re-layouts: 39.3 us -> 3.3 us
    reduce_sum x4 -> x1, other arithmetic: 7.21 us -> 0.12 us  [local_step(): sums = jnp.sum(total[384:388], axis=1)]
  transfers between devices with their start and end apart: 6 -> 1, of which waited for: 5 -> 1; matrix products, arithmetic and copies ran while one was open for 6% -> 14% of each run, Pallas kernels for 0% -> 0%
where the time goes in v1:
time: 98.5 us; the launch traced here: 98.3 us
  Pallas kernels  64.5 us (65%)
  matrix products  12.1 us (12%)
  between operations  6.54 us (7%)
  local copies, waits for them, and re-layouts  5.83 us (6%)
  waiting for transfers between devices  4.56 us (5%)
  other arithmetic  3.19 us (3%)
  starting transfers between devices  1.6 us (2%)
    pallas_call x1, Pallas kernels, local_step(): pl.pallas_call(functools.partial(main_kernel, 1.0 / batch_total), out_sha...  64.5 us
    dot_general x1, matrix products, local_step(): jnp.dot(e_all, w_full, preferred_element_type=F32) / sig[0]  12.1 us
    ppermute x1, waiting for transfers between devices, local_step(): other = lax.ppermute(dw_part, 'data', [(0, 1), (1, 0)])  4.56 us
    unnamed x22, local copies, waits for them, and re-layouts  3.3 us
    sub x1, other arithmetic, local_step(): total[128 * k:128 * k + 128] / sig[k]  2.93 us
  transfers between devices with their start and end apart: 1, of which 1 were waited for; matrix products, arithmetic and copies ran while one was open for 14% of the time, Pallas kernels for 0%

profile of v1, /device:TPU:0, one launch (start us, length us, event | category | flops | bytes accessed | tf_op | source)
XLA Modules:
  0.0 98.3 jit_solution(18217950111975287508)
XLA Ops:
  0.6 64.5 %fused_step.1 = (bf16[8192,512]{1,0:T(8,128)(2,1)}, bf16[512,512]{1,0:T(8,128)(2,1)}, f32[392,512]{1,0:T(8,128)}, f32[1,512]{1,0:T(1,128)}, f32[1,512]{1,0:T(1,1...) custom-call(bf16[8192,512]{1,0:T(8,128)(2,1)} %x_hbm.1, ...), custom_call_target="tpu_custom_call" | custom-call | tf_op jit(solution)/shard_map/fused_step/pallas_call | solution.py:251
  65.2 1.6 %collective-permute-start = (f32[392,512]{1,0:T(8,128)}, f32[392,512]{1,0:T(8,128)S(1)}, u32[]{:S(2)}, u32[]{:S(2)}) collective-permute-start(f32[392,512]{1,0:T(8,128)} %get-tuple-element.22), channel_id=1, source_target_pairs={{0,4},{4,0},{1,5},{5,1},{2,6},{6,2},{3,7},{7,3}} | collective-permute-start | bytes 2408456 | tf_op jit(solution)/shard_map/ppermute | solution.py:283
  66.8 1.3 %fusion.3 = (f32[1,1]{1,0:T(1,128)}, f32[1,1]{1,0:T(1,128)}, f32[1,1]{1,0:T(1,128)}) fusion(f32[8,128]{1,0:T(8,128)} %get-tuple-element.25), kind=kLoop, calls=%fused_computation.9 | loop fusion | bytes 24 | tf_op jit(solution)/shard_map/slice | solution.py:291
  68.1 0.0 copy-start.4
  68.1 0.0 copy-start
  68.1 0.0 copy-start.1
  68.1 0.0 copy-start.2
  68.1 0.0 copy-start.3
  68.1 0.0 copy-start.5
  68.1 0.0 copy-start.6
  68.1 0.0 copy-start.7
  68.1 12.1 %divide_convert_fusion = bf16[8192,512]{1,0:T(8,128)(2,1)} fusion(f32[]{:T(128)} %bitcast.3, bf16[8192,512]{1,0:T(8,128)(2,1)} %get-tuple-element.23, bf16[512,512]{1,0:T(8,128)(2,1)} %get-tuple-element.24), kind=kOutput, calls=%fused_computation | convolution fusion | flops 4303355904 | bytes 17301508 | tf_op jit(solution)/shard_map/dot_general | solution.py:284
  80.2 0.0 copy-done.4
  80.2 0.6 slice_reduce_fusion.1
  80.8 4.6 %collective-permute-done = f32[392,512]{1,0:T(8,128)S(1)} collective-permute-done((f32[392,512]{1,0:T(8,128)}, f32[392,512]{1,0:T(8,128)S(1)}, u32[]{:S(2)}, u32[]{:S(2)}) %collective-permute-start) | collective-permute-done | bytes 802848 | tf_op jit(solution)/shard_map/ppermute | solution.py:283
  85.4 0.0 copy-done
  85.4 0.1 add.3
  85.5 0.1 slice_reduce_fusion
  85.6 0.6 fusion.4
  90.9 0.0 copy-done.1
  90.9 0.0 copy-done.2
  90.9 0.0 copy-done.3
  90.9 0.0 copy-done.5
  90.9 0.0 copy-done.6
  90.9 0.0 copy-done.7
  91.0 2.9 %fusion = (f32[128,512]{1,0:T(8,128)}, f32[128,512]{1,0:T(8,128)}, f32[128,512]{1,0:T(8,128)}) fusion(f32[392,512]{1,0:T(8,128)S(1)} %add.3, f32[512]{0:T(512)S(1)} %bitcast.17, f32[128]{0:T(128)S(1)} %bitcast.26, f32[]{:T(128)S(6)} %div.43, f32[]{:T(128)} %bitcast.11, f32[512]{0:T(512)S(1)} %bitcast.19, f32[128]{0:T(128)S(1)} %bitcast.28, f32[]{:T(128)S(6)} %div.40, ...), kind=kLoop, calls=%fused_computation.2 | loop fusion | flops 786432 | bytes 1580568 | tf_op jit(solution)/shard_map/sub | solution.py:291
  93.9 0.5 copy.26
  94.4 0.5 copy.27
  94.9 0.5 copy.28
  95.4 0.6 copy.29
  96.0 0.6 copy.30
  96.6 0.6 copy.31
Async XLA Ops:
  65.2 20.2 %collective-permute-start = (f32[392,512]{1,0:T(8,128)}, f32[392,512]{1,0:T(8,128)S(1)}, u32[]{:S(2)}, u32[]{:S(2)}) collective-permute-start(f32[392,512]{1,0:T(8,128)} %get-tuple-element.22), channel_id=1, source_target_pairs={{0,4},{4,0},{1,5},{5,1},{2,6},{6,2},{3,7},{7,3}} | collective-permute-start | bytes 2408456 | tf_op jit(solution)/shard_map/ppermute | solution.py:283
  68.1 12.1 %copy-start.4 = (f32[8,128]{1,0:T(8,128)S(1)}, f32[8,128]{1,0:T(8,128)}, u32[]{:S(2)}) copy-start(f32[8,128]{1,0:T(8,128)} %get-tuple-element.25) | copy-start | bytes 12292
  68.1 17.3 %copy-start = (f32[392,512]{1,0:T(8,128)S(1)}, f32[392,512]{1,0:T(8,128)}, u32[]{:S(2)}) copy-start(f32[392,512]{1,0:T(8,128)} %get-tuple-element.22) | copy-start | bytes 2408452
  68.1 22.8 %copy-start.1 = (f32[1,512]{1,0:T(1,128)S(1)}, f32[1,512]{1,0:T(1,128)}, u32[]{:S(2)}) copy-start(f32[1,512]{1,0:T(1,128)} %get-tuple-element.31) | copy-start | bytes 6148
  68.1 22.8 %copy-start.2 = (f32[1,512]{1,0:T(1,128)S(1)}, f32[1,512]{1,0:T(1,128)}, u32[]{:S(2)}) copy-start(f32[1,512]{1,0:T(1,128)} %get-tuple-element.29) | copy-start | bytes 6148
  68.1 22.8 %copy-start.3 = (f32[1,512]{1,0:T(1,128)S(1)}, f32[1,512]{1,0:T(1,128)}, u32[]{:S(2)}) copy-start(f32[1,512]{1,0:T(1,128)} %get-tuple-element.27) | copy-start | bytes 6148
  68.1 22.8 %copy-start.5 = (f32[1,128]{1,0:T(1,128)S(1)}, f32[1,128]{1,0:T(1,128)}, u32[]{:S(2)}) copy-start(f32[1,128]{1,0:T(1,128)} %get-tuple-element.30) | copy-start | bytes 1540
  68.1 22.8 %copy-start.6 = (f32[1,128]{1,0:T(1,128)S(1)}, f32[1,128]{1,0:T(1,128)}, u32[]{:S(2)}) copy-start(f32[1,128]{1,0:T(1,128)} %get-tuple-element.28) | copy-start | bytes 1540
  68.1 22.8 %copy-start.7 = (f32[1,128]{1,0:T(1,128)S(1)}, f32[1,128]{1,0:T(1,128)}, u32[]{:S(2)}) copy-start(f32[1,128]{1,0:T(1,128)} %get-tuple-element.26) | copy-start | bytes 1540

commit v2 on v1

v2 whole, which is shorter than its diff:
```python
import functools

import jax
import jax.numpy as jnp
from jax import lax
from jax.experimental import pallas as pl
from jax.experimental.pallas import tpu as pltpu
from jax.sharding import PartitionSpec as P

MESH = pl.DeviceIdType.MESH
F32 = jnp.float32
BF16 = jnp.bfloat16
NT = 16
NF = 4


def dot_nt(lhs, rhs):
    return lax.dot_general(lhs, rhs, (((1,), (1,)), ((), ())), preferred_element_type=F32)


def dot_nn(lhs, rhs):
    return lax.dot_general(lhs, rhs, (((1,), (0,)), ((), ())), preferred_element_type=F32)


def dot_tn(lhs, rhs):
    return lax.dot_general(lhs, rhs, (((0,), (0,)), ((), ())), preferred_element_type=F32)


def split_rows(vec):
    width = vec.shape[1]
    high = vec.astype(BF16).astype(F32)
    rest = vec - high
    mid = rest.astype(BF16).astype(F32)
    low = rest - mid
    row = lax.broadcasted_iota(jnp.int32, (16, width), 0)
    stacked = jnp.where(row == 0, high, jnp.where(row == 1, mid, jnp.where(row == 2, low, 0.0)))
    return stacked.astype(BF16)


def main_kernel(inv_batch, x_hbm, w0_hbm, w1_hbm, w2_hbm, u0_hbm, u1_hbm, u2_hbm, t_hbm,
                e_out, w_out, dw_out, g2_out, v0_out, v1_out, v2_out, n0_out, n1_out, n2_out, sig_out,
                x0, x1, x2, y0, y1, y2, tbuf, wbuf, ubuf, e2, e1, e0, acc, rbuf, g2own, g2other, stat, rstat, sstat, srow,
                w_send, w_recv, u_send, u_recv, t_send, t_recv, s_send, s_recv, e_send, e_recv, d_send, d_recv, g_send, g_recv,
                l_w, l_u, l_t, l_x, l_e, l_o):
    rep, dat, mod = lax.axis_index("replica"), lax.axis_index("data"), lax.axis_index("model")
    core = lax.rem(mod, 2)
    chip = mod // 2
    sib = mod + 1 - 2 * core
    cnt = lax.rem(mod + 2, 4)
    crs = lax.rem(sib + 2, 4)
    p_sib, p_cnt, p_crs, p_y = (rep, dat, sib), (rep, dat, cnt), (rep, dat, crs), (rep, 1 - dat, mod)
    rows_own = x0.shape[0]
    chunk = rows_own // NT
    fwd_chunk = rows_own // NF
    row_base = core * rows_own
    w_hbm = [w0_hbm, w1_hbm, w2_hbm]
    u_hbm = [u0_hbm, u1_hbm, u2_hbm]
    xs = [x0, x1, x2]
    ys = [y0, y1, y2]
    es = [e0, e1, e2]
    v_outs = [v0_out, v1_out, v2_out]
    n_outs = [n0_out, n1_out, n2_out]

    def remote(src, dst, ssem, rsem, peer):
        return pltpu.make_async_remote_copy(src_ref=src, dst_ref=dst, send_sem=ssem, recv_sem=rsem,
                                            device_id=peer, device_id_type=MESH)

    def span(start, size):
        return pl.ds(pl.multiple_of(start, size), size)

    def w_copy(layer, kind):
        ssem, rsem = w_send.at[layer, kind], w_recv.at[layer, kind]
        if kind == 0:
            return remote(w_hbm[layer], wbuf.at[layer, span(128 * mod, 128)], ssem, rsem, p_sib)
        if kind == 1:
            return remote(w_hbm[layer].at[span(64 * dat, 64)], wbuf.at[layer, span(128 * mod + 64 * dat, 64)], ssem, rsem, p_cnt)
        half = 1 - dat if kind == 4 else dat
        ref = wbuf.at[layer, span(128 * cnt + 64 * half, 64)]
        return remote(ref, ref, ssem, rsem, p_y if kind == 2 else p_sib)

    def u_copy(layer, kind):
        return remote(u_hbm[layer], ubuf.at[layer, mod], u_send.at[layer, kind], u_recv.at[layer, kind],
                      (p_sib, p_cnt, p_crs)[kind])

    def t_copy(kind, c):
        other_core = core if kind == 0 else 1 - core
        return remote(t_hbm.at[span(other_core * rows_own + c * chunk, chunk)], tbuf.at[mod, span(c * chunk, chunk)],
                      t_send.at[kind, c], t_recv.at[kind, c], p_cnt if kind == 0 else p_crs)

    barrier = pltpu.get_barrier_semaphore()
    for peer in (p_sib, p_cnt, p_crs, p_y):
        pl.semaphore_signal(barrier, inc=1, device_id=peer, device_id_type=MESH)
    local_x = pltpu.make_async_copy(x_hbm.at[span(row_base, rows_own)], x0, l_x)
    local_w = [pltpu.make_async_copy(w_hbm[k], wbuf.at[k, span(128 * mod, 128)], l_w.at[k]) for k in range(3)]
    local_u = [pltpu.make_async_copy(u_hbm[k], ubuf.at[k, mod], l_u.at[k]) for k in range(3)]
    local_t = pltpu.make_async_copy(t_hbm.at[span(row_base, rows_own)], tbuf.at[mod], l_t)
    for k in range(3):
        local_w[k].start()
        local_u[k].start()
    local_x.start()
    local_t.start()
    pl.semaphore_wait(barrier, 4)

    for k in range(3):
        w_copy(k, 1).start()
        w_copy(k, 0).start()
        for kind in range(3):
            u_copy(k, kind).start()

    def start_targets(c, carry):
        t_copy(0, c).start()
        t_copy(1, c).start()
        return carry

    lax.fori_loop(0, NT, start_targets, 0)
    t_sib = remote(t_hbm.at[span((1 - core) * rows_own, rows_own)], tbuf.at[mod], s_send, s_recv, p_sib)
    t_sib.start()
    acc[...] = jnp.zeros_like(acc)
    stat[...] = jnp.zeros_like(stat)

    def relay_x(k):
        w_copy(k, 1).wait_recv()
        w_copy(k, 2).start()
        w_copy(k, 3).start()

    def relay_y(k):
        w_copy(k, 2).wait_recv()
        w_copy(k, 4).start()

    own_cols = span(256 * chip, 256)

    def fold(val):
        return jnp.sum(val.reshape(val.shape[0] // 8, 8, val.shape[1]), axis=0)

    def add_grad(k, rows):
        part = dot_tn(es[k][rows, own_cols], xs[k][rows, :])
        acc[k, 0] += part[:128]
        acc[k, 1] += part[128:]

    def residual(slab, rows):
        cols = span(128 * slab, 128)
        y_val = y2[rows, cols]
        res = y_val - tbuf[slab, rows, :].astype(F32)
        grad = res * inv_batch
        stat[0, :, cols] += fold(res * res)
        stat[1, :, cols] += fold(grad * y_val)
        e2[rows, cols] = grad.astype(BF16)

    inv_sigma = []
    w_full_copy = pltpu.make_async_copy(wbuf.at[0], w_out, l_o)
    relay_x(0)
    relay_y(0)
    for k in range(3):
        local_w[k].wait()
        local_u[k].wait()
        for kind in range(3):
            u_copy(k, kind).wait_recv()
        for kind in (0, 3, 4):
            w_copy(k, kind).wait_recv()
        if k == 0:
            w_full_copy.start()
        u_row = jnp.concatenate([ubuf[k, j] for j in range(4)], axis=1)
        p_vec = jnp.sum(dot_nn(split_rows(u_row), wbuf[k]), axis=0, keepdims=True)
        norm = jnp.sqrt(jnp.sum(p_vec * p_vec, axis=1, keepdims=True))
        v_vec = p_vec / jnp.maximum(norm, 1e-12)
        s_vec = jnp.sum(dot_nt(split_rows(v_vec), wbuf[k]), axis=0, keepdims=True)
        sigma = jnp.sqrt(jnp.sum(s_vec * s_vec, axis=1, keepdims=True))
        v_outs[k][...] = v_vec
        srow[k] = jnp.broadcast_to(s_vec / sigma, srow.shape[1:])
        n_outs[k][...] = srow[k, 0:1, span(128 * mod, 128)]
        sig_out[k:k + 1, :] = jnp.broadcast_to(sigma, (1, 128))
        inv = 1.0 / sigma
        inv_sigma.append(inv)
        if k < 2:
            relay_x(k + 1)
            relay_y(k + 1)
        if k == 0:
            local_x.wait()
        if k == 2:
            local_t.wait()
            t_sib.wait_recv()

        def forward(c, carry, k=k, inv=inv):
            rows = span(c * fwd_chunk, fwd_chunk)
            y_val = dot_nt(xs[k][rows, :], wbuf[k]) * inv
            ys[k][rows, :] = y_val
            if k < 2:
                xs[k + 1][rows, :] = jnp.maximum(y_val, 0.2 * y_val).astype(BF16)
            else:
                for j in range(2):
                    residual(2 * chip + j, rows)
                add_grad(2, rows)
            return carry

        lax.fori_loop(0, NF, forward, 0)

    def d_copy(k):
        return remote(acc.at[k, 1 - core], rbuf.at[k], d_send.at[k], d_recv.at[k], p_sib)

    g_copy = remote(g2own, g2other, g_send, g_recv, p_y)

    def e_local(c):
        return pltpu.make_async_copy(e0.at[span(c * chunk, chunk)], e_out.at[span(row_base + c * chunk, chunk)], l_e.at[c])

    def e_remote(c):
        return remote(e0.at[span(c * chunk, chunk)], e_out.at[span(row_base + c * chunk, chunk)], e_send.at[c], e_recv.at[c], p_sib)

    def backward(c, carry):
        @pl.when(c == 1)
        def _():
            d_copy(2).start()

        @pl.when(c == 3)
        def _():
            d_copy(2).wait_recv()
            g2own[...] = acc[2, core] + rbuf[2]

        @pl.when(c == 4)
        def _():
            g_copy.start()

        rows = span(c * chunk, chunk)
        for kind in range(2):
            t_copy(kind, c).wait_recv()
        for j in range(2):
            residual(2 - 2 * chip + j, rows)
        for k in (2, 1):
            back = (dot_nn(es[k][rows, :], wbuf[k]) * inv_sigma[k]).astype(BF16).astype(F32)
            y_val = ys[k - 1][rows, :]
            grad = back * jnp.where(y_val > 0, 1.0, 0.2)
            stat[4 - k] += fold(grad * y_val)
            es[k - 1][rows, :] = grad.astype(BF16)
            add_grad(k - 1, rows)
        e_local(c).start()
        e_remote(c).start()
        return carry

    lax.fori_loop(0, NT, backward, 0)

    d_copy(1).start()
    row = lax.broadcasted_iota(jnp.int32, sstat.shape, 0)
    mine = jnp.zeros(sstat.shape, F32)
    for i in range(4):
        mine = jnp.where(row == i, jnp.sum(stat[i], axis=0, keepdims=True), mine)
    sstat[...] = mine
    d_copy(0).start()
    s_copy = remote(sstat, rstat, d_send.at[3], d_recv.at[3], p_sib)
    s_copy.start()
    g_copy.wait_recv()
    g2_out[...] = g2own[...] + g2other[...]
    for i, k in enumerate((1, 0)):
        d_copy(k).wait_recv()
        dw_out[128 * i:128 * i + 128, :] = acc[k, core] + rbuf[k]
    s_copy.wait_recv()
    dw_out[256:264, :] = sstat[...] + rstat[...]

    for k in range(3):
        d_copy(k).wait_send()
    s_copy.wait_send()
    g_copy.wait_send()
    t_sib.wait_send()

    def drain(c, carry):
        for kind in range(2):
            t_copy(kind, c).wait_send()
        e_local(c).wait()
        e_remote(c).wait_send()
        e_remote(c).wait_recv()
        return carry

    lax.fori_loop(0, NT, drain, 0)
    for k in range(3):
        for kind in range(5):
            w_copy(k, kind).wait_send()
        for kind in range(3):
            u_copy(k, kind).wait_send()
    w_full_copy.wait()


def dx_kernel(e_ref, w_ref, sig_ref, v0, v1, v2, n0, n1, n2, dx_ref, v0_out, v1_out, v2_out, n0_out, n1_out, n2_out, sig_out):
    inv = 1.0 / sig_ref[0:1, 0:1]
    dx_ref[...] = (dot_nn(e_ref[...], w_ref[...]) * inv).astype(BF16)

    @pl.when(pl.program_id(0) == 0)
    def _():
        for src, dst in ((v0, v0_out), (v1, v1_out), (v2, v2_out), (n0, n0_out), (n1, n1_out), (n2, n2_out)):
            dst[...] = src[...]
        lane = lax.broadcasted_iota(jnp.int32, (1, 128), 1)
        row = jnp.where(lane == 0, sig_ref[0:1, :], jnp.where(lane == 1, sig_ref[1:2, :], sig_ref[2:3, :]))
        sig_out[...] = row[:, :3]


def final_kernel(loss_scale, own, other, g2, sig_ref, v0, v1, v2, n0, n1, n2, dw0, dw1, dw2, loss_out):
    stats = jnp.sum(own[256:264, :] + other[256:264, :], axis=1, keepdims=True)
    loss_out[...] = loss_scale * stats[0:1]
    grads = (own[128:256, :] + other[128:256, :], own[0:128, :] + other[0:128, :], g2[...])
    for k, (grad, v_ref, n_ref, out) in enumerate(zip(grads, (v0, v1, v2), (n0, n1, n2), (dw0, dw1, dw2))):
        inv = 1.0 / sig_ref[k:k + 1, 0:1]
        u_col = jnp.transpose(jnp.broadcast_to(n_ref[...], (128, 128)))[:, 0:1]
        out[...] = grad * inv - (stats[3 - k:4 - k] * inv) * (u_col * v_ref[...])


def solution(mesh):
    data_size = mesh.shape["data"]
    row_spec = P(("replica", "model"), None)
    vec_spec = P(("replica", "model"))
    batch_spec = P(("replica", "data"), None)
    target_spec = P(("replica", "data"), "model")
    part_spec = P("replica")

    def local_step(x_in, w_in, w_mid, w_out, u_in, u_mid, u_out, target):
        rows, width = x_in.shape
        half = rows // 2
        batch_total = rows * data_size
        any_spec = pl.BlockSpec(memory_space=pl.ANY)
        vmem_spec = pl.BlockSpec(memory_space=pltpu.VMEM)
        dma = pltpu.SemaphoreType.DMA
        small = [jax.ShapeDtypeStruct((1, width), F32)] * 3 + [jax.ShapeDtypeStruct((1, 128), F32)] * 3
        outs = pl.pallas_call(
            functools.partial(main_kernel, 1.0 / batch_total),
            out_shape=[
                jax.ShapeDtypeStruct((rows, width), BF16),
                jax.ShapeDtypeStruct((width, width), BF16),
                jax.ShapeDtypeStruct((264, width), F32),
                jax.ShapeDtypeStruct((128, width), F32),
            ] + small + [jax.ShapeDtypeStruct((8, 128), F32)],
            in_specs=[any_spec] * 8,
            out_specs=[any_spec] * 2 + [vmem_spec] * 9,
            scratch_shapes=[pltpu.VMEM((half, width), BF16)] * 3 + [pltpu.VMEM((half, width), F32)] * 3 + [
                pltpu.VMEM((4, half, 128), BF16),
                pltpu.VMEM((3, width, width), BF16),
                pltpu.VMEM((3, 4, 1, 128), F32),
                pltpu.VMEM((half, width), BF16),
                pltpu.VMEM((half, width), BF16),
                pltpu.VMEM((half, width), BF16),
                pltpu.VMEM((3, 2, 128, width), F32),
                pltpu.VMEM((3, 128, width), F32),
                pltpu.VMEM((128, width), F32),
                pltpu.VMEM((128, width), F32),
                pltpu.VMEM((4, 8, width), F32),
                pltpu.VMEM((8, width), F32),
                pltpu.VMEM((8, width), F32),
                pltpu.VMEM((3, 8, width), F32),
                dma((3, 5)), dma((3, 5)), dma((3, 3)), dma((3, 3)),
                dma((2, NT)), dma((2, NT)), dma(()), dma(()), dma((NT,)), dma((NT,)), dma((4,)), dma((4,)), dma(()), dma(()),
                dma((3,)), dma((3,)), dma(()), dma(()), dma((NT,)), dma(()),
            ],
            compiler_params=pltpu.CompilerParams(
                collective_id=0, has_side_effects=True, vmem_limit_bytes=63 * 2**20),
            name="fused_step",
        )(x_in, w_in, w_mid, w_out, u_in.reshape(1, 128), u_mid.reshape(1, 128), u_out.reshape(1, 128), target)
        e_all, w_full, dw_part, g2_sum = outs[:4]
        vecs, sig = outs[4:10], outs[10]
        other = lax.ppermute(dw_part, "data", [(0, 1), (1, 0)])

        block = 1024
        full = lambda shape: pl.BlockSpec(shape, lambda i: (0, 0))
        vec_specs = [full((1, width))] * 3 + [full((1, 128))] * 3
        passed = pl.pallas_call(
            dx_kernel,
            grid=(rows // block,),
            out_shape=[jax.ShapeDtypeStruct((rows, width), BF16)] + small + [jax.ShapeDtypeStruct((1, 3), F32)],
            in_specs=[pl.BlockSpec((block, width), lambda i: (i, 0)), full((width, width)), full((8, 128))] + vec_specs,
            out_specs=[pl.BlockSpec((block, width), lambda i: (i, 0))] + vec_specs + [full((1, 3))],
            cost_estimate=pl.CostEstimate(flops=2 * rows * width * width, bytes_accessed=4 * rows * width, transcendentals=0),
            compiler_params=pltpu.CompilerParams(vmem_limit_bytes=24 * 2**20),
            name="dx",
        )(e_all, w_full, sig, *vecs)
        grad_x, sig_row = passed[0], passed[7]

        finals = pl.pallas_call(
            functools.partial(final_kernel, 0.5 / batch_total),
            out_shape=[jax.ShapeDtypeStruct((128, width), F32)] * 3 + [jax.ShapeDtypeStruct((1, 1), F32)],
            in_specs=[vmem_spec] * 10,
            out_specs=[vmem_spec] * 4,
            compiler_params=pltpu.CompilerParams(vmem_limit_bytes=8 * 2**20),
            name="finish",
        )(dw_part, other, g2_sum, sig, *vecs)
        v_row, u_row = passed[1:4], passed[4:7]
        return (finals[3].reshape(1), grad_x, finals[0], finals[1], finals[2],
                u_row[0].reshape(128), u_row[1].reshape(128), u_row[2].reshape(128),
                v_row[0].reshape(width), v_row[1].reshape(width), v_row[2].reshape(width), sig_row.reshape(3))

    in_specs = (batch_spec, row_spec, row_spec, row_spec, vec_spec, vec_spec, vec_spec, target_spec)
    out_specs = (part_spec, batch_spec, row_spec, row_spec, row_spec, vec_spec, vec_spec, vec_spec, part_spec, part_spec, part_spec, part_spec)
    return jax.shard_map(local_step, mesh=mesh, in_specs=in_specs, out_specs=out_specs, check_vma=False)
```

time: 98.5 us -> 80 us (0.81)
  matrix products: 12.1 us -> 0 us
  between operations: 6.54 us -> 0.69 us
  waiting for transfers between devices: 4.56 us -> 0.01 us
  Pallas kernels: 64.5 us -> 68.8 us
  local copies, waits for them, and re-layouts: 5.83 us -> 9.06 us
  other arithmetic: 3.19 us -> 0 us
    dot_general x1 -> x0, matrix products: 12.1 us -> none  [local_step(): jnp.dot(e_all, w_full, preferred_element_type=F32) / sig[0]]
    pallas_call x0 -> x2, Pallas kernels: none -> 8.62 us  [the longest x1 7.5 us: local_step(): pl.pallas_call(dx_kernel, grid=(rows // block,), out_shape=[jax.ShapeDtyp...]
    unnamed x22, local copies, waits for them, and re-layouts: 3.3 us -> 9.06 us
    ppermute x1, waiting for transfers between devices: 4.56 us -> 0.01 us  [local_step(): other = lax.ppermute(dw_part, 'data', [(0, 1), (1, 0)])]
    pallas_call x1, Pallas kernels: 64.5 us -> 60.2 us  [local_step(): pl.pallas_call(functools.partial(main_kernel, 1.0 / batch_total), out_sha...]
    sub x1 -> x0, other arithmetic: 2.93 us -> none  [local_step(): total[128 * k:128 * k + 128] / sig[k]]
    slice x3 -> x0, local copies, waits for them, and re-layouts: 2.53 us -> none  [the longest x1 1.31 us: local_step(): sig[k]]
  transfers between devices with their start and end apart: 1 -> 1, of which waited for: 1 -> 0; matrix products, arithmetic and copies ran while one was open for 14% -> 0% of each run, Pallas kernels for 0% -> 9%
where the time goes in v2:
time: 80 us; the launch traced here: 79.7 us
  Pallas kernels  68.8 us (86%)
  local copies, waits for them, and re-layouts  9.06 us (11%)
  starting transfers between devices  1.11 us (1%)
    pallas_call x1, Pallas kernels, local_step(): pl.pallas_call(functools.partial(main_kernel, 1.0 / batch_total), out_sha...  60.2 us
    unnamed x22, local copies, waits for them, and re-layouts  9.06 us
    pallas_call x1, Pallas kernels, local_step(): pl.pallas_call(dx_kernel, grid=(rows // block,), out_shape=[jax.ShapeDtyp...  7.5 us
  transfers between devices with their start and end apart: 1, of which 0 were waited for; matrix products, arithmetic and copies ran while one was open for 0% of the time, Pallas kernels for 9%

profile of v2, /device:TPU:0, one launch (start us, length us, event | category | flops | bytes accessed | tf_op | source)
XLA Modules:
  0.0 79.7 jit_solution(7554927987149887356)
XLA Ops:
  0.6 60.2 %fused_step.1 = (bf16[8192,512]{1,0:T(8,128)(2,1)}, bf16[512,512]{1,0:T(8,128)(2,1)}, f32[264,512]{1,0:T(8,128)}, f32[128,512]{1,0:T(8,128)}, f32[1,512]{1,0:T(1...) custom-call(bf16[8192,512]{1,0:T(8,128)(2,1)} %x_hbm.1, ...), custom_call_target="tpu_custom_call" | custom-call | tf_op jit(solution)/shard_map/fused_step/pallas_call | solution.py:319
  60.8 0.0 copy-start
  60.9 0.0 copy-start.1
  60.9 1.1 %collective-permute-start = (f32[264,512]{1,0:T(8,128)}, f32[264,512]{1,0:T(8,128)S(1)}, u32[]{:S(2)}, u32[]{:S(2)}) collective-permute-start(f32[264,512]{1,0:T(8,128)} %get-tuple-element.35.own), channel_id=1, source_target_pairs={{0,4},{4,0},{1,5},{5,1},{2,6},{6,2},{3,7},{7,3}} | collective-permute-start | bytes 1622024 | tf_op jit(solution)/shard_map/ppermute | solution.py:354
  62.0 0.0 copy-start.2
  62.0 0.7 copy-done.2
  62.6 0.0 copy-start.3
  62.6 0.7 copy-done.3
  63.3 0.0 copy-start.4
  63.3 0.7 copy-done.4
  64.0 0.0 copy-start.5
  64.0 0.7 copy-done.5
  64.7 0.0 copy-start.6
  64.7 0.7 copy-done.6
  65.3 0.0 copy-start.7
  65.3 0.7 copy-done.7
  66.0 0.0 copy-start.8
  66.0 0.6 copy-done.8
  66.6 0.0 copy-start.9
  66.6 3.4 %copy-done.9 = bf16[8192,512]{1,0:T(8,128)(2,1)S(1)} copy-done((bf16[8192,512]{1,0:T(8,128)(2,1)S(1)}, bf16[8192,512]{1,0:T(8,128)(2,1)}, u32[]{:S(2)}) %copy-start.9) | copy-done | bytes 8388632
  70.0 0.0 copy-start.10
  70.0 1.0 %copy-done.10 = bf16[512,512]{1,0:T(8,128)(2,1)S(1)} copy-done((bf16[512,512]{1,0:T(8,128)(2,1)S(1)}, bf16[512,512]{1,0:T(8,128)(2,1)}, u32[]{:S(2)}) %copy-start.10) | copy-done | bytes 524312
  71.0 7.5 %dx.1 = (bf16[8192,512]{1,0:T(8,128)(2,1)}, f32[1,512]{1,0:T(1,128)}, f32[1,512]{1,0:T(1,128)}, f32[1,512]{1,0:T(1,128)}, f32[1,128]{1,0:T(1,128)}, /*index=5*/f...) custom-call(bf16[8192,512]{1,0:T(8,128)(2,1)S(1)} %copy-done.9, bf16[512,512]{1,0:T(8,128)(2,1)S(1)} %copy-done.10, ...), custom_call_target="tpu_custom_call" | custom-call | flops 4294967296 | bytes 16777216 | tf_op jit(solution)/shard_map/dx/pallas_call | solution.py:359
  78.5 0.0 collective-permute-done.other
  78.5 0.0 copy-done
  78.5 0.0 copy-done.1
  78.5 1.1 %finish.1 = (f32[128,512]{1,0:T(8,128)}, f32[128,512]{1,0:T(8,128)}, f32[128,512]{1,0:T(8,128)}, f32[1,1]{1,0:T(1,128)}) custom-call(f32[264,512]{1,0:T(8,128)S(1)} %copy-done, f32[264,512]{1,0:T(8,128)S(1)} %collective-permute-done.other, f32[128,512]{1,0:T(8,128)S(1)} %copy-done.1, f32[8,128]{1,0:T(8,128)S(1)} %copy-done.2, f32[1,512]{1,0:T(1,128)S(1)} %copy-done.3, ...), custom_call_target="tpu_custom_call" | custom-call | tf_op jit(solution)/shard_map/finish/pallas_call | solution.py:371
Async XLA Ops:
  60.8 17.7 %copy-start = (f32[264,512]{1,0:T(8,128)S(1)}, f32[264,512]{1,0:T(8,128)}, u32[]{:S(2)}) copy-start(f32[264,512]{1,0:T(8,128)} %get-tuple-element.35.own) | copy-start | bytes 1622020
  60.9 17.7 %copy-start.1 = (f32[128,512]{1,0:T(8,128)S(1)}, f32[128,512]{1,0:T(8,128)}, u32[]{:S(2)}) copy-start(f32[128,512]{1,0:T(8,128)} %get-tuple-element.36.g2) | copy-start | bytes 786436
  60.9 17.7 %collective-permute-start = (f32[264,512]{1,0:T(8,128)}, f32[264,512]{1,0:T(8,128)S(1)}, u32[]{:S(2)}, u32[]{:S(2)}) collective-permute-start(f32[264,512]{1,0:T(8,128)} %get-tuple-element.35.own), channel_id=1, source_target_pairs={{0,4},{4,0},{1,5},{5,1},{2,6},{6,2},{3,7},{7,3}} | collective-permute-start | bytes 1622024 | tf_op jit(solution)/shard_map/ppermute | solution.py:354
  62.0 0.7 copy-start.2
  62.6 0.7 copy-start.3
  63.3 0.7 copy-start.4
  64.0 0.7 copy-start.5
  64.7 0.7 copy-start.6
  65.3 0.7 copy-start.7
  66.0 0.6 copy-start.8
  66.6 3.4 %copy-start.9 = (bf16[8192,512]{1,0:T(8,128)(2,1)S(1)}, bf16[8192,512]{1,0:T(8,128)(2,1)}, u32[]{:S(2)}) copy-start(bf16[8192,512]{1,0:T(8,128)(2,1)} %get-tuple-element.45.e_ref) | copy-start | bytes 25165828
  70.0 1.0 %copy-start.10 = (bf16[512,512]{1,0:T(8,128)(2,1)S(1)}, bf16[512,512]{1,0:T(8,128)(2,1)}, u32[]{:S(2)}) copy-start(bf16[512,512]{1,0:T(8,128)(2,1)} %get-tuple-element.46.w_ref) | copy-start | bytes 1572868

commit v3 on v2

--- a/solution.py
+++ b/solution.py
@@ -38,7 +38,7 @@
 
 
 def main_kernel(inv_batch, x_hbm, w0_hbm, w1_hbm, w2_hbm, u0_hbm, u1_hbm, u2_hbm, t_hbm,
-                e_out, w_out, dw_out, g2_out, v0_out, v1_out, v2_out, n0_out, n1_out, n2_out, sig_out,
+                e_out, w_out, dw_out, g2_out, pack_out,
                 x0, x1, x2, y0, y1, y2, tbuf, wbuf, ubuf, e2, e1, e0, acc, rbuf, g2own, g2other, stat, rstat, sstat, srow,
                 w_send, w_recv, u_send, u_recv, t_send, t_recv, s_send, s_recv, e_send, e_recv, d_send, d_recv, g_send, g_recv,
                 l_w, l_u, l_t, l_x, l_e, l_o):
@@ -58,8 +58,6 @@
     xs = [x0, x1, x2]
     ys = [y0, y1, y2]
     es = [e0, e1, e2]
-    v_outs = [v0_out, v1_out, v2_out]
-    n_outs = [n0_out, n1_out, n2_out]
 
     def remote(src, dst, ssem, rsem, peer):
         return pltpu.make_async_remote_copy(src_ref=src, dst_ref=dst, send_sem=ssem, recv_sem=rsem,
@@ -129,11 +127,14 @@
 
     own_cols = span(256 * chip, 256)
 
+    def e_rows(k, rows):
+        return slice(None) if k == 1 else rows
+
     def fold(val):
         return jnp.sum(val.reshape(val.shape[0] // 8, 8, val.shape[1]), axis=0)
 
     def add_grad(k, rows):
-        part = dot_tn(es[k][rows, own_cols], xs[k][rows, :])
+        part = dot_tn(es[k][e_rows(k, rows), own_cols], xs[k][rows, :])
         acc[k, 0] += part[:128]
         acc[k, 1] += part[128:]
 
@@ -165,10 +166,10 @@
         v_vec = p_vec / jnp.maximum(norm, 1e-12)
         s_vec = jnp.sum(dot_nt(split_rows(v_vec), wbuf[k]), axis=0, keepdims=True)
         sigma = jnp.sqrt(jnp.sum(s_vec * s_vec, axis=1, keepdims=True))
-        v_outs[k][...] = v_vec
+        pack_out[k:k + 1, :] = v_vec
         srow[k] = jnp.broadcast_to(s_vec / sigma, srow.shape[1:])
-        n_outs[k][...] = srow[k, 0:1, span(128 * mod, 128)]
-        sig_out[k:k + 1, :] = jnp.broadcast_to(sigma, (1, 128))
+        pack_out[3 + k:4 + k, 0:128] = srow[k, 0:1, span(128 * mod, 128)]
+        pack_out[6 + k:7 + k, :] = jnp.broadcast_to(sigma, (1, pack_out.shape[1]))
         inv = 1.0 / sigma
         inv_sigma.append(inv)
         if k < 2:
@@ -225,11 +226,11 @@
         for j in range(2):
             residual(2 - 2 * chip + j, rows)
         for k in (2, 1):
-            back = (dot_nn(es[k][rows, :], wbuf[k]) * inv_sigma[k]).astype(BF16).astype(F32)
+            back = (dot_nn(es[k][e_rows(k, rows), :], wbuf[k]) * inv_sigma[k]).astype(BF16).astype(F32)
             y_val = ys[k - 1][rows, :]
             grad = back * jnp.where(y_val > 0, 1.0, 0.2)
             stat[4 - k] += fold(grad * y_val)
-            es[k - 1][rows, :] = grad.astype(BF16)
+            es[k - 1][e_rows(k - 1, rows), :] = grad.astype(BF16)
             add_grad(k - 1, rows)
         e_local(c).start()
         e_remote(c).start()
@@ -277,27 +278,28 @@
     w_full_copy.wait()
 
 
-def dx_kernel(e_ref, w_ref, sig_ref, v0, v1, v2, n0, n1, n2, dx_ref, v0_out, v1_out, v2_out, n0_out, n1_out, n2_out, sig_out):
-    inv = 1.0 / sig_ref[0:1, 0:1]
+def dx_kernel(e_ref, w_ref, pack, dx_ref, v0_out, v1_out, v2_out, n0_out, n1_out, n2_out, sig_out):
+    inv = 1.0 / pack[6:7, 0:1]
     dx_ref[...] = (dot_nn(e_ref[...], w_ref[...]) * inv).astype(BF16)
 
     @pl.when(pl.program_id(0) == 0)
     def _():
-        for src, dst in ((v0, v0_out), (v1, v1_out), (v2, v2_out), (n0, n0_out), (n1, n1_out), (n2, n2_out)):
-            dst[...] = src[...]
+        for k, (v_out, n_out) in enumerate(((v0_out, n0_out), (v1_out, n1_out), (v2_out, n2_out))):
+            v_out[...] = pack[k:k + 1, :]
+            n_out[...] = pack[3 + k:4 + k, 0:128]
         lane = lax.broadcasted_iota(jnp.int32, (1, 128), 1)
-        row = jnp.where(lane == 0, sig_ref[0:1, :], jnp.where(lane == 1, sig_ref[1:2, :], sig_ref[2:3, :]))
+        row = jnp.where(lane == 0, pack[6:7, 0:128], jnp.where(lane == 1, pack[7:8, 0:128], pack[8:9, 0:128]))
         sig_out[...] = row[:, :3]
 
 
-def final_kernel(loss_scale, own, other, g2, sig_ref, v0, v1, v2, n0, n1, n2, dw0, dw1, dw2, loss_out):
+def final_kernel(loss_scale, own, other, g2, pack, dw0, dw1, dw2, loss_out):
     stats = jnp.sum(own[256:264, :] + other[256:264, :], axis=1, keepdims=True)
     loss_out[...] = loss_scale * stats[0:1]
     grads = (own[128:256, :] + other[128:256, :], own[0:128, :] + other[0:128, :], g2[...])
-    for k, (grad, v_ref, n_ref, out) in enumerate(zip(grads, (v0, v1, v2), (n0, n1, n2), (dw0, dw1, dw2))):
-        inv = 1.0 / sig_ref[k:k + 1, 0:1]
-        u_col = jnp.transpose(jnp.broadcast_to(n_ref[...], (128, 128)))[:, 0:1]
-        out[...] = grad * inv - (stats[3 - k:4 - k] * inv) * (u_col * v_ref[...])
+    for k, (grad, out) in enumerate(zip(grads, (dw0, dw1, dw2))):
+        inv = 1.0 / pack[6 + k:7 + k, 0:1]
+        u_col = jnp.transpose(jnp.broadcast_to(pack[3 + k:4 + k, 0:128], (128, 128)))[:, 0:1]
+        out[...] = grad * inv - (stats[3 - k:4 - k] * inv) * (u_col * pack[k:k + 1, :])
 
 
 def solution(mesh):
@@ -323,15 +325,16 @@
                 jax.ShapeDtypeStruct((width, width), BF16),
                 jax.ShapeDtypeStruct((264, width), F32),
                 jax.ShapeDtypeStruct((128, width), F32),
-            ] + small + [jax.ShapeDtypeStruct((8, 128), F32)],
+                jax.ShapeDtypeStruct((16, width), F32),
+            ],
             in_specs=[any_spec] * 8,
-            out_specs=[any_spec] * 2 + [vmem_spec] * 9,
+            out_specs=[any_spec] * 2 + [vmem_spec] * 3,
             scratch_shapes=[pltpu.VMEM((half, width), BF16)] * 3 + [pltpu.VMEM((half, width), F32)] * 3 + [
                 pltpu.VMEM((4, half, 128), BF16),
                 pltpu.VMEM((3, width, width), BF16),
                 pltpu.VMEM((3, 4, 1, 128), F32),
                 pltpu.VMEM((half, width), BF16),
-                pltpu.VMEM((half, width), BF16),
+                pltpu.VMEM((half // NT, width), BF16),
                 pltpu.VMEM((half, width), BF16),
                 pltpu.VMEM((3, 2, 128, width), F32),
                 pltpu.VMEM((3, 128, width), F32),
@@ -349,8 +352,7 @@
                 collective_id=0, has_side_effects=True, vmem_limit_bytes=63 * 2**20),
             name="fused_step",
         )(x_in, w_in, w_mid, w_out, u_in.reshape(1, 128), u_mid.reshape(1, 128), u_out.reshape(1, 128), target)
-        e_all, w_full, dw_part, g2_sum = outs[:4]
-        vecs, sig = outs[4:10], outs[10]
+        e_all, w_full, dw_part, g2_sum, pack = outs
         other = lax.ppermute(dw_part, "data", [(0, 1), (1, 0)])
 
         block = 1024
@@ -360,22 +362,21 @@
             dx_kernel,
             grid=(rows // block,),
             out_shape=[jax.ShapeDtypeStruct((rows, width), BF16)] + small + [jax.ShapeDtypeStruct((1, 3), F32)],
-            in_specs=[pl.BlockSpec((block, width), lambda i: (i, 0)), full((width, width)), full((8, 128))] + vec_specs,
+            in_specs=[pl.BlockSpec((block, width), lambda i: (i, 0)), full((width, width)), full((16, width))],
             out_specs=[pl.BlockSpec((block, width), lambda i: (i, 0))] + vec_specs + [full((1, 3))],
             cost_estimate=pl.CostEstimate(flops=2 * rows * width * width, bytes_accessed=4 * rows * width, transcendentals=0),
-            compiler_params=pltpu.CompilerParams(vmem_limit_bytes=24 * 2**20),
             name="dx",
-        )(e_all, w_full, sig, *vecs)
+        )(e_all, w_full, pack)
         grad_x, sig_row = passed[0], passed[7]
 
         finals = pl.pallas_call(
             functools.partial(final_kernel, 0.5 / batch_total),
             out_shape=[jax.ShapeDtypeStruct((128, width), F32)] * 3 + [jax.ShapeDtypeStruct((1, 1), F32)],
-            in_specs=[vmem_spec] * 10,
+            in_specs=[vmem_spec] * 4,
             out_specs=[vmem_spec] * 4,
             compiler_params=pltpu.CompilerParams(vmem_limit_bytes=8 * 2**20),
             name="finish",
-        )(dw_part, other, g2_sum, sig, *vecs)
+        )(dw_part, other, g2_sum, pack)
         v_row, u_row = passed[1:4], passed[4:7]
         return (finals[3].reshape(1), grad_x, finals[0], finals[1], finals[2],
                 u_row[0].reshape(128), u_row[1].reshape(128), u_row[2].reshape(128),

time: 80 us -> 76.6 us (0.957)
  local copies, waits for them, and re-layouts: 9.06 us -> 0.01 us
  Pallas kernels: 68.8 us -> 72.3 us
  waiting for transfers between devices: 0.01 us -> 2.2 us
    unnamed x22 -> x6, local copies, waits for them, and re-layouts: 9.06 us -> 0.01 us
    pallas_call x1, Pallas kernels: 7.5 us -> 11 us  [local_step(): pl.pallas_call(dx_kernel, grid=(rows // block,), out_shape=[jax.ShapeDtyp...]
    ppermute x1, waiting for transfers between devices: 0.01 us -> 2.2 us  [local_step(): other = lax.ppermute(dw_part, 'data', [(0, 1), (1, 0)])]
  transfers between devices with their start and end apart: 1 -> 1, of which waited for: 0 -> 1; matrix products, arithmetic and copies ran while one was open for 0% -> 0% of each run, Pallas kernels for 9% -> 14%
where the time goes in v3:
time: 76.6 us; the launch traced here: 76.3 us
  Pallas kernels  72.3 us (94%)
  waiting for transfers between devices  2.2 us (3%)
  starting transfers between devices  1.12 us (1%)
    pallas_call x1, Pallas kernels, local_step(): pl.pallas_call(functools.partial(main_kernel, 1.0 / batch_total), out_sha...  60.2 us
    pallas_call x1, Pallas kernels, local_step(): pl.pallas_call(dx_kernel, grid=(rows // block,), out_shape=[jax.ShapeDtyp...  11 us
    ppermute x1, waiting for transfers between devices, local_step(): other = lax.ppermute(dw_part, 'data', [(0, 1), (1, 0)])  2.2 us
  transfers between devices with their start and end apart: 1, of which 1 were waited for; matrix products, arithmetic and copies ran while one was open for 0% of the time, Pallas kernels for 14%

profile of v3, /device:TPU:0, one launch (start us, length us, event | category | flops | bytes accessed | tf_op | source)
XLA Modules:
  0.0 76.3 jit_solution(14534281254081784142)
XLA Ops:
  0.6 60.2 %fused_step.1 = (bf16[8192,512]{1,0:T(8,128)(2,1)}, bf16[512,512]{1,0:T(8,128)(2,1)}, f32[264,512]{1,0:T(8,128)}, f32[128,512]{1,0:T(8,128)}, f32[16,512]{1,0:T(8,128)}) custom-call(bf16[8192,512]{1,0:T(8,128)(2,1)} %x_hbm.1, bf16[128,512]{1,0:T(8,128)(2,1)} %w0_hbm.1, bf16[128,512]{1,0:T(8,128)(2,1)} %w1_hbm.1, bf16[128,512]{1,0:T(8,128)(2,1)} %w2_hbm.1, ...), custom_call_target="tpu_custom_call" | custom-call | tf_op jit(solution)/shard_map/fused_step/pallas_call | solution.py:321
  60.8 0.0 copy-start
  60.9 0.0 copy-start.1
  60.9 0.0 copy-start.2
  60.9 1.1 %collective-permute-start = (f32[264,512]{1,0:T(8,128)}, f32[264,512]{1,0:T(8,128)S(1)}, u32[]{:S(2)}, u32[]{:S(2)}) collective-permute-start(f32[264,512]{1,0:T(8,128)} %get-tuple-element.29.own), channel_id=1, source_target_pairs={{0,4},{4,0},{1,5},{5,1},{2,6},{6,2},{3,7},{7,3}} | collective-permute-start | bytes 1622024 | tf_op jit(solution)/shard_map/ppermute | solution.py:356
  62.0 11.0 %dx.1 = (bf16[8192,512]{1,0:T(8,128)(2,1)}, f32[1,512]{1,0:T(1,128)}, f32[1,512]{1,0:T(1,128)}, f32[1,512]{1,0:T(1,128)}, f32[1,128]{1,0:T(1,128)}, /*index=5*/f...) custom-call(bf16[8192,512]{1,0:T(8,128)(2,1)} %get-tuple-element.33.e_ref, bf16[512,512]{1,0:T(8,128)(2,1)} %get-tuple-element.34.w_ref, ...), custom_call_target="tpu_custom_call" | custom-call | flops 4294967296 | bytes 16777216 | tf_op jit(solution)/shard_map/dx/pallas_call | solution.py:361
  73.0 2.2 %collective-permute-done.other = f32[264,512]{1,0:T(8,128)S(1)} collective-permute-done((f32[264,512]{1,0:T(8,128)}, f32[264,512]{1,0:T(8,128)S(1)}, u32[]{:S(2)}, u32[]{:S(2)}) %collective-permute-start) | collective-permute-done | bytes 540704 | tf_op jit(solution)/shard_map/ppermute | solution.py:356
  75.2 0.0 copy-done
  75.2 0.0 copy-done.1
  75.2 0.0 copy-done.2
  75.2 1.1 %finish.1 = (f32[128,512]{1,0:T(8,128)}, f32[128,512]{1,0:T(8,128)}, f32[128,512]{1,0:T(8,128)}, f32[1,1]{1,0:T(1,128)}) custom-call(f32[264,512]{1,0:T(8,128)S(1)} %copy-done, f32[264,512]{1,0:T(8,128)S(1)} %collective-permute-done.other, f32[128,512]{1,0:T(8,128)S(1)} %copy-done.1, f32[16,512]{1,0:T(8,128)S(1)} %copy-done.2), custom_call_target="tpu_custom_call" | custom-call | tf_op jit(solution)/shard_map/finish/pallas_call | solution.py:372
Async XLA Ops:
  60.8 14.3 %copy-start = (f32[264,512]{1,0:T(8,128)S(1)}, f32[264,512]{1,0:T(8,128)}, u32[]{:S(2)}) copy-start(f32[264,512]{1,0:T(8,128)} %get-tuple-element.29.own) | copy-start | bytes 1622020
  60.9 14.3 %copy-start.1 = (f32[128,512]{1,0:T(8,128)S(1)}, f32[128,512]{1,0:T(8,128)}, u32[]{:S(2)}) copy-start(f32[128,512]{1,0:T(8,128)} %get-tuple-element.30.g2) | copy-start | bytes 786436
  60.9 14.3 %copy-start.2 = (f32[16,512]{1,0:T(8,128)S(1)}, f32[16,512]{1,0:T(8,128)}, u32[]{:S(2)}) copy-start(f32[16,512]{1,0:T(8,128)} %get-tuple-element.31.pack) | copy-start | bytes 98308
  60.9 14.3 %collective-permute-start = (f32[264,512]{1,0:T(8,128)}, f32[264,512]{1,0:T(8,128)S(1)}, u32[]{:S(2)}, u32[]{:S(2)}) collective-permute-start(f32[264,512]{1,0:T(8,128)} %get-tuple-element.29.own), channel_id=1, source_target_pairs={{0,4},{4,0},{1,5},{5,1},{2,6},{6,2},{3,7},{7,3}} | collective-permute-start | bytes 1622024 | tf_op jit(solution)/shard_map/ppermute | solution.py:356

commit v4 on v3

v4 whole, which is shorter than its diff:
```python
import functools

import jax
import jax.numpy as jnp
from jax import lax
from jax.experimental import pallas as pl
from jax.experimental.pallas import tpu as pltpu
from jax.sharding import PartitionSpec as P

MESH = pl.DeviceIdType.MESH
F32 = jnp.float32
BF16 = jnp.bfloat16
DMA_ROWS = 256
FWD_ROWS = 1024
BIG_ROWS = 512
SHARED_ROWS = 512


def dot_nt(lhs, rhs):
    return lax.dot_general(lhs, rhs, (((1,), (1,)), ((), ())), preferred_element_type=F32)


def dot_nn(lhs, rhs):
    return lax.dot_general(lhs, rhs, (((1,), (0,)), ((), ())), preferred_element_type=F32)


def dot_tn(lhs, rhs):
    return lax.dot_general(lhs, rhs, (((0,), (0,)), ((), ())), preferred_element_type=F32)


def split_rows(vec):
    width = vec.shape[1]
    high = vec.astype(BF16).astype(F32)
    rest = vec - high
    mid = rest.astype(BF16).astype(F32)
    low = rest - mid
    row = lax.broadcasted_iota(jnp.int32, (16, width), 0)
    stacked = jnp.where(row == 0, high, jnp.where(row == 1, mid, jnp.where(row == 2, low, 0.0)))
    return stacked.astype(BF16)


def main_kernel(inv_batch, x_hbm, w0_hbm, w1_hbm, w2_hbm, u0_hbm, u1_hbm, u2_hbm, t_hbm,
                dx_out, tot_out, pack_out,
                x1, x2, y0, y1, y2, tbuf, wbuf, ubuf, e2, e1, e0, xfor, acc, facc, rbuf, frbuf, fsend,
                g_own, g_other, p_own, p_other, stat, fstat, sstat, rstat, fsstat, frstat, srow,
                w_send, w_recv, u_send, u_recv, t_send, t_recv, s_send, s_recv, e_send, e_recv, d_send, d_recv,
                f_send, f_recv, h_send, h_recv, l_w, l_u, l_t, l_x):
    rep, dat, mod = lax.axis_index("replica"), lax.axis_index("data"), lax.axis_index("model")
    core = lax.rem(mod, 2)
    chip = mod // 2
    sib = mod + 1 - 2 * core
    cnt = lax.rem(mod + 2, 4)
    crs = lax.rem(sib + 2, 4)
    p_sib, p_cnt, p_crs = (rep, dat, sib), (rep, dat, cnt), (rep, dat, crs)
    p_y, p_ys = (rep, 1 - dat, mod), (rep, 1 - dat, sib)
    rows_own = x_hbm.shape[0] // 2
    shared_at = rows_own - SHARED_ROWS
    row_base = core * rows_own
    n_dma = rows_own // DMA_ROWS
    n_shared = SHARED_ROWS // DMA_ROWS
    w_hbm = [w0_hbm, w1_hbm, w2_hbm]
    u_hbm = [u0_hbm, u1_hbm, u2_hbm]

    def remote(src, dst, ssem, rsem, peer):
        return pltpu.make_async_remote_copy(src_ref=src, dst_ref=dst, send_sem=ssem, recv_sem=rsem,
                                            device_id=peer, device_id_type=MESH)

    def span(start, size):
        return pl.ds(pl.multiple_of(start, size), size)

    def w_copy(layer, kind):
        ssem, rsem = w_send.at[layer, kind], w_recv.at[layer, kind]
        if kind == 0:
            return remote(w_hbm[layer], wbuf.at[layer, span(128 * mod, 128)], ssem, rsem, p_sib)
        if kind == 1:
            return remote(w_hbm[layer].at[span(64 * dat, 64)], wbuf.at[layer, span(128 * mod + 64 * dat, 64)], ssem, rsem, p_cnt)
        half = 1 - dat if kind == 4 else dat
        ref = wbuf.at[layer, span(128 * cnt + 64 * half, 64)]
        return remote(ref, ref, ssem, rsem, p_y if kind == 2 else p_sib)

    def u_copy(layer, kind):
        return remote(u_hbm[layer], ubuf.at[layer, mod], u_send.at[layer, kind], u_recv.at[layer, kind],
                      (p_sib, p_cnt, p_crs)[kind])

    def t_copy(kind, c):
        other_core = core if kind == 0 else 1 - core
        return remote(t_hbm.at[span(other_core * rows_own + c * DMA_ROWS, DMA_ROWS)], tbuf.at[mod, span(c * DMA_ROWS, DMA_ROWS)],
                      t_send.at[kind, c], t_recv.at[kind, c], p_cnt if kind == 0 else p_crs)

    def f_copy(kind):
        if kind == 0:
            src, dst, peer = x_hbm.at[span(row_base + shared_at, SHARED_ROWS)], xfor, p_y
        else:
            other_core = core if kind == 1 else 1 - core
            src = t_hbm.at[span(other_core * rows_own + shared_at, SHARED_ROWS)]
            dst, peer = tbuf.at[mod, span(rows_own, SHARED_ROWS)], p_y if kind == 1 else p_ys
        return remote(src, dst, f_send.at[kind], f_recv.at[kind], peer)

    def h_copy(kind, j):
        ref = tbuf.at[mod if kind == 0 else sib, span(rows_own + j * DMA_ROWS, DMA_ROWS)]
        return remote(ref, ref, h_send.at[kind, j], h_recv.at[kind, j], p_cnt)

    barrier = pltpu.get_barrier_semaphore()
    peers = (p_sib, p_cnt, p_crs, p_y, p_ys)
    for peer in peers:
        pl.semaphore_signal(barrier, inc=1, device_id=peer, device_id_type=MESH)
    local_w = [pltpu.make_async_copy(w_hbm[k], wbuf.at[k, span(128 * mod, 128)], l_w.at[k]) for k in range(3)]
    local_u = [pltpu.make_async_copy(u_hbm[k], ubuf.at[k, mod], l_u.at[k]) for k in range(3)]
    own_rows = span(row_base, rows_own)
    local_x = pltpu.make_async_copy(x_hbm.at[own_rows], dx_out.at[own_rows], l_x)
    local_t = pltpu.make_async_copy(t_hbm.at[own_rows], tbuf.at[mod, pl.ds(0, rows_own)], l_t)
    for k in range(3):
        local_w[k].start()
        local_u[k].start()
    local_x.start()
    local_t.start()
    pl.semaphore_wait(barrier, len(peers))

    for k in range(3):
        w_copy(k, 1).start()
        w_copy(k, 0).start()
        for kind in range(3):
            u_copy(k, kind).start()

    def start_targets(c, carry):
        t_copy(0, c).start()
        t_copy(1, c).start()
        return carry

    lax.fori_loop(0, n_dma, start_targets, 0)
    t_sib = remote(t_hbm.at[span((1 - core) * rows_own, rows_own)], tbuf.at[mod, pl.ds(0, rows_own)], s_send, s_recv, p_sib)
    t_sib.start()
    acc[...] = jnp.zeros_like(acc)
    facc[...] = jnp.zeros_like(facc)
    stat[...] = jnp.zeros_like(stat)
    fstat[...] = jnp.zeros_like(fstat)

    def relay_x(k):
        w_copy(k, 1).wait_recv()
        w_copy(k, 2).start()
        w_copy(k, 3).start()

    def relay_y(k):
        w_copy(k, 2).wait_recv()
        w_copy(k, 4).start()

    own_cols = span(256 * chip, 256)

    def fold(val):
        return jnp.sum(val.reshape(val.shape[0] // 8, 8, val.shape[1]), axis=0)

    def leaky(val):
        return jnp.maximum(val, 0.2 * val).astype(BF16)

    def add_grad(ref, e_val, x_val):
        part = dot_tn(e_val, x_val)
        ref[0] += part[:128]
        ref[1] += part[128:]

    def residual(y_val, slab, rows, sums, at):
        res = y_val - tbuf[slab, rows, :].astype(F32)
        grad = res * inv_batch
        if sums is not None:
            sums[0, :, at:at + 128] += fold(res * res)
            sums[1, :, at:at + 128] += fold(grad * y_val)
        e2[rows, span(128 * slab, 128)] = grad.astype(BF16)

    def last_layer(rows, sums):
        y_val = dot_nt(x2[rows, :], wbuf[2]) * inv_sigma[2]
        first = chip == 0
        own = jnp.where(first, y_val[:, :256], y_val[:, 256:])
        y2[rows, :] = jnp.where(first, y_val[:, 256:], y_val[:, :256])
        for j in range(2):
            residual(own[:, 128 * j:128 * j + 128], 2 * chip + j, rows, sums, 256 + 128 * j)

    inv_sigma = []
    relay_x(0)
    relay_y(0)
    for k in range(3):
        local_w[k].wait()
        local_u[k].wait()
        for kind in range(3):
            u_copy(k, kind).wait_recv()
        for kind in (0, 3, 4):
            w_copy(k, kind).wait_recv()
        u_row = jnp.concatenate([ubuf[k, j] for j in range(4)], axis=1)
        p_vec = jnp.sum(dot_nn(split_rows(u_row), wbuf[k]), axis=0, keepdims=True)
        norm = jnp.sqrt(jnp.sum(p_vec * p_vec, axis=1, keepdims=True))
        v_vec = p_vec / jnp.maximum(norm, 1e-12)
        s_vec = jnp.sum(dot_nt(split_rows(v_vec), wbuf[k]), axis=0, keepdims=True)
        sigma = jnp.sqrt(jnp.sum(s_vec * s_vec, axis=1, keepdims=True))
        pack_out[k:k + 1, :] = v_vec
        srow[k] = jnp.broadcast_to(s_vec / sigma, srow.shape[1:])
        pack_out[3 + k:4 + k, 0:128] = srow[k, 0:1, span(128 * mod, 128)]
        pack_out[6 + k:7 + k, :] = jnp.broadcast_to(sigma, (1, pack_out.shape[1]))
        inv = 1.0 / sigma
        inv_sigma.append(inv)
        if k < 2:
            relay_x(k + 1)
            relay_y(k + 1)
        if k == 0:
            local_x.wait()
        if k == 1:
            for kind in range(3):
                f_copy(kind).start()
        if k == 2:
            local_t.wait()
            t_sib.wait_recv()

        def forward(c, carry, k=k, inv=inv):
            rows = span(c * FWD_ROWS, FWD_ROWS)
            if k == 0:
                y_val = dot_nt(dx_out[span(row_base + c * FWD_ROWS, FWD_ROWS), :], wbuf[0]) * inv
                y0[rows, :] = y_val
                x1[rows, :] = leaky(y_val)
            elif k == 1:
                y_val = dot_nt(x1[rows, :], wbuf[1]) * inv
                y1[rows, :] = y_val
                x2[rows, :] = leaky(y_val)
            else:
                last_layer(rows, stat)
                add_grad(acc.at[2], e2[rows, own_cols], x2[rows, :])
            return carry

        lax.fori_loop(0, rows_own // FWD_ROWS, forward, 0)

    def d_copy(k):
        return remote(acc.at[k, 1 - core], rbuf.at[k], d_send.at[k], d_recv.at[k], p_sib)

    def fd_copy(k):
        return remote(fsend.at[k], frbuf.at[k], d_send.at[4 + k], d_recv.at[4 + k], p_sib)

    s_copy = remote(sstat, rstat, d_send.at[3], d_recv.at[3], p_sib)
    fs_copy = remote(fsstat, frstat, d_send.at[6], d_recv.at[6], p_sib)
    g_copy = remote(g_own, g_other, d_send.at[7], d_recv.at[7], p_y)
    p_copy = remote(p_own, p_other, d_send.at[8], d_recv.at[8], p_y)

    def dx_copy(idx, at, size):
        ref = dx_out.at[span(row_base + at, size)]
        return remote(ref, ref, e_send.at[idx], e_recv.at[idx], p_sib)

    def backward(at, size, sums, grad1, grad0, idx=None):
        rows = span(at, size)
        for j in range(2):
            residual(y2[rows, 128 * j:128 * j + 128], 2 - 2 * chip + j, rows, sums, 128 * j)
        back = (dot_nn(e2[rows, :], wbuf[2]) * inv_sigma[2]).astype(BF16).astype(F32)
        y_val = y1[rows, :]
        grad = back * jnp.where(y_val > 0, 1.0, 0.2)
        sums[2] += fold(grad * y_val)
        e1[:size] = grad.astype(BF16)
        back = (dot_nn(e1[:size], wbuf[1]) * inv_sigma[1]).astype(BF16).astype(F32)
        y_val = y0[rows, :]
        grad = back * jnp.where(y_val > 0, 1.0, 0.2)
        sums[3] += fold(grad * y_val)
        e0[:size] = grad.astype(BF16)
        if idx is None:
            add_grad(grad0, e0[:size, own_cols], xfor[span(at - rows_own, size), :])
            add_grad(grad1, e1[:size, own_cols], x1[rows, :])
        else:
            x_rows = span(row_base + at, size)
            add_grad(grad0, e0[:size, own_cols], dx_out[x_rows, :])
            dx_out[x_rows, :] = (dot_nn(e0[:size], wbuf[0]) * inv_sigma[0]).astype(BF16)
            add_grad(grad1, e1[:size, own_cols], x1[rows, :])
            dx_copy(idx, at, size).start()

    n_big = shared_at // BIG_ROWS - 1
    per_big = BIG_ROWS // DMA_ROWS

    def big_step(i, carry):
        @pl.when(i == 0)
        def _():
            d_copy(2).start()

        @pl.when(i == 1)
        def _():
            d_copy(2).wait_recv()
            g_own[...] = acc[2, core] + rbuf[2]

        @pl.when(i == 2)
        def _():
            g_copy.start()

        @pl.when(i == n_big - 2)
        def _():
            for kind in range(3):
                f_copy(kind).wait_recv()
            for j in range(n_shared):
                h_copy(0, j).start()
                h_copy(1, j).start()

        @pl.when(i == n_big - 1)
        def _():
            rows = pl.ds(rows_own, SHARED_ROWS)
            y_val = dot_nt(xfor[...], wbuf[0]) * inv_sigma[0]
            y0[rows, :] = y_val
            x1[rows, :] = leaky(y_val)
            y_val = dot_nt(x1[rows, :], wbuf[1]) * inv_sigma[1]
            y1[rows, :] = y_val
            x2[rows, :] = leaky(y_val)
            last_layer(rows, None)

        for c in range(per_big):
            t_copy(0, i * per_big + c).wait_recv()
            t_copy(1, i * per_big + c).wait_recv()
        backward(i * BIG_ROWS, BIG_ROWS, stat, acc.at[1], acc.at[0], i)
        return carry

    lax.fori_loop(0, n_big, big_step, 0)

    def small_step(c, carry):
        t_copy(0, c).wait_recv()
        t_copy(1, c).wait_recv()
        backward(c * DMA_ROWS, DMA_ROWS, stat, acc.at[1], acc.at[0], n_big + c - n_big * per_big)
        return carry

    lax.fori_loop(n_big * per_big, n_dma - n_shared, small_step, 0)

    row = lax.broadcasted_iota(jnp.int32, sstat.shape, 0)

    def gather_sums(ref_sums):
        mine = jnp.zeros(sstat.shape, F32)
        for i in range(4):
            mine = jnp.where(row == i, jnp.sum(ref_sums(i), axis=0, keepdims=True), mine)
        return mine

    d_copy(0).start()
    sstat[...] = gather_sums(lambda i: stat[i])
    d_copy(1).start()
    s_copy.start()
    d_copy(0).wait_recv()
    p_own[128:256, :] = acc[0, core] + rbuf[0]
    d_copy(1).wait_recv()
    p_own[0:128, :] = acc[1, core] + rbuf[1]
    s_copy.wait_recv()
    p_own[256:264, :] = sstat[...] + rstat[...]

    def shared_step(j, carry):
        t_copy(0, n_dma - n_shared + j).wait_recv()
        t_copy(1, n_dma - n_shared + j).wait_recv()

        @pl.when(j == 0)
        def _():
            p_copy.start()

        backward(shared_at + j * DMA_ROWS, DMA_ROWS, fstat.at[0], facc.at[0, 1], facc.at[0, 0], n_big + per_big + j)
        return carry

    lax.fori_loop(0, n_shared, shared_step, 0)

    def foreign_step(j, carry):
        h_copy(0, j).wait_recv()
        h_copy(1, j).wait_recv()
        backward(rows_own + j * DMA_ROWS, DMA_ROWS, fstat.at[1], facc.at[1, 1], facc.at[1, 0])
        return carry

    lax.fori_loop(0, n_shared, foreign_step, 0)

    for k in (0, 1):
        fsend[k] = facc[0, k, 1 - core] + facc[1, k, 1 - core]
    fsstat[...] = gather_sums(lambda i: fstat[0, i] + fstat[1, i])
    for k in (0, 1):
        fd_copy(k).start()
    fs_copy.start()
    g_copy.wait_recv()
    tot_out[256:384, :] = g_own[...] + g_other[...]
    p_copy.wait_recv()
    for i, k in enumerate((1, 0)):
        part = slice(128 * i, 128 * i + 128)
        fd_copy(k).wait_recv()
        tot_out[part, :] = (p_own[part, :] + p_other[part, :]) + ((facc[0, k, core] + facc[1, k, core]) + frbuf[k])
    fs_copy.wait_recv()
    tot_out[384:392, :] = (p_own[256:264, :] + p_other[256:264, :]) + (fsstat[...] + frstat[...])

    for k in range(3):
        d_copy(k).wait_send()
        for kind in range(5):
            w_copy(k, kind).wait_send()
        for kind in range(3):
            u_copy(k, kind).wait_send()
        f_copy(k).wait_send()
    for copy in (fd_copy(0), fd_copy(1), s_copy, fs_copy, g_copy, p_copy, t_sib):
        copy.wait_send()

    def drain_targets(c, carry):
        t_copy(0, c).wait_send()
        t_copy(1, c).wait_send()
        return carry

    lax.fori_loop(0, n_dma, drain_targets, 0)
    for j in range(n_shared):
        h_copy(0, j).wait_send()
        h_copy(1, j).wait_send()

    def drain_big(i, carry):
        dx_copy(i, i * BIG_ROWS, BIG_ROWS).wait()
        return carry

    lax.fori_loop(0, n_big, drain_big, 0)

    def drain_small(i, carry):
        dx_copy(n_big + i, n_big * BIG_ROWS + i * DMA_ROWS, DMA_ROWS).wait()
        return carry

    lax.fori_loop(0, per_big + n_shared, drain_small, 0)


def finish_kernel(loss_scale, dx_in, tot, pack, dx_ref, dw0, dw1, dw2, v0, v1, v2, n0, n1, n2, sig_out, loss_out, sems):
    parts = sems.shape[0]
    rows = dx_in.shape[0] // parts
    copies = [pltpu.make_async_copy(dx_in.at[pl.ds(i * rows, rows)], dx_ref.at[pl.ds(i * rows, rows)], sems.at[i]) for i in range(parts)]
    for copy in copies:
        copy.start()
    stats = jnp.sum(tot[384:392, :], axis=1, keepdims=True)
    loss_out[...] = loss_scale * stats[0:1]
    for k, (at, out, v_out, n_out) in enumerate(((128, dw0, v0, n0), (0, dw1, v1, n1), (256, dw2, v2, n2))):
        inv = 1.0 / pack[6 + k:7 + k, 0:1]
        v_out[...] = pack[k:k + 1, :]
        n_out[...] = pack[3 + k:4 + k, 0:128]
        u_col = jnp.transpose(jnp.broadcast_to(pack[3 + k:4 + k, 0:128], (128, 128)))[:, 0:1]
        out[...] = tot[at:at + 128, :] * inv - (stats[3 - k:4 - k] * inv) * (u_col * pack[k:k + 1, :])
    lane = lax.broadcasted_iota(jnp.int32, (1, 128), 1)
    row = jnp.where(lane == 0, pack[6:7, 0:128], jnp.where(lane == 1, pack[7:8, 0:128], pack[8:9, 0:128]))
    sig_out[...] = row[:, :3]
    for copy in copies:
        copy.wait()


def solution(mesh):
    data_size = mesh.shape["data"]
    row_spec = P(("replica", "model"), None)
    vec_spec = P(("replica", "model"))
    batch_spec = P(("replica", "data"), None)
    target_spec = P(("replica", "data"), "model")
    part_spec = P("replica")

    def local_step(x_in, w_in, w_mid, w_out, u_in, u_mid, u_out, target):
        rows, width = x_in.shape
        half = rows // 2
        ext = half + SHARED_ROWS
        batch_total = rows * data_size
        any_spec = pl.BlockSpec(memory_space=pl.ANY)
        vmem_spec = pl.BlockSpec(memory_space=pltpu.VMEM)
        dma = pltpu.SemaphoreType.DMA
        vm = pltpu.VMEM
        n_dma = half // DMA_ROWS
        n_shared = SHARED_ROWS // DMA_ROWS
        n_dx = (half - SHARED_ROWS) // BIG_ROWS - 1 + BIG_ROWS // DMA_ROWS + n_shared
        dx_all, tot, pack = pl.pallas_call(
            functools.partial(main_kernel, 1.0 / batch_total),
            out_shape=[vm((rows, width), BF16), vm((392, width), F32), vm((16, width), F32)],
            in_specs=[any_spec] * 8,
            out_specs=[vmem_spec] * 3,
            scratch_shapes=[
                vm((ext, width), BF16), vm((ext, width), BF16),
                vm((ext, width), F32), vm((ext, width), F32), vm((ext, 256), F32),
                vm((4, ext, 128), BF16),
                vm((3, width, width), BF16),
                vm((3, 4, 1, 128), F32),
                vm((ext, width), BF16), vm((BIG_ROWS, width), BF16), vm((BIG_ROWS, width), BF16),
                vm((SHARED_ROWS, width), BF16),
                vm((3, 2, 128, width), F32), vm((2, 2, 2, 128, width), F32),
                vm((3, 128, width), F32), vm((2, 128, width), F32), vm((2, 128, width), F32),
                vm((128, width), F32), vm((128, width), F32),
                vm((264, width), F32), vm((264, width), F32),
                vm((4, 8, width), F32), vm((2, 4, 8, width), F32),
                vm((8, width), F32), vm((8, width), F32), vm((8, width), F32), vm((8, width), F32),
                vm((3, 8, width), F32),
                dma((3, 5)), dma((3, 5)), dma((3, 3)), dma((3, 3)),
                dma((2, n_dma)), dma((2, n_dma)), dma(()), dma(()), dma((n_dx,)), dma((n_dx,)), dma((9,)), dma((9,)),
                dma((3,)), dma((3,)), dma((2, n_shared)), dma((2, n_shared)),
                dma((3,)), dma((3,)), dma(()), dma(()),
            ],
            compiler_params=pltpu.CompilerParams(
                collective_id=0, has_side_effects=True, vmem_limit_bytes=54 * 2**20),
            name="fused_step",
        )(x_in, w_in, w_mid, w_out, u_in.reshape(1, 128), u_mid.reshape(1, 128), u_out.reshape(1, 128), target)

        f32 = lambda *shape: jax.ShapeDtypeStruct(shape, F32)
        finals = pl.pallas_call(
            functools.partial(finish_kernel, 0.5 / batch_total),
            out_shape=[jax.ShapeDtypeStruct((rows, width), BF16)] + [f32(128, width)] * 3 + [f32(1, width)] * 3 + [
                f32(1, 128)] * 3 + [f32(1, 3), f32(1, 1)],
            in_specs=[vmem_spec] * 3,
            out_specs=[any_spec] + [vmem_spec] * 11,
            scratch_shapes=[dma((4,))],
            compiler_params=pltpu.CompilerParams(vmem_limit_bytes=8 * 2**20),
            name="finish",
        )(dx_all, tot, pack)
        grad_x, dw0, dw1, dw2, v0, v1, v2, n0, n1, n2, sig, loss = finals
        return (loss.reshape(1), grad_x, dw0, dw1, dw2, n0.reshape(128), n1.reshape(128), n2.reshape(128),
                v0.reshape(width), v1.reshape(width), v2.reshape(width), sig.reshape(3))

    in_specs = (batch_spec, row_spec, row_spec, row_spec, vec_spec, vec_spec, vec_spec, target_spec)
    out_specs = (part_spec, batch_spec, row_spec, row_spec, row_spec, vec_spec, vec_spec, vec_spec, part_spec, part_spec, part_spec, part_spec)
    return jax.shard_map(local_step, mesh=mesh, in_specs=in_specs, out_specs=out_specs, check_vma=False)
```

time: 76.6 us -> 72.8 us (0.950)
  waiting for transfers between devices: 2.2 us -> 0 us
  starting transfers between devices: 1.12 us -> 0 us
    pallas_call x2 -> x1, Pallas kernels: 12.1 us -> 4.27 us  [local_step(): pl.pallas_call(functools.partial(finish_kernel, 0.5 / batch_total), out_s...]
    pallas_call x1, Pallas kernels: 60.2 us -> 67.8 us  [local_step(): pl.pallas_call(functools.partial(main_kernel, 1.0 / batch_total), out_sha...]
    ppermute x1 -> x0, waiting for transfers between devices: 2.2 us -> none  [local_step(): other = lax.ppermute(dw_part, 'data', [(0, 1), (1, 0)])]
    ppermute x1 -> x0, starting transfers between devices: 1.12 us -> none  [local_step(): other = lax.ppermute(dw_part, 'data', [(0, 1), (1, 0)])]
  transfers between devices with their start and end apart: 1 -> 0, of which waited for: 1 -> 0; matrix products, arithmetic and copies ran while one was open for 0% -> 0% of each run, Pallas kernels for 14% -> 0%
where the time goes in v4:
time: 72.8 us; the launch traced here: 72.7 us
  Pallas kernels  72 us (99%)
    pallas_call x1, Pallas kernels, local_step(): pl.pallas_call(functools.partial(main_kernel, 1.0 / batch_total), out_sha...  67.8 us
    pallas_call x1, Pallas kernels, local_step(): pl.pallas_call(functools.partial(finish_kernel, 0.5 / batch_total), out_s...  4.27 us

profile of v4, /device:TPU:0, one launch (start us, length us, event | category | flops | bytes accessed | tf_op | source)
XLA Modules:
  0.0 72.7 jit_solution(3376189750876272300)
XLA Ops:
  0.6 67.8 %fused_step.1 = (bf16[8192,512]{1,0:T(8,128)(2,1)S(1)}, f32[392,512]{1,0:T(8,128)S(1)}, f32[16,512]{1,0:T(8,128)S(1)}) custom-call(bf16[8192,512]{1,0:T(8,128)(2,1)} %x_hbm.1, bf16[128,512]{1,0:T(8,128)(2,1)} %w0_hbm.1, bf16[128,512]{1,0:T(8,128)(2,1)} %w1_hbm.1, bf16[128,512]{1,0:T(8,128)(2,1)} %w2_hbm.1, f32[1,128]{1,0:T(1,128)} %bitcast.11, ...), custom_call_target="tpu_custom_call" | custom-call | tf_op jit(solution)/shard_map/fused_step/pallas_call | solution.py:448
  68.4 4.3 %finish.1 = (bf16[8192,512]{1,0:T(8,128)(2,1)}, f32[128,512]{1,0:T(8,128)}, f32[128,512]{1,0:T(8,128)}, f32[128,512]{1,0:T(8,128)}, f32[1,512]{1,0:T(1,128)}, /*...) custom-call(bf16[8192,512]{1,0:T(8,128)(2,1)S(1)} %get-tuple-element, ...), custom_call_target="tpu_custom_call" | custom-call | tf_op jit(solution)/shard_map/finish/pallas_call | solution.py:479

commit v5 on v4

v5 whole, which is shorter than its diff:
```python
import functools

import jax
import jax.numpy as jnp
from jax import lax
from jax.experimental import pallas as pl
from jax.experimental.pallas import tpu as pltpu
from jax.sharding import PartitionSpec as P

MESH = pl.DeviceIdType.MESH
F32 = jnp.float32
BF16 = jnp.bfloat16
FWD_ROWS = 1024
BIG_ROWS = 512
PLAIN = ((512, 6), (256, 1), (128, 1))
SHARED = ((256, 2), (128, 1))
SHARED_ROWS = sum(size * count for size, count in SHARED)
N_PLAIN = sum(count for _, count in PLAIN)
N_SHARED = sum(count for _, count in SHARED)


def dot_nt(lhs, rhs):
    return lax.dot_general(lhs, rhs, (((1,), (1,)), ((), ())), preferred_element_type=F32)


def dot_nn(lhs, rhs):
    return lax.dot_general(lhs, rhs, (((1,), (0,)), ((), ())), preferred_element_type=F32)


def dot_tn(lhs, rhs):
    return lax.dot_general(lhs, rhs, (((0,), (0,)), ((), ())), preferred_element_type=F32)


def split_rows(vec):
    width = vec.shape[1]
    high = vec.astype(BF16).astype(F32)
    rest = vec - high
    mid = rest.astype(BF16).astype(F32)
    low = rest - mid
    row = lax.broadcasted_iota(jnp.int32, (16, width), 0)
    stacked = jnp.where(row == 0, high, jnp.where(row == 1, mid, jnp.where(row == 2, low, 0.0)))
    return stacked.astype(BF16)


def main_kernel(inv_batch, x_hbm, w0_hbm, w1_hbm, w2_hbm, u0_hbm, u1_hbm, u2_hbm, t_hbm,
                dx_out, tot_out, pack_out,
                x1, x2, y0, y1, y2, tbuf, wbuf, ubuf, e2, e1, e0, xfor, acc, facc, rbuf, frbuf, fsend,
                g_own, g_other, p_own, p_other, stat, fstat, sstat, rstat, fsstat, frstat, srow,
                w_send, w_recv, u_send, u_recv, t_send, t_recv, s_send, s_recv, e_send, e_recv, d_send, d_recv,
                f_send, f_recv, h_send, h_recv, l_w, l_u, l_t, l_x):
    rep, dat, mod = lax.axis_index("replica"), lax.axis_index("data"), lax.axis_index("model")
    core = lax.rem(mod, 2)
    chip = mod // 2
    sib = mod + 1 - 2 * core
    cnt = lax.rem(mod + 2, 4)
    crs = lax.rem(sib + 2, 4)
    p_sib, p_cnt, p_crs = (rep, dat, sib), (rep, dat, cnt), (rep, dat, crs)
    p_y, p_ys = (rep, 1 - dat, mod), (rep, 1 - dat, sib)
    rows_own = x_hbm.shape[0] // 2
    shared_at = rows_own - SHARED_ROWS
    row_base = core * rows_own

    def each_chunk(groups, first, at, body):
        for size, count in groups:
            def step(i, carry, size=size, first=first, at=at):
                body(first + i, at + i * size, size)
                return carry
            if count == 1:
                step(0, 0)
            else:
                lax.fori_loop(0, count, step, 0)
            first, at = first + count, at + size * count
    w_hbm = [w0_hbm, w1_hbm, w2_hbm]
    u_hbm = [u0_hbm, u1_hbm, u2_hbm]

    def remote(src, dst, ssem, rsem, peer):
        return pltpu.make_async_remote_copy(src_ref=src, dst_ref=dst, send_sem=ssem, recv_sem=rsem,
                                            device_id=peer, device_id_type=MESH)

    def arrived(ref, sem):
        pltpu.make_async_copy(ref, ref, sem).wait()

    def span(start, size):
        return pl.ds(pl.multiple_of(start, size), size)

    def tile(start, size):
        return pl.ds(pl.multiple_of(start, 128), size)

    def w_copy(layer, kind):
        ssem, rsem = w_send, w_recv.at[layer, (0, 1, 2, 0, 0)[kind]]
        if kind == 0:
            return remote(w_hbm[layer], wbuf.at[layer, span(128 * mod, 128)], ssem, rsem, p_sib)
        if kind == 1:
            return remote(w_hbm[layer].at[span(64 * dat, 64)], wbuf.at[layer, span(128 * mod + 64 * dat, 64)], ssem, rsem, p_cnt)
        half = 1 - dat if kind == 4 else dat
        ref = wbuf.at[layer, span(128 * cnt + 64 * half, 64)]
        return remote(ref, ref, ssem, rsem, p_y if kind == 2 else p_sib)

    def u_copy(kind):
        ref = ubuf.at[:, mod]
        return remote(ref, ref, u_send, u_recv, (p_sib, p_cnt, p_crs)[kind])

    def t_copy(kind, idx, at, size):
        other_core = core if kind == 0 else 1 - core
        return remote(t_hbm.at[tile(other_core * rows_own + at, size)], tbuf.at[mod, tile(at, size)],
                      t_send, t_recv.at[idx], p_cnt if kind == 0 else p_crs)

    def f_copy(kind):
        if kind == 0:
            src, dst, peer = x_hbm.at[tile(row_base + shared_at, SHARED_ROWS)], xfor, p_y
        else:
            other_core = core if kind == 1 else 1 - core
            src = t_hbm.at[tile(other_core * rows_own + shared_at, SHARED_ROWS)]
            dst, peer = tbuf.at[mod, tile(rows_own, SHARED_ROWS)], p_y if kind == 1 else p_ys
        return remote(src, dst, f_send, f_recv, peer)

    def h_copy(kind, idx, at, size):
        ref = tbuf.at[mod if kind == 0 else sib, tile(at, size)]
        return remote(ref, ref, h_send, h_recv.at[idx], p_cnt)

    barrier = pltpu.get_barrier_semaphore()
    peers = (p_sib, p_cnt, p_crs, p_y, p_ys)
    for peer in peers:
        pl.semaphore_signal(barrier, inc=1, device_id=peer, device_id_type=MESH)
    local_w = [pltpu.make_async_copy(w_hbm[k], wbuf.at[k, span(128 * mod, 128)], l_w.at[k]) for k in range(3)]
    local_u = [pltpu.make_async_copy(u_hbm[k], ubuf.at[k, mod], l_u.at[k]) for k in range(3)]
    own_rows = span(row_base, rows_own)
    local_x = pltpu.make_async_copy(x_hbm.at[own_rows], dx_out.at[own_rows], l_x)
    local_t = pltpu.make_async_copy(t_hbm.at[own_rows], tbuf.at[mod, pl.ds(0, rows_own)], l_t)
    for k in range(3):
        local_w[k].start()
        local_u[k].start()
    local_x.start()
    local_t.start()
    pl.semaphore_wait(barrier, len(peers))

    for k in range(3):
        w_copy(k, 1).start()
        w_copy(k, 0).start()

    for copy in local_u:
        copy.wait()
    for kind in range(3):
        u_copy(kind).start()

    def start_targets(idx, at, size):
        t_copy(0, idx, at, size).start()
        t_copy(1, idx, at, size).start()

    each_chunk(PLAIN + SHARED, 0, 0, start_targets)
    t_sib = remote(t_hbm.at[span((1 - core) * rows_own, rows_own)], tbuf.at[mod, pl.ds(0, rows_own)], s_send, s_recv, p_sib)
    t_sib.start()
    acc[...] = jnp.zeros_like(acc)
    facc[...] = jnp.zeros_like(facc)
    stat[...] = jnp.zeros_like(stat)
    fstat[...] = jnp.zeros_like(fstat)

    def relay_x(k):
        w_copy(k, 1).wait_recv()
        w_copy(k, 2).start()
        w_copy(k, 3).start()

    def relay_y(k):
        w_copy(k, 2).wait_recv()
        w_copy(k, 4).start()

    own_cols = span(256 * chip, 256)

    def fold(val):
        return jnp.sum(val.reshape(val.shape[0] // 8, 8, val.shape[1]), axis=0)

    def leaky(val):
        return jnp.maximum(val, 0.2 * val).astype(BF16)

    def add_grad(ref, e_val, x_val):
        part = dot_tn(e_val, x_val)
        ref[0] += part[:128]
        ref[1] += part[128:]

    def residual(y_val, slab, rows, sums, at):
        res = y_val - tbuf[slab, rows, :].astype(F32)
        grad = res * inv_batch
        if sums is not None:
            sums[0, :, at:at + 128] += fold(res * res)
            sums[1, :, at:at + 128] += fold(grad * y_val)
        e2[rows, span(128 * slab, 128)] = grad.astype(BF16)

    def last_layer(rows, sums):
        y_val = dot_nt(x2[rows, :], wbuf[2]) * inv_sigma[2]
        first = chip == 0
        own = jnp.where(first, y_val[:, :256], y_val[:, 256:])
        y2[rows, :] = jnp.where(first, y_val[:, 256:], y_val[:, :256])
        for j in range(2):
            residual(own[:, 128 * j:128 * j + 128], 2 * chip + j, rows, sums, 256 + 128 * j)

    inv_sigma = []
    for k in range(3):
        relay_x(k)
    for kind in range(3):
        f_copy(kind).start()
    relay_y(0)
    relay_y(1)
    for k in range(3):
        local_w[k].wait()
        if k == 0:
            arrived(ubuf.at[:, pl.ds(0, 3)], u_recv)
        arrived(wbuf.at[k, pl.ds(0, 256)], w_recv.at[k, 0])
        u_row = jnp.concatenate([ubuf[k, j] for j in range(4)], axis=1)
        p_vec = jnp.sum(dot_nn(split_rows(u_row), wbuf[k]), axis=0, keepdims=True)
        norm = jnp.sqrt(jnp.sum(p_vec * p_vec, axis=1, keepdims=True))
        v_vec = p_vec / jnp.maximum(norm, 1e-12)
        s_vec = jnp.sum(dot_nt(split_rows(v_vec), wbuf[k]), axis=0, keepdims=True)
        sigma = jnp.sqrt(jnp.sum(s_vec * s_vec, axis=1, keepdims=True))
        pack_out[k:k + 1, :] = v_vec
        srow[k] = jnp.broadcast_to(s_vec / sigma, srow.shape[1:])
        pack_out[3 + k:4 + k, 0:128] = srow[k, 0:1, span(128 * mod, 128)]
        pack_out[6 + k:7 + k, :] = jnp.broadcast_to(sigma, (1, pack_out.shape[1]))
        inv = 1.0 / sigma
        inv_sigma.append(inv)
        if k == 0:
            relay_y(2)
        if k == 0:
            local_x.wait()
        if k == 2:
            local_t.wait()
            t_sib.wait_recv()

        def forward(c, carry, k=k, inv=inv):
            rows = span(c * FWD_ROWS, FWD_ROWS)
            if k == 0:
                y_val = dot_nt(dx_out[span(row_base + c * FWD_ROWS, FWD_ROWS), :], wbuf[0]) * inv
                y0[rows, :] = y_val
                x1[rows, :] = leaky(y_val)
            elif k == 1:
                y_val = dot_nt(x1[rows, :], wbuf[1]) * inv
                y1[rows, :] = y_val
                x2[rows, :] = leaky(y_val)
            else:
                last_layer(rows, stat)
                add_grad(acc.at[2], e2[rows, own_cols], x2[rows, :])
            return carry

        lax.fori_loop(0, rows_own // FWD_ROWS, forward, 0)

    def d_copy(k):
        return remote(acc.at[k, 1 - core], rbuf.at[k], d_send, d_recv.at[k], p_sib)

    def fd_copy(k):
        return remote(fsend.at[k], frbuf.at[k], d_send, d_recv.at[4 + k], p_sib)

    def p_copy(k):
        part = pl.ds((256, 0, 128)[k], (8, 128, 128)[k])
        return remote(p_own.at[part], p_other.at[part], d_send, d_recv.at[8 + k], p_y)

    s_copy = remote(sstat, rstat, d_send, d_recv.at[3], p_sib)
    fs_copy = remote(fsstat, frstat, d_send, d_recv.at[6], p_sib)
    g_copy = remote(g_own, g_other, d_send, d_recv.at[7], p_y)

    def dx_copy(at, size):
        ref = dx_out.at[tile(row_base + at, size)]
        return remote(ref, ref, e_send, e_recv, p_sib)

    def backward(at, size, sums, grads, idx=None, mid=None):
        rows = tile(at, size)
        for j in range(2):
            residual(y2[rows, 128 * j:128 * j + 128], 2 - 2 * chip + j, rows, sums, 128 * j)
        back = (dot_nn(e2[rows, :], wbuf[2]) * inv_sigma[2]).astype(BF16).astype(F32)
        y_val = y1[rows, :]
        grad = back * jnp.where(y_val > 0, 1.0, 0.2)
        sums[2] += fold(grad * y_val)
        e1[:size] = grad.astype(BF16)
        add_grad(grads.at[1], e1[:size, own_cols], x1[rows, :])
        back = (dot_nn(e1[:size], wbuf[1]) * inv_sigma[1]).astype(BF16).astype(F32)
        y_val = y0[rows, :]
        grad = back * jnp.where(y_val > 0, 1.0, 0.2)
        sums[3] += fold(grad * y_val)
        e0[:size] = grad.astype(BF16)
        if mid is not None:
            mid(1)
        if idx is None:
            add_grad(grads.at[0], e0[:size, own_cols], xfor[tile(at - rows_own, size), :])
            if mid is not None:
                mid(0)
        else:
            x_rows = tile(row_base + at, size)
            add_grad(grads.at[0], e0[:size, own_cols], dx_out[x_rows, :])
            if mid is not None:
                mid(0)
            dx_out[x_rows, :] = (dot_nn(e0[:size], wbuf[0]) * inv_sigma[0]).astype(BF16)

    row = lax.broadcasted_iota(jnp.int32, sstat.shape, 0)

    def gather_sums(ref_sums):
        mine = jnp.zeros(sstat.shape, F32)
        for i in range(4):
            mine = jnp.where(row == i, jnp.sum(ref_sums(i), axis=0, keepdims=True), mine)
        return mine

    def own_chunk(idx, at, size, sums, grads, mid=None):
        arrived(tbuf.at[pl.ds(0, 2), tile(at, size)], t_recv.at[idx])
        backward(at, size, sums, grads, idx, mid)

    n_big = PLAIN[0][1]

    def plain_send(k):
        if k == 0:
            sstat[...] = gather_sums(lambda i: stat[i])
        d_copy(k).start()
        if k == 0:
            s_copy.start()

    def plain_chunk(idx, at, size):
        if size == BIG_ROWS:
            @pl.when(idx == 0)
            def _():
                d_copy(2).start()

            @pl.when(idx == 1)
            def _():
                d_copy(2).wait_recv()
                g_own[...] = acc[2, core] + rbuf[2]

            @pl.when(idx == 2)
            def _():
                g_copy.start()

            @pl.when(idx == n_big - 2)
            def _():
                arrived(x1.at[pl.ds(0, 3 * SHARED_ROWS // 2)], f_recv)

                def forward_on(j, h_at, h_size):
                    h_copy(0, j, h_at, h_size).start()
                    h_copy(1, j, h_at, h_size).start()

                each_chunk(SHARED, 0, rows_own, forward_on)

            @pl.when(idx == n_big - 1)
            def _():
                rows = pl.ds(rows_own, SHARED_ROWS)
                y_val = dot_nt(xfor[...], wbuf[0]) * inv_sigma[0]
                y0[rows, :] = y_val
                x1[rows, :] = leaky(y_val)
                y_val = dot_nt(x1[rows, :], wbuf[1]) * inv_sigma[1]
                y1[rows, :] = y_val
                x2[rows, :] = leaky(y_val)
                last_layer(rows, None)

        last = isinstance(at, int) and at + size == shared_at
        own_chunk(idx, at, size, stat, acc, plain_send if last else None)
        dx_copy(at, size).start()

    each_chunk(PLAIN, 0, 0, plain_chunk)

    d_copy(1).wait_recv()
    p_own[0:128, :] = acc[1, core] + rbuf[1]
    d_copy(0).wait_recv()
    p_copy(1).start()
    p_own[128:256, :] = acc[0, core] + rbuf[0]
    s_copy.wait_recv()
    p_copy(2).start()
    p_own[256:264, :] = sstat[...] + rstat[...]

    def shared_chunk(idx, at, size):
        own_chunk(idx, at, size, fstat.at[0], facc.at[0])
        dx_copy(at, size).start()

        @pl.when(idx == N_PLAIN)
        def _():
            p_copy(0).start()

    each_chunk(SHARED, N_PLAIN, shared_at, shared_chunk)

    def last_send(k):
        fsend[k] = facc[0, k, 1 - core] + facc[1, k, 1 - core]
        if k == 0:
            fd_copy(1).start()
            fsstat[...] = gather_sums(lambda i: fstat[0, i] + fstat[1, i])
            fd_copy(0).start()
            fs_copy.start()

    def foreign_chunk(idx, at, size):
        arrived(tbuf.at[pl.ds(0, 2), tile(at, size)], h_recv.at[idx])
        last = isinstance(at, int) and at + size == rows_own + SHARED_ROWS
        backward(at, size, fstat.at[1], facc.at[1], None, last_send if last else None)

    each_chunk(SHARED, 0, rows_own, foreign_chunk)

    g_copy.wait_recv()
    tot_out[256:384, :] = g_own[...] + g_other[...]
    for k in range(3):
        p_copy(k).wait_recv()
    for i, k in enumerate((1, 0)):
        part = slice(128 * i, 128 * i + 128)
        fd_copy(k).wait_recv()
        tot_out[part, :] = (p_own[part, :] + p_other[part, :]) + ((facc[0, k, core] + facc[1, k, core]) + frbuf[k])
    fs_copy.wait_recv()
    tot_out[384:392, :] = (p_own[256:264, :] + p_other[256:264, :]) + (fsstat[...] + frstat[...])

    arrived(x1.at[pl.ds(0, 3 * 384)], w_send)
    arrived(ubuf.at[:, pl.ds(0, 3)], u_send)
    arrived(t_hbm, t_send)
    arrived(tbuf.at[mod, pl.ds(0, rows_own)], s_send)
    arrived(x1.at[pl.ds(0, 3 * SHARED_ROWS // 2)], f_send)
    arrived(tbuf.at[pl.ds(0, 2), pl.ds(rows_own, SHARED_ROWS)], h_send)
    arrived(y0.at[pl.ds(0, 8 * 128 + 24)], d_send)
    arrived(dx_out.at[own_rows], e_send)
    arrived(dx_out.at[own_rows], e_recv)


def finish_kernel(loss_scale, dx_in, tot, pack, dx_ref, dw0, dw1, dw2, v0, v1, v2, n0, n1, n2, sig_out, loss_out,
                  grads, sig_row, loss_row, sems, out_sems):
    parts = sems.shape[0]
    rows = dx_in.shape[0] // parts
    copies = [pltpu.make_async_copy(dx_in.at[pl.ds(i * rows, rows)], dx_ref.at[pl.ds(i * rows, rows)], sems.at[i]) for i in range(parts)]
    for copy in copies:
        copy.start()

    def out_copy(src, dst):
        copy = pltpu.make_async_copy(src, dst, out_sems.at[len(copies) - parts])
        copy.start()
        copies.append(copy)

    for k, (v_out, n_out) in enumerate(((v0, n0), (v1, n1), (v2, n2))):
        out_copy(pack.at[k:k + 1, :], v_out)
        out_copy(pack.at[3 + k:4 + k, 0:128], n_out)
    lane = lax.broadcasted_iota(jnp.int32, (1, 128), 1)
    row = jnp.where(lane == 0, pack[6:7, 0:128], jnp.where(lane == 1, pack[7:8, 0:128], pack[8:9, 0:128]))
    sig_row[...] = row[:, :3]
    stats = jnp.sum(tot[384:392, :], axis=1, keepdims=True)
    loss_row[...] = loss_scale * stats[0:1]
    for k, at in enumerate((128, 0, 256)):
        inv = 1.0 / pack[6 + k:7 + k, 0:1]
        u_col = jnp.transpose(jnp.broadcast_to(pack[3 + k:4 + k, 0:128], (128, 128)))[:, 0:1]
        grads[k] = tot[at:at + 128, :] * inv - (stats[3 - k:4 - k] * inv) * (u_col * pack[k:k + 1, :])
    out_copy(sig_row, sig_out)
    out_copy(loss_row, loss_out)
    for k, out in enumerate((dw0, dw1, dw2)):
        out_copy(grads.at[k], out)
    for copy in copies:
        copy.wait()


def solution(mesh):
    data_size = mesh.shape["data"]
    row_spec = P(("replica", "model"), None)
    vec_spec = P(("replica", "model"))
    batch_spec = P(("replica", "data"), None)
    target_spec = P(("replica", "data"), "model")
    part_spec = P("replica")

    def local_step(x_in, w_in, w_mid, w_out, u_in, u_mid, u_out, target):
        rows, width = x_in.shape
        half = rows // 2
        ext = half + SHARED_ROWS
        batch_total = rows * data_size
        any_spec = pl.BlockSpec(memory_space=pl.ANY)
        vmem_spec = pl.BlockSpec(memory_space=pltpu.VMEM)
        dma = pltpu.SemaphoreType.DMA
        vm = pltpu.VMEM
        dx_all, tot, pack = pl.pallas_call(
            functools.partial(main_kernel, 1.0 / batch_total),
            out_shape=[vm((rows, width), BF16), vm((392, width), F32), vm((16, width), F32)],
            in_specs=[any_spec] * 8,
            out_specs=[vmem_spec] * 3,
            scratch_shapes=[
                vm((ext, width), BF16), vm((ext, width), BF16),
                vm((ext, width), F32), vm((ext, width), F32), vm((ext, 256), F32),
                vm((4, ext, 128), BF16),
                vm((3, width, width), BF16),
                vm((3, 4, 1, 128), F32),
                vm((ext, width), BF16), vm((BIG_ROWS, width), BF16), vm((BIG_ROWS, width), BF16),
                vm((SHARED_ROWS, width), BF16),
                vm((3, 2, 128, width), F32), vm((2, 2, 2, 128, width), F32),
                vm((3, 128, width), F32), vm((2, 128, width), F32), vm((2, 128, width), F32),
                vm((128, width), F32), vm((128, width), F32),
                vm((264, width), F32), vm((264, width), F32),
                vm((4, 8, width), F32), vm((2, 4, 8, width), F32),
                vm((8, width), F32), vm((8, width), F32), vm((8, width), F32), vm((8, width), F32),
                vm((3, 8, width), F32),
                dma(()), dma((3, 3)), dma(()), dma(()),
                dma(()), dma((N_PLAIN + N_SHARED,)), dma(()), dma(()), dma(()), dma(()), dma(()), dma((11,)),
                dma(()), dma(()), dma(()), dma((N_SHARED,)),
                dma((3,)), dma((3,)), dma(()), dma(()),
            ],
            compiler_params=pltpu.CompilerParams(
                collective_id=0, has_side_effects=True, vmem_limit_bytes=55 * 2**20),
            name="fused_step",
        )(x_in, w_in, w_mid, w_out, u_in.reshape(1, 128), u_mid.reshape(1, 128), u_out.reshape(1, 128), target)

        f32 = lambda *shape: jax.ShapeDtypeStruct(shape, F32)
        finals = pl.pallas_call(
            functools.partial(finish_kernel, 0.5 / batch_total),
            out_shape=[jax.ShapeDtypeStruct((rows, width), BF16)] + [f32(128, width)] * 3 + [f32(1, width)] * 3 + [
                f32(1, 128)] * 3 + [f32(1, 3), f32(1, 1)],
            in_specs=[vmem_spec] * 3,
            out_specs=[any_spec] * 12,
            scratch_shapes=[vm((3, 128, width), F32), vm((1, 3), F32), vm((1, 1), F32), dma((4,)), dma((11,))],
            compiler_params=pltpu.CompilerParams(vmem_limit_bytes=8 * 2**20),
            name="finish",
        )(dx_all, tot, pack)
        grad_x, dw0, dw1, dw2, v0, v1, v2, n0, n1, n2, sig, loss = finals
        return (loss.reshape(1), grad_x, dw0, dw1, dw2, n0.reshape(128), n1.reshape(128), n2.reshape(128),
                v0.reshape(width), v1.reshape(width), v2.reshape(width), sig.reshape(3))

    in_specs = (batch_spec, row_spec, row_spec, row_spec, vec_spec, vec_spec, vec_spec, target_spec)
    out_specs = (part_spec, batch_spec, row_spec, row_spec, row_spec, vec_spec, vec_spec, vec_spec, part_spec, part_spec, part_spec, part_spec)
    return jax.shard_map(local_step, mesh=mesh, in_specs=in_specs, out_specs=out_specs, check_vma=False)
```

time: 72.8 us -> 69.8 us (0.959)
  Pallas kernels: 72 us -> 69.1 us
    pallas_call x1, Pallas kernels: 67.8 us -> 65.4 us  [local_step(): pl.pallas_call(functools.partial(main_kernel, 1.0 / batch_total), out_sha...]
where the time goes in v5:
time: 69.8 us; the launch traced here: 69.7 us
  Pallas kernels  69.1 us (99%)
    pallas_call x1, Pallas kernels, local_step(): pl.pallas_call(functools.partial(main_kernel, 1.0 / batch_total), out_sha...  65.4 us
    pallas_call x1, Pallas kernels, local_step(): pl.pallas_call(functools.partial(finish_kernel, 0.5 / batch_total), out_s...  3.67 us

profile of v5, /device:TPU:0, one launch (start us, length us, event | category | flops | bytes accessed | tf_op | source)
XLA Modules:
  0.0 69.7 jit_solution(11176311502791931648)
XLA Ops:
  0.6 65.4 %fused_step.1 = (bf16[8192,512]{1,0:T(8,128)(2,1)S(1)}, f32[392,512]{1,0:T(8,128)S(1)}, f32[16,512]{1,0:T(8,128)S(1)}) custom-call(bf16[8192,512]{1,0:T(8,128)(2,1)} %x_hbm.1, bf16[128,512]{1,0:T(8,128)(2,1)} %w0_hbm.1, bf16[128,512]{1,0:T(8,128)(2,1)} %w1_hbm.1, bf16[128,512]{1,0:T(8,128)(2,1)} %w2_hbm.1, f32[1,128]{1,0:T(1,128)} %bitcast.11, ...), custom_call_target="tpu_custom_call" | custom-call | tf_op jit(solution)/shard_map/fused_step/pallas_call | solution.py:460
  66.1 3.7 %finish.1 = (bf16[8192,512]{1,0:T(8,128)(2,1)}, f32[128,512]{1,0:T(8,128)}, f32[128,512]{1,0:T(8,128)}, f32[128,512]{1,0:T(8,128)}, f32[1,512]{1,0:T(1,128)}, /*...) custom-call(bf16[8192,512]{1,0:T(8,128)(2,1)S(1)} %get-tuple-element, ...), custom_call_target="tpu_custom_call" | custom-call | tf_op jit(solution)/shard_map/finish/pallas_call | solution.py:491

commit v6 on v5

--- a/solution.py
+++ b/solution.py
@@ -12,10 +12,11 @@
 BF16 = jnp.bfloat16
 FWD_ROWS = 1024
 BIG_ROWS = 512
-PLAIN = ((512, 6), (256, 1), (128, 1))
-SHARED = ((256, 2), (128, 1))
+PLAIN = ((512, 6), (256, 1), (192, 1))
+SHARED = ((256, 1), (192, 1), (128, 1))
 SHARED_ROWS = sum(size * count for size, count in SHARED)
 N_PLAIN = sum(count for _, count in PLAIN)
+LAST = PLAIN[-1][0]
 N_SHARED = sum(count for _, count in SHARED)
 
 
@@ -45,9 +46,9 @@
 def main_kernel(inv_batch, x_hbm, w0_hbm, w1_hbm, w2_hbm, u0_hbm, u1_hbm, u2_hbm, t_hbm,
                 dx_out, tot_out, pack_out,
                 x1, x2, y0, y1, y2, tbuf, wbuf, ubuf, e2, e1, e0, xfor, acc, facc, rbuf, frbuf, fsend,
-                g_own, g_other, p_own, p_other, stat, fstat, sstat, rstat, fsstat, frstat, srow,
+                g_own, g_other, p_own, p_other, stat, fstat, sstat, rstat, fsstat, frstat, srow, sx, se, eq,
                 w_send, w_recv, u_send, u_recv, t_send, t_recv, s_send, s_recv, e_send, e_recv, d_send, d_recv,
-                f_send, f_recv, h_send, h_recv, l_w, l_u, l_t, l_x):
+                f_send, f_recv, h_send, h_recv, q_send, q_recv, l_w, l_u, l_t, l_x, l_q):
     rep, dat, mod = lax.axis_index("replica"), lax.axis_index("data"), lax.axis_index("model")
     core = lax.rem(mod, 2)
     chip = mod // 2
@@ -84,7 +85,7 @@
         return pl.ds(pl.multiple_of(start, size), size)
 
     def tile(start, size):
-        return pl.ds(pl.multiple_of(start, 128), size)
+        return pl.ds(pl.multiple_of(start, 64), size)
 
     def w_copy(layer, kind):
         ssem, rsem = w_send, w_recv.at[layer, (0, 1, 2, 0, 0)[kind]]
@@ -132,6 +133,9 @@
         local_u[k].start()
     local_x.start()
     local_t.start()
+    last_at = shared_at - LAST
+    local_q = pltpu.make_async_copy(x_hbm.at[tile((1 - core) * rows_own + last_at, LAST)], sx.at[0], l_q)
+    local_q.start()
     pl.semaphore_wait(barrier, len(peers))
 
     for k in range(3):
@@ -165,6 +169,14 @@
         w_copy(k, 4).start()
 
     own_cols = span(256 * chip, 256)
+    my_cols = span(128 * mod, 128)
+
+    def q_copy(kind):
+        if kind == 2:
+            src, dst = x1.at[pl.ds(last_at, LAST)], sx.at[1]
+        else:
+            src, dst = eq.at[kind, :, span(128 * sib, 128)], se.at[kind]
+        return remote(src, dst, q_send, q_recv.at[kind], p_sib)
 
     def fold(val):
         return jnp.sum(val.reshape(val.shape[0] // 8, 8, val.shape[1]), axis=0)
@@ -260,33 +272,39 @@
         ref = dx_out.at[tile(row_base + at, size)]
         return remote(ref, ref, e_send, e_recv, p_sib)
 
-    def backward(at, size, sums, grads, idx=None, mid=None):
+    def backward(at, size, sums, grads, idx=None, mid=None, split=False):
         rows = tile(at, size)
+        b0, b1 = (eq.at[0], eq.at[1]) if split else (e0, e1)
         for j in range(2):
             residual(y2[rows, 128 * j:128 * j + 128], 2 - 2 * chip + j, rows, sums, 128 * j)
         back = (dot_nn(e2[rows, :], wbuf[2]) * inv_sigma[2]).astype(BF16).astype(F32)
         y_val = y1[rows, :]
         grad = back * jnp.where(y_val > 0, 1.0, 0.2)
         sums[2] += fold(grad * y_val)
-        e1[:size] = grad.astype(BF16)
-        add_grad(grads.at[1], e1[:size, own_cols], x1[rows, :])
-        back = (dot_nn(e1[:size], wbuf[1]) * inv_sigma[1]).astype(BF16).astype(F32)
+        b1[:size] = grad.astype(BF16)
+        if split:
+            grads[1, core] += dot_tn(b1[:size, my_cols], x1[rows, :])
+        else:
+            add_grad(grads.at[1], b1[:size, own_cols], x1[rows, :])
+        back = (dot_nn(b1[:size], wbuf[1]) * inv_sigma[1]).astype(BF16).astype(F32)
+        if mid is not None:
+            mid(1)
         y_val = y0[rows, :]
         grad = back * jnp.where(y_val > 0, 1.0, 0.2)
         sums[3] += fold(grad * y_val)
-        e0[:size] = grad.astype(BF16)
-        if mid is not None:
-            mid(1)
+        b0[:size] = grad.astype(BF16)
         if idx is None:
-            add_grad(grads.at[0], e0[:size, own_cols], xfor[tile(at - rows_own, size), :])
+            add_grad(grads.at[0], b0[:size, own_cols], xfor[tile(at - rows_own, size), :])
             if mid is not None:
                 mid(0)
         else:
             x_rows = tile(row_base + at, size)
-            add_grad(grads.at[0], e0[:size, own_cols], dx_out[x_rows, :])
-            if mid is not None:
+            if split:
+                grads[0, core] += dot_tn(b0[:size, my_cols], dx_out[x_rows, :])
                 mid(0)
-            dx_out[x_rows, :] = (dot_nn(e0[:size], wbuf[0]) * inv_sigma[0]).astype(BF16)
+            else:
+                add_grad(grads.at[0], b0[:size, own_cols], dx_out[x_rows, :])
+            dx_out[x_rows, :] = (dot_nn(b0[:size], wbuf[0]) * inv_sigma[0]).astype(BF16)
 
     row = lax.broadcasted_iota(jnp.int32, sstat.shape, 0)
 
@@ -296,24 +314,23 @@
             mine = jnp.where(row == i, jnp.sum(ref_sums(i), axis=0, keepdims=True), mine)
         return mine
 
-    def own_chunk(idx, at, size, sums, grads, mid=None):
+    def own_chunk(idx, at, size, sums, grads, mid=None, split=False):
         arrived(tbuf.at[pl.ds(0, 2), tile(at, size)], t_recv.at[idx])
-        backward(at, size, sums, grads, idx, mid)
+        if isinstance(idx, int) and idx == N_PLAIN:
+            p_copy(2).start()
+        backward(at, size, sums, grads, idx, mid, split)
 
     n_big = PLAIN[0][1]
 
     def plain_send(k):
-        if k == 0:
-            sstat[...] = gather_sums(lambda i: stat[i])
-        d_copy(k).start()
-        if k == 0:
-            s_copy.start()
+        q_copy(k).start()
 
     def plain_chunk(idx, at, size):
         if size == BIG_ROWS:
             @pl.when(idx == 0)
             def _():
                 d_copy(2).start()
+                q_copy(2).start()
 
             @pl.when(idx == 1)
             def _():
@@ -345,35 +362,43 @@
                 x2[rows, :] = leaky(y_val)
                 last_layer(rows, None)
 
-        last = isinstance(at, int) and at + size == shared_at
-        own_chunk(idx, at, size, stat, acc, plain_send if last else None)
+        last = idx == N_PLAIN - 1 if isinstance(idx, int) else False
+        own_chunk(idx, at, size, stat, acc, plain_send if last else None, last)
         dx_copy(at, size).start()
+        if isinstance(idx, int) and idx == N_PLAIN - 2:
+            d_copy(1).start()
+            d_copy(0).start()
 
     each_chunk(PLAIN, 0, 0, plain_chunk)
 
     d_copy(1).wait_recv()
-    p_own[0:128, :] = acc[1, core] + rbuf[1]
+    q_copy(2).wait_recv()
+    q_copy(1).wait_recv()
+    p_own[0:128, :] = (acc[1, core] + rbuf[1]) + dot_tn(se[1], sx[1])
+    sstat[...] = gather_sums(lambda i: stat[i])
+    s_copy.start()
+    p_copy(1).start()
     d_copy(0).wait_recv()
-    p_copy(1).start()
-    p_own[128:256, :] = acc[0, core] + rbuf[0]
-    s_copy.wait_recv()
-    p_copy(2).start()
-    p_own[256:264, :] = sstat[...] + rstat[...]
+    local_q.wait()
+    q_copy(0).wait_recv()
+    p_own[128:256, :] = (acc[0, core] + rbuf[0]) + dot_tn(se[0], sx[0])
 
     def shared_chunk(idx, at, size):
+        if idx == N_PLAIN + 1:
+            p_copy(0).start()
         own_chunk(idx, at, size, fstat.at[0], facc.at[0])
         dx_copy(at, size).start()
-
-        @pl.when(idx == N_PLAIN)
-        def _():
-            p_copy(0).start()
+        if idx == N_PLAIN:
+            s_copy.wait_recv()
+            p_own[256:264, :] = sstat[...] + rstat[...]
 
     each_chunk(SHARED, N_PLAIN, shared_at, shared_chunk)
 
     def last_send(k):
         fsend[k] = facc[0, k, 1 - core] + facc[1, k, 1 - core]
+        if k == 1:
+            fd_copy(1).start()
         if k == 0:
-            fd_copy(1).start()
             fsstat[...] = gather_sums(lambda i: fstat[0, i] + fstat[1, i])
             fd_copy(0).start()
             fs_copy.start()
@@ -403,6 +428,7 @@
     arrived(x1.at[pl.ds(0, 3 * SHARED_ROWS // 2)], f_send)
     arrived(tbuf.at[pl.ds(0, 2), pl.ds(rows_own, SHARED_ROWS)], h_send)
     arrived(y0.at[pl.ds(0, 8 * 128 + 24)], d_send)
+    arrived(x1.at[pl.ds(0, 3 * LAST // 2)], q_send)
     arrived(dx_out.at[own_rows], e_send)
     arrived(dx_out.at[own_rows], e_recv)
 
@@ -477,10 +503,11 @@
                 vm((4, 8, width), F32), vm((2, 4, 8, width), F32),
                 vm((8, width), F32), vm((8, width), F32), vm((8, width), F32), vm((8, width), F32),
                 vm((3, 8, width), F32),
+                vm((2, LAST, width), BF16), vm((2, LAST, 128), BF16), vm((2, LAST, width), BF16),
                 dma(()), dma((3, 3)), dma(()), dma(()),
                 dma(()), dma((N_PLAIN + N_SHARED,)), dma(()), dma(()), dma(()), dma(()), dma(()), dma((11,)),
-                dma(()), dma(()), dma(()), dma((N_SHARED,)),
-                dma((3,)), dma((3,)), dma(()), dma(()),
+                dma(()), dma(()), dma(()), dma((N_SHARED,)), dma(()), dma((3,)),
+                dma((3,)), dma((3,)), dma(()), dma(()), dma(()),
             ],
             compiler_params=pltpu.CompilerParams(
                 collective_id=0, has_side_effects=True, vmem_limit_bytes=55 * 2**20),

time: 69.8 us -> 68.7 us (0.984)
  Pallas kernels: 69.1 us -> 68 us
    pallas_call x1, Pallas kernels: 65.4 us -> 64.3 us  [local_step(): pl.pallas_call(functools.partial(main_kernel, 1.0 / batch_total), out_sha...]
where the time goes in v6:
time: 68.7 us; the launch traced here: 68.6 us
  Pallas kernels  68 us (99%)
    pallas_call x1, Pallas kernels, local_step(): pl.pallas_call(functools.partial(main_kernel, 1.0 / batch_total), out_sha...  64.3 us
    pallas_call x1, Pallas kernels, local_step(): pl.pallas_call(functools.partial(finish_kernel, 0.5 / batch_total), out_s...  3.67 us

profile of v6, /device:TPU:0, one launch (start us, length us, event | category | flops | bytes accessed | tf_op | source)
XLA Modules:
  0.0 68.6 jit_solution(12010909665269050731)
XLA Ops:
  0.6 64.3 %fused_step.1 = (bf16[8192,512]{1,0:T(8,128)(2,1)S(1)}, f32[392,512]{1,0:T(8,128)S(1)}, f32[16,512]{1,0:T(8,128)S(1)}) custom-call(bf16[8192,512]{1,0:T(8,128)(2,1)} %x_hbm.1, bf16[128,512]{1,0:T(8,128)(2,1)} %w0_hbm.1, bf16[128,512]{1,0:T(8,128)(2,1)} %w1_hbm.1, bf16[128,512]{1,0:T(8,128)(2,1)} %w2_hbm.1, f32[1,128]{1,0:T(1,128)} %bitcast.11, ...), custom_call_target="tpu_custom_call" | custom-call | tf_op jit(solution)/shard_map/fused_step/pallas_call | solution.py:486
  65.0 3.7 %finish.1 = (bf16[8192,512]{1,0:T(8,128)(2,1)}, f32[128,512]{1,0:T(8,128)}, f32[128,512]{1,0:T(8,128)}, f32[128,512]{1,0:T(8,128)}, f32[1,512]{1,0:T(1,128)}, /*...) custom-call(bf16[8192,512]{1,0:T(8,128)(2,1)S(1)} %get-tuple-element, ...), custom_call_target="tpu_custom_call" | custom-call | tf_op jit(solution)/shard_map/finish/pallas_call | solution.py:518

commit v7 on v6

--- a/solution.py
+++ b/solution.py
@@ -10,6 +10,8 @@
 MESH = pl.DeviceIdType.MESH
 F32 = jnp.float32
 BF16 = jnp.bfloat16
+LANE = 128
+PAIR = 2 * LANE
 FWD_ROWS = 1024
 BIG_ROWS = 512
 PLAIN = ((512, 6), (256, 1), (192, 1))
@@ -90,11 +92,11 @@
     def w_copy(layer, kind):
         ssem, rsem = w_send, w_recv.at[layer, (0, 1, 2, 0, 0)[kind]]
         if kind == 0:
-            return remote(w_hbm[layer], wbuf.at[layer, span(128 * mod, 128)], ssem, rsem, p_sib)
+            return remote(w_hbm[layer], wbuf.at[layer, span(LANE * mod, LANE)], ssem, rsem, p_sib)
         if kind == 1:
-            return remote(w_hbm[layer].at[span(64 * dat, 64)], wbuf.at[layer, span(128 * mod + 64 * dat, 64)], ssem, rsem, p_cnt)
+            return remote(w_hbm[layer].at[span(64 * dat, 64)], wbuf.at[layer, span(LANE * mod + 64 * dat, 64)], ssem, rsem, p_cnt)
         half = 1 - dat if kind == 4 else dat
-        ref = wbuf.at[layer, span(128 * cnt + 64 * half, 64)]
+        ref = wbuf.at[layer, span(LANE * cnt + 64 * half, 64)]
         return remote(ref, ref, ssem, rsem, p_y if kind == 2 else p_sib)
 
     def u_copy(kind):
@@ -123,7 +125,7 @@
     peers = (p_sib, p_cnt, p_crs, p_y, p_ys)
     for peer in peers:
         pl.semaphore_signal(barrier, inc=1, device_id=peer, device_id_type=MESH)
-    local_w = [pltpu.make_async_copy(w_hbm[k], wbuf.at[k, span(128 * mod, 128)], l_w.at[k]) for k in range(3)]
+    local_w = [pltpu.make_async_copy(w_hbm[k], wbuf.at[k, span(LANE * mod, LANE)], l_w.at[k]) for k in range(3)]
     local_u = [pltpu.make_async_copy(u_hbm[k], ubuf.at[k, mod], l_u.at[k]) for k in range(3)]
     own_rows = span(row_base, rows_own)
     local_x = pltpu.make_async_copy(x_hbm.at[own_rows], dx_out.at[own_rows], l_x)
@@ -168,14 +170,14 @@
         w_copy(k, 2).wait_recv()
         w_copy(k, 4).start()
 
-    own_cols = span(256 * chip, 256)
-    my_cols = span(128 * mod, 128)
+    own_cols = span(PAIR * chip, PAIR)
+    my_cols = span(LANE * mod, LANE)
 
     def q_copy(kind):
         if kind == 2:
             src, dst = x1.at[pl.ds(last_at, LAST)], sx.at[1]
         else:
-            src, dst = eq.at[kind, :, span(128 * sib, 128)], se.at[kind]
+            src, dst = eq.at[kind, :, span(LANE * sib, LANE)], se.at[kind]
         return remote(src, dst, q_send, q_recv.at[kind], p_sib)
 
     def fold(val):
@@ -186,24 +188,24 @@
 
     def add_grad(ref, e_val, x_val):
         part = dot_tn(e_val, x_val)
-        ref[0] += part[:128]
-        ref[1] += part[128:]
+        ref[0] += part[:LANE]
+        ref[1] += part[LANE:]
 
     def residual(y_val, slab, rows, sums, at):
         res = y_val - tbuf[slab, rows, :].astype(F32)
         grad = res * inv_batch
         if sums is not None:
-            sums[0, :, at:at + 128] += fold(res * res)
-            sums[1, :, at:at + 128] += fold(grad * y_val)
-        e2[rows, span(128 * slab, 128)] = grad.astype(BF16)
+            sums[0, :, at:at + LANE] += fold(res * res)
+            sums[1, :, at:at + LANE] += fold(grad * y_val)
+        e2[rows, span(LANE * slab, LANE)] = grad.astype(BF16)
 
     def last_layer(rows, sums):
         y_val = dot_nt(x2[rows, :], wbuf[2]) * inv_sigma[2]
         first = chip == 0
-        own = jnp.where(first, y_val[:, :256], y_val[:, 256:])
-        y2[rows, :] = jnp.where(first, y_val[:, 256:], y_val[:, :256])
+        own = jnp.where(first, y_val[:, :PAIR], y_val[:, PAIR:])
+        y2[rows, :] = jnp.where(first, y_val[:, PAIR:], y_val[:, :PAIR])
         for j in range(2):
-            residual(own[:, 128 * j:128 * j + 128], 2 * chip + j, rows, sums, 256 + 128 * j)
+            residual(own[:, LANE * j:LANE * j + LANE], 2 * chip + j, rows, sums, PAIR + LANE * j)
 
     inv_sigma = []
     for k in range(3):
@@ -216,7 +218,7 @@
         local_w[k].wait()
         if k == 0:
             arrived(ubuf.at[:, pl.ds(0, 3)], u_recv)
-        arrived(wbuf.at[k, pl.ds(0, 256)], w_recv.at[k, 0])
+        arrived(wbuf.at[k, pl.ds(0, PAIR)], w_recv.at[k, 0])
         u_row = jnp.concatenate([ubuf[k, j] for j in range(4)], axis=1)
         p_vec = jnp.sum(dot_nn(split_rows(u_row), wbuf[k]), axis=0, keepdims=True)
         norm = jnp.sqrt(jnp.sum(p_vec * p_vec, axis=1, keepdims=True))
@@ -225,7 +227,7 @@
         sigma = jnp.sqrt(jnp.sum(s_vec * s_vec, axis=1, keepdims=True))
         pack_out[k:k + 1, :] = v_vec
         srow[k] = jnp.broadcast_to(s_vec / sigma, srow.shape[1:])
-        pack_out[3 + k:4 + k, 0:128] = srow[k, 0:1, span(128 * mod, 128)]
+        pack_out[3 + k:4 + k, 0:LANE] = srow[k, 0:1, span(LANE * mod, LANE)]
         pack_out[6 + k:7 + k, :] = jnp.broadcast_to(sigma, (1, pack_out.shape[1]))
         inv = 1.0 / sigma
         inv_sigma.append(inv)
@@ -261,7 +263,7 @@
         return remote(fsend.at[k], frbuf.at[k], d_send, d_recv.at[4 + k], p_sib)
 
     def p_copy(k):
-        part = pl.ds((256, 0, 128)[k], (8, 128, 128)[k])
+        part = pl.ds((PAIR, 0, LANE)[k], (8, LANE, LANE)[k])
         return remote(p_own.at[part], p_other.at[part], d_send, d_recv.at[8 + k], p_y)
 
     s_copy = remote(sstat, rstat, d_send, d_recv.at[3], p_sib)
@@ -276,7 +278,7 @@
         rows = tile(at, size)
         b0, b1 = (eq.at[0], eq.at[1]) if split else (e0, e1)
         for j in range(2):
-            residual(y2[rows, 128 * j:128 * j + 128], 2 - 2 * chip + j, rows, sums, 128 * j)
+            residual(y2[rows, LANE * j:LANE * j + LANE], 2 - 2 * chip + j, rows, sums, LANE * j)
         back = (dot_nn(e2[rows, :], wbuf[2]) * inv_sigma[2]).astype(BF16).astype(F32)
         y_val = y1[rows, :]
         grad = back * jnp.where(y_val > 0, 1.0, 0.2)
@@ -364,24 +366,24 @@
 
         last = idx == N_PLAIN - 1 if isinstance(idx, int) else False
         own_chunk(idx, at, size, stat, acc, plain_send if last else None, last)
-        dx_copy(at, size).start()
         if isinstance(idx, int) and idx == N_PLAIN - 2:
             d_copy(1).start()
             d_copy(0).start()
+        dx_copy(at, size).start()
 
     each_chunk(PLAIN, 0, 0, plain_chunk)
 
     d_copy(1).wait_recv()
     q_copy(2).wait_recv()
     q_copy(1).wait_recv()
-    p_own[0:128, :] = (acc[1, core] + rbuf[1]) + dot_tn(se[1], sx[1])
+    p_own[0:LANE, :] = (acc[1, core] + rbuf[1]) + dot_tn(se[1], sx[1])
     sstat[...] = gather_sums(lambda i: stat[i])
     s_copy.start()
     p_copy(1).start()
     d_copy(0).wait_recv()
     local_q.wait()
     q_copy(0).wait_recv()
-    p_own[128:256, :] = (acc[0, core] + rbuf[0]) + dot_tn(se[0], sx[0])
+    p_own[LANE:PAIR, :] = (acc[0, core] + rbuf[0]) + dot_tn(se[0], sx[0])
 
     def shared_chunk(idx, at, size):
         if idx == N_PLAIN + 1:
@@ -390,7 +392,7 @@
         dx_copy(at, size).start()
         if idx == N_PLAIN:
             s_copy.wait_recv()
-            p_own[256:264, :] = sstat[...] + rstat[...]
+            p_own[PAIR:264, :] = sstat[...] + rstat[...]
 
     each_chunk(SHARED, N_PLAIN, shared_at, shared_chunk)
 
@@ -411,15 +413,15 @@
     each_chunk(SHARED, 0, rows_own, foreign_chunk)
 
     g_copy.wait_recv()
-    tot_out[256:384, :] = g_own[...] + g_other[...]
+    tot_out[PAIR:384, :] = g_own[...] + g_other[...]
     for k in range(3):
         p_copy(k).wait_recv()
     for i, k in enumerate((1, 0)):
-        part = slice(128 * i, 128 * i + 128)
+        part = slice(LANE * i, LANE * i + LANE)
         fd_copy(k).wait_recv()
         tot_out[part, :] = (p_own[part, :] + p_other[part, :]) + ((facc[0, k, core] + facc[1, k, core]) + frbuf[k])
     fs_copy.wait_recv()
-    tot_out[384:392, :] = (p_own[256:264, :] + p_other[256:264, :]) + (fsstat[...] + frstat[...])
+    tot_out[384:392, :] = (p_own[PAIR:264, :] + p_other[PAIR:264, :]) + (fsstat[...] + frstat[...])
 
     arrived(x1.at[pl.ds(0, 3 * 384)], w_send)
     arrived(ubuf.at[:, pl.ds(0, 3)], u_send)
@@ -427,7 +429,7 @@
     arrived(tbuf.at[mod, pl.ds(0, rows_own)], s_send)
     arrived(x1.at[pl.ds(0, 3 * SHARED_ROWS // 2)], f_send)
     arrived(tbuf.at[pl.ds(0, 2), pl.ds(rows_own, SHARED_ROWS)], h_send)
-    arrived(y0.at[pl.ds(0, 8 * 128 + 24)], d_send)
+    arrived(y0.at[pl.ds(0, 8 * LANE + 24)], d_send)
     arrived(x1.at[pl.ds(0, 3 * LAST // 2)], q_send)
     arrived(dx_out.at[own_rows], e_send)
     arrived(dx_out.at[own_rows], e_recv)
@@ -448,16 +450,16 @@
 
     for k, (v_out, n_out) in enumerate(((v0, n0), (v1, n1), (v2, n2))):
         out_copy(pack.at[k:k + 1, :], v_out)
-        out_copy(pack.at[3 + k:4 + k, 0:128], n_out)
-    lane = lax.broadcasted_iota(jnp.int32, (1, 128), 1)
-    row = jnp.where(lane == 0, pack[6:7, 0:128], jnp.where(lane == 1, pack[7:8, 0:128], pack[8:9, 0:128]))
+        out_copy(pack.at[3 + k:4 + k, 0:LANE], n_out)
+    lane = lax.broadcasted_iota(jnp.int32, (1, LANE), 1)
+    row = jnp.where(lane == 0, pack[6:7, 0:LANE], jnp.where(lane == 1, pack[7:8, 0:LANE], pack[8:9, 0:LANE]))
     sig_row[...] = row[:, :3]
     stats = jnp.sum(tot[384:392, :], axis=1, keepdims=True)
     loss_row[...] = loss_scale * stats[0:1]
-    for k, at in enumerate((128, 0, 256)):
+    for k, at in enumerate((LANE, 0, PAIR)):
         inv = 1.0 / pack[6 + k:7 + k, 0:1]
-        u_col = jnp.transpose(jnp.broadcast_to(pack[3 + k:4 + k, 0:128], (128, 128)))[:, 0:1]
-        grads[k] = tot[at:at + 128, :] * inv - (stats[3 - k:4 - k] * inv) * (u_col * pack[k:k + 1, :])
+        u_col = jnp.transpose(jnp.broadcast_to(pack[3 + k:4 + k, 0:LANE], (LANE, LANE)))[:, 0:1]
+        grads[k] = tot[at:at + LANE, :] * inv - (stats[3 - k:4 - k] * inv) * (u_col * pack[k:k + 1, :])
     out_copy(sig_row, sig_out)
     out_copy(loss_row, loss_out)
     for k, out in enumerate((dw0, dw1, dw2)):
@@ -490,20 +492,20 @@
             out_specs=[vmem_spec] * 3,
             scratch_shapes=[
                 vm((ext, width), BF16), vm((ext, width), BF16),
-                vm((ext, width), F32), vm((ext, width), F32), vm((ext, 256), F32),
-                vm((4, ext, 128), BF16),
+                vm((ext, width), F32), vm((ext, width), F32), vm((ext, PAIR), F32),
+                vm((4, ext, LANE), BF16),
                 vm((3, width, width), BF16),
-                vm((3, 4, 1, 128), F32),
+                vm((3, 4, 1, LANE), F32),
                 vm((ext, width), BF16), vm((BIG_ROWS, width), BF16), vm((BIG_ROWS, width), BF16),
                 vm((SHARED_ROWS, width), BF16),
-                vm((3, 2, 128, width), F32), vm((2, 2, 2, 128, width), F32),
-                vm((3, 128, width), F32), vm((2, 128, width), F32), vm((2, 128, width), F32),
-                vm((128, width), F32), vm((128, width), F32),
+                vm((3, 2, LANE, width), F32), vm((2, 2, 2, LANE, width), F32),
+                vm((3, LANE, width), F32), vm((2, LANE, width), F32), vm((2, LANE, width), F32),
+                vm((LANE, width), F32), vm((LANE, width), F32),
                 vm((264, width), F32), vm((264, width), F32),
                 vm((4, 8, width), F32), vm((2, 4, 8, width), F32),
                 vm((8, width), F32), vm((8, width), F32), vm((8, width), F32), vm((8, width), F32),
                 vm((3, 8, width), F32),
-                vm((2, LAST, width), BF16), vm((2, LAST, 128), BF16), vm((2, LAST, width), BF16),
+                vm((2, LAST, width), BF16), vm((2, LAST, LANE), BF16), vm((2, LAST, width), BF16),
                 dma(()), dma((3, 3)), dma(()), dma(()),
                 dma(()), dma((N_PLAIN + N_SHARED,)), dma(()), dma(()), dma(()), dma(()), dma(()), dma((11,)),
                 dma(()), dma(()), dma(()), dma((N_SHARED,)), dma(()), dma((3,)),
@@ -512,21 +514,21 @@
             compiler_params=pltpu.CompilerParams(
                 collective_id=0, has_side_effects=True, vmem_limit_bytes=55 * 2**20),
             name="fused_step",
-        )(x_in, w_in, w_mid, w_out, u_in.reshape(1, 128), u_mid.reshape(1, 128), u_out.reshape(1, 128), target)
+        )(x_in, w_in, w_mid, w_out, u_in.reshape(1, LANE), u_mid.reshape(1, LANE), u_out.reshape(1, LANE), target)
 
         f32 = lambda *shape: jax.ShapeDtypeStruct(shape, F32)
         finals = pl.pallas_call(
             functools.partial(finish_kernel, 0.5 / batch_total),
-            out_shape=[jax.ShapeDtypeStruct((rows, width), BF16)] + [f32(128, width)] * 3 + [f32(1, width)] * 3 + [
-                f32(1, 128)] * 3 + [f32(1, 3), f32(1, 1)],
+            out_shape=[jax.ShapeDtypeStruct((rows, width), BF16)] + [f32(LANE, width)] * 3 + [f32(1, width)] * 3 + [
+                f32(1, LANE)] * 3 + [f32(1, 3), f32(1, 1)],
             in_specs=[vmem_spec] * 3,
             out_specs=[any_spec] * 12,
-            scratch_shapes=[vm((3, 128, width), F32), vm((1, 3), F32), vm((1, 1), F32), dma((4,)), dma((11,))],
+            scratch_shapes=[vm((3, LANE, width), F32), vm((1, 3), F32), vm((1, 1), F32), dma((4,)), dma((11,))],
             compiler_params=pltpu.CompilerParams(vmem_limit_bytes=8 * 2**20),
             name="finish",
         )(dx_all, tot, pack)
         grad_x, dw0, dw1, dw2, v0, v1, v2, n0, n1, n2, sig, loss = finals
-        return (loss.reshape(1), grad_x, dw0, dw1, dw2, n0.reshape(128), n1.reshape(128), n2.reshape(128),
+        return (loss.reshape(1), grad_x, dw0, dw1, dw2, n0.reshape(LANE), n1.reshape(LANE), n2.reshape(LANE),
                 v0.reshape(width), v1.reshape(width), v2.reshape(width), sig.reshape(3))
 
     in_specs = (batch_spec, row_spec, row_spec, row_spec, vec_spec, vec_spec, vec_spec, target_spec)

time: 68.7 us -> 68.7 us (level)
  no operation moved by 1% of the time
where the time goes in v7:
time: 68.7 us; the launch traced here: 68.6 us
  Pallas kernels  68 us (99%)
    pallas_call x1, Pallas kernels, local_step(): pl.pallas_call(functools.partial(main_kernel, 1.0 / batch_total), out_sha...  64.3 us
    pallas_call x1, Pallas kernels, local_step(): pl.pallas_call(functools.partial(finish_kernel, 0.5 / batch_total), out_s...  3.67 us

profile of v7, /device:TPU:0, one launch (start us, length us, event | category | flops | bytes accessed | tf_op | source)
XLA Modules:
  0.0 68.6 jit_solution(13969694606416813443)
XLA Ops:
  0.6 64.3 %fused_step.1 = (bf16[8192,512]{1,0:T(8,128)(2,1)S(1)}, f32[392,512]{1,0:T(8,128)S(1)}, f32[16,512]{1,0:T(8,128)S(1)}) custom-call(bf16[8192,512]{1,0:T(8,128)(2,1)} %x_hbm.1, bf16[128,512]{1,0:T(8,128)(2,1)} %w0_hbm.1, bf16[128,512]{1,0:T(8,128)(2,1)} %w1_hbm.1, bf16[128,512]{1,0:T(8,128)(2,1)} %w2_hbm.1, f32[1,128]{1,0:T(1,128)} %bitcast.11, ...), custom_call_target="tpu_custom_call" | custom-call | tf_op jit(solution)/shard_map/fused_step/pallas_call | solution.py:488
  65.0 3.7 %finish.1 = (bf16[8192,512]{1,0:T(8,128)(2,1)}, f32[128,512]{1,0:T(8,128)}, f32[128,512]{1,0:T(8,128)}, f32[128,512]{1,0:T(8,128)}, f32[1,512]{1,0:T(1,128)}, /*...) custom-call(bf16[8192,512]{1,0:T(8,128)(2,1)S(1)} %get-tuple-element, ...), custom_call_target="tpu_custom_call" | custom-call | tf_op jit(solution)/shard_map/finish/pallas_call | solution.py:520

commit v8 on v7

--- a/solution.py
+++ b/solution.py
@@ -36,7 +36,8 @@
 
 def split_rows(vec):
     width = vec.shape[1]
-    high = vec.astype(BF16).astype(F32)
+    limit = float(jnp.finfo(BF16).max)
+    high = jnp.clip(vec, -limit, limit).astype(BF16).astype(F32)
     rest = vec - high
     mid = rest.astype(BF16).astype(F32)
     low = rest - mid
@@ -48,9 +49,9 @@
 def main_kernel(inv_batch, x_hbm, w0_hbm, w1_hbm, w2_hbm, u0_hbm, u1_hbm, u2_hbm, t_hbm,
                 dx_out, tot_out, pack_out,
                 x1, x2, y0, y1, y2, tbuf, wbuf, ubuf, e2, e1, e0, xfor, acc, facc, rbuf, frbuf, fsend,
-                g_own, g_other, p_own, p_other, stat, fstat, sstat, rstat, fsstat, frstat, srow, sx, se, eq,
+                g_own, g_other, p_own, p_other, stat, fstat, sstat, rstat, fsstat, frstat, srow, sx, se, eq, xstat, xb,
                 w_send, w_recv, u_send, u_recv, t_send, t_recv, s_send, s_recv, e_send, e_recv, d_send, d_recv,
-                f_send, f_recv, h_send, h_recv, q_send, q_recv, l_w, l_u, l_t, l_x, l_q):
+                f_send, f_recv, h_send, h_recv, q_send, q_recv, x_send, x_recv, l_w, l_u, l_t, l_x, l_q):
     rep, dat, mod = lax.axis_index("replica"), lax.axis_index("data"), lax.axis_index("model")
     core = lax.rem(mod, 2)
     chip = mod // 2
@@ -159,6 +160,7 @@
     acc[...] = jnp.zeros_like(acc)
     facc[...] = jnp.zeros_like(facc)
     stat[...] = jnp.zeros_like(stat)
+    xstat[...] = jnp.zeros_like(xstat)
     fstat[...] = jnp.zeros_like(fstat)
 
     def relay_x(k):
@@ -191,12 +193,12 @@
         ref[0] += part[:LANE]
         ref[1] += part[LANE:]
 
-    def residual(y_val, slab, rows, sums, at):
+    def residual(y_val, slab, rows, sums=None):
         res = y_val - tbuf[slab, rows, :].astype(F32)
         grad = res * inv_batch
         if sums is not None:
-            sums[0, :, at:at + LANE] += fold(res * res)
-            sums[1, :, at:at + LANE] += fold(grad * y_val)
+            sums[0] += fold(res * res)
+            sums[1] += fold(grad * y_val)
         e2[rows, span(LANE * slab, LANE)] = grad.astype(BF16)
 
     def last_layer(rows, sums):
@@ -205,7 +207,7 @@
         own = jnp.where(first, y_val[:, :PAIR], y_val[:, PAIR:])
         y2[rows, :] = jnp.where(first, y_val[:, PAIR:], y_val[:, :PAIR])
         for j in range(2):
-            residual(own[:, LANE * j:LANE * j + LANE], 2 * chip + j, rows, sums, PAIR + LANE * j)
+            residual(own[:, LANE * j:LANE * j + LANE], 2 * chip + j, rows, sums)
 
     inv_sigma = []
     for k in range(3):
@@ -250,7 +252,7 @@
                 y1[rows, :] = y_val
                 x2[rows, :] = leaky(y_val)
             else:
-                last_layer(rows, stat)
+                last_layer(rows, xstat)
                 add_grad(acc.at[2], e2[rows, own_cols], x2[rows, :])
             return carry
 
@@ -278,11 +280,11 @@
         rows = tile(at, size)
         b0, b1 = (eq.at[0], eq.at[1]) if split else (e0, e1)
         for j in range(2):
-            residual(y2[rows, LANE * j:LANE * j + LANE], 2 - 2 * chip + j, rows, sums, LANE * j)
+            residual(y2[rows, LANE * j:LANE * j + LANE], 2 - 2 * chip + j, rows)
         back = (dot_nn(e2[rows, :], wbuf[2]) * inv_sigma[2]).astype(BF16).astype(F32)
         y_val = y1[rows, :]
         grad = back * jnp.where(y_val > 0, 1.0, 0.2)
-        sums[2] += fold(grad * y_val)
+        sums[0] += fold(grad * y_val)
         b1[:size] = grad.astype(BF16)
         if split:
             grads[1, core] += dot_tn(b1[:size, my_cols], x1[rows, :])
@@ -293,7 +295,7 @@
             mid(1)
         y_val = y0[rows, :]
         grad = back * jnp.where(y_val > 0, 1.0, 0.2)
-        sums[3] += fold(grad * y_val)
+        sums[1] += fold(grad * y_val)
         b0[:size] = grad.astype(BF16)
         if idx is None:
             add_grad(grads.at[0], b0[:size, own_cols], xfor[tile(at - rows_own, size), :])
@@ -312,9 +314,15 @@
 
     def gather_sums(ref_sums):
         mine = jnp.zeros(sstat.shape, F32)
-        for i in range(4):
-            mine = jnp.where(row == i, jnp.sum(ref_sums(i), axis=0, keepdims=True), mine)
+        for i in range(2):
+            mine = jnp.where(row == 2 + i, jnp.sum(ref_sums(i), axis=0, keepdims=True), mine)
         return mine
+
+    first_sums = [jnp.sum(xstat[i], axis=0, keepdims=True) for i in range(2)]
+    xb[0] = jnp.where(row[:, :LANE] == 0, first_sums[0], jnp.where(row[:, :LANE] == 1, first_sums[1], 0.0))
+
+    def x_copy(k):
+        return remote(xb.at[2 * k], xb.at[2 * k + 1], x_send, x_recv.at[k], (p_sib, p_y, p_cnt)[k])
 
     def own_chunk(idx, at, size, sums, grads, mid=None, split=False):
         arrived(tbuf.at[pl.ds(0, 2), tile(at, size)], t_recv.at[idx])
@@ -333,18 +341,28 @@
             def _():
                 d_copy(2).start()
                 q_copy(2).start()
+                x_copy(0).start()
 
             @pl.when(idx == 1)
             def _():
                 d_copy(2).wait_recv()
                 g_own[...] = acc[2, core] + rbuf[2]
+                x_copy(0).wait_recv()
+                xb[2] = xb[0] + xb[1]
 
             @pl.when(idx == 2)
             def _():
                 g_copy.start()
+                x_copy(1).start()
+
+            @pl.when(idx == n_big - 3)
+            def _():
+                x_copy(1).wait_recv()
+                xb[4] = xb[2] + xb[3]
 
             @pl.when(idx == n_big - 2)
             def _():
+                x_copy(2).start()
                 arrived(x1.at[pl.ds(0, 3 * SHARED_ROWS // 2)], f_recv)
 
                 def forward_on(j, h_at, h_size):
@@ -422,6 +440,8 @@
         tot_out[part, :] = (p_own[part, :] + p_other[part, :]) + ((facc[0, k, core] + facc[1, k, core]) + frbuf[k])
     fs_copy.wait_recv()
     tot_out[384:392, :] = (p_own[PAIR:264, :] + p_other[PAIR:264, :]) + (fsstat[...] + frstat[...])
+    x_copy(2).wait_recv()
+    tot_out[384:392, :LANE] += xb[4] + xb[5]
 
     arrived(x1.at[pl.ds(0, 3 * 384)], w_send)
     arrived(ubuf.at[:, pl.ds(0, 3)], u_send)
@@ -430,6 +450,7 @@
     arrived(x1.at[pl.ds(0, 3 * SHARED_ROWS // 2)], f_send)
     arrived(tbuf.at[pl.ds(0, 2), pl.ds(rows_own, SHARED_ROWS)], h_send)
     arrived(y0.at[pl.ds(0, 8 * LANE + 24)], d_send)
+    arrived(xb.at[pl.ds(0, 3)], x_send)
     arrived(x1.at[pl.ds(0, 3 * LAST // 2)], q_send)
     arrived(dx_out.at[own_rows], e_send)
     arrived(dx_out.at[own_rows], e_recv)
@@ -502,13 +523,14 @@
                 vm((3, LANE, width), F32), vm((2, LANE, width), F32), vm((2, LANE, width), F32),
                 vm((LANE, width), F32), vm((LANE, width), F32),
                 vm((264, width), F32), vm((264, width), F32),
-                vm((4, 8, width), F32), vm((2, 4, 8, width), F32),
+                vm((2, 8, width), F32), vm((2, 2, 8, width), F32),
                 vm((8, width), F32), vm((8, width), F32), vm((8, width), F32), vm((8, width), F32),
                 vm((3, 8, width), F32),
                 vm((2, LAST, width), BF16), vm((2, LAST, LANE), BF16), vm((2, LAST, width), BF16),
+                vm((2, 8, LANE), F32), vm((6, 8, LANE), F32),
                 dma(()), dma((3, 3)), dma(()), dma(()),
                 dma(()), dma((N_PLAIN + N_SHARED,)), dma(()), dma(()), dma(()), dma(()), dma(()), dma((11,)),
-                dma(()), dma(()), dma(()), dma((N_SHARED,)), dma(()), dma((3,)),
+                dma(()), dma(()), dma(()), dma((N_SHARED,)), dma(()), dma((3,)), dma(()), dma((3,)),
                 dma((3,)), dma((3,)), dma(()), dma(()), dma(()),
             ],
             compiler_params=pltpu.CompilerParams(

time: 68.7 us -> 68.8 us (level)
  no operation moved by 1% of the time
where the time goes in v8:
time: 68.8 us; the launch traced here: 68.7 us
  Pallas kernels  68 us (99%)
    pallas_call x1, Pallas kernels, local_step(): pl.pallas_call(functools.partial(main_kernel, 1.0 / batch_total), out_sha...  64.3 us
    pallas_call x1, Pallas kernels, local_step(): pl.pallas_call(functools.partial(finish_kernel, 0.5 / batch_total), out_s...  3.67 us

profile of v8, /device:TPU:0, one launch (start us, length us, event | category | flops | bytes accessed | tf_op | source)
XLA Modules:
  0.0 68.7 jit_solution(592876779496047132)
XLA Ops:
  0.6 64.3 %fused_step.1 = (bf16[8192,512]{1,0:T(8,128)(2,1)S(1)}, f32[392,512]{1,0:T(8,128)S(1)}, f32[16,512]{1,0:T(8,128)S(1)}) custom-call(bf16[8192,512]{1,0:T(8,128)(2,1)} %x_hbm.1, bf16[128,512]{1,0:T(8,128)(2,1)} %w0_hbm.1, bf16[128,512]{1,0:T(8,128)(2,1)} %w1_hbm.1, bf16[128,512]{1,0:T(8,128)(2,1)} %w2_hbm.1, f32[1,128]{1,0:T(1,128)} %bitcast.11, ...), custom_call_target="tpu_custom_call" | custom-call | tf_op jit(solution)/shard_map/fused_step/pallas_call | solution.py:509
  65.0 3.7 %finish.1 = (bf16[8192,512]{1,0:T(8,128)(2,1)}, f32[128,512]{1,0:T(8,128)}, f32[128,512]{1,0:T(8,128)}, f32[128,512]{1,0:T(8,128)}, f32[1,512]{1,0:T(1,128)}, /*...) custom-call(bf16[8192,512]{1,0:T(8,128)(2,1)S(1)} %get-tuple-element, ...), custom_call_target="tpu_custom_call" | custom-call | tf_op jit(solution)/shard_map/finish/pallas_call | solution.py:542

commit v9 on v8

--- a/solution.py
+++ b/solution.py
@@ -355,14 +355,8 @@
                 g_copy.start()
                 x_copy(1).start()
 
-            @pl.when(idx == n_big - 3)
-            def _():
-                x_copy(1).wait_recv()
-                xb[4] = xb[2] + xb[3]
-
             @pl.when(idx == n_big - 2)
             def _():
-                x_copy(2).start()
                 arrived(x1.at[pl.ds(0, 3 * SHARED_ROWS // 2)], f_recv)
 
                 def forward_on(j, h_at, h_size):
@@ -382,11 +376,15 @@
                 x2[rows, :] = leaky(y_val)
                 last_layer(rows, None)
 
+        if isinstance(idx, int) and idx == n_big:
+            x_copy(1).wait_recv()
+            xb[4] = xb[2] + xb[3]
         last = idx == N_PLAIN - 1 if isinstance(idx, int) else False
         own_chunk(idx, at, size, stat, acc, plain_send if last else None, last)
         if isinstance(idx, int) and idx == N_PLAIN - 2:
             d_copy(1).start()
             d_copy(0).start()
+            x_copy(2).start()
         dx_copy(at, size).start()
 
     each_chunk(PLAIN, 0, 0, plain_chunk)

time: 68.8 us -> 68.7 us (level)
  no operation moved by 1% of the time
where the time goes in v9:
time: 68.7 us; the launch traced here: 68.6 us
  Pallas kernels  68 us (99%)
    pallas_call x1, Pallas kernels, local_step(): pl.pallas_call(functools.partial(main_kernel, 1.0 / batch_total), out_sha...  64.3 us
    pallas_call x1, Pallas kernels, local_step(): pl.pallas_call(functools.partial(finish_kernel, 0.5 / batch_total), out_s...  3.67 us

profile of v9, /device:TPU:0, one launch (start us, length us, event | category | flops | bytes accessed | tf_op | source)
XLA Modules:
  0.0 68.6 jit_solution(4399139386872920764)
XLA Ops:
  0.6 64.3 %fused_step.1 = (bf16[8192,512]{1,0:T(8,128)(2,1)S(1)}, f32[392,512]{1,0:T(8,128)S(1)}, f32[16,512]{1,0:T(8,128)S(1)}) custom-call(bf16[8192,512]{1,0:T(8,128)(2,1)} %x_hbm.1, bf16[128,512]{1,0:T(8,128)(2,1)} %w0_hbm.1, bf16[128,512]{1,0:T(8,128)(2,1)} %w1_hbm.1, bf16[128,512]{1,0:T(8,128)(2,1)} %w2_hbm.1, f32[1,128]{1,0:T(1,128)} %bitcast.11, ...), custom_call_target="tpu_custom_call" | custom-call | tf_op jit(solution)/shard_map/fused_step/pallas_call | solution.py:507
  65.0 3.7 %finish.1 = (bf16[8192,512]{1,0:T(8,128)(2,1)}, f32[128,512]{1,0:T(8,128)}, f32[128,512]{1,0:T(8,128)}, f32[128,512]{1,0:T(8,128)}, f32[1,512]{1,0:T(1,128)}, /*...) custom-call(bf16[8192,512]{1,0:T(8,128)(2,1)S(1)} %get-tuple-element, ...), custom_call_target="tpu_custom_call" | custom-call | tf_op jit(solution)/shard_map/finish/pallas_call | solution.py:540

commit v10 on v9

--- a/solution.py
+++ b/solution.py
@@ -126,8 +126,8 @@
     peers = (p_sib, p_cnt, p_crs, p_y, p_ys)
     for peer in peers:
         pl.semaphore_signal(barrier, inc=1, device_id=peer, device_id_type=MESH)
-    local_w = [pltpu.make_async_copy(w_hbm[k], wbuf.at[k, span(LANE * mod, LANE)], l_w.at[k]) for k in range(3)]
-    local_u = [pltpu.make_async_copy(u_hbm[k], ubuf.at[k, mod], l_u.at[k]) for k in range(3)]
+    local_w = [pltpu.make_async_copy(w_hbm[k], wbuf.at[k, span(LANE * mod, LANE)], l_w) for k in range(3)]
+    local_u = [pltpu.make_async_copy(u_hbm[k], ubuf.at[k, mod], l_u) for k in range(3)]
     own_rows = span(row_base, rows_own)
     local_x = pltpu.make_async_copy(x_hbm.at[own_rows], dx_out.at[own_rows], l_x)
     local_t = pltpu.make_async_copy(t_hbm.at[own_rows], tbuf.at[mod, pl.ds(0, rows_own)], l_t)
@@ -145,8 +145,7 @@
         w_copy(k, 1).start()
         w_copy(k, 0).start()
 
-    for copy in local_u:
-        copy.wait()
+    arrived(ubuf.at[:, mod], l_u)
     for kind in range(3):
         u_copy(kind).start()
 
@@ -217,8 +216,8 @@
     relay_y(0)
     relay_y(1)
     for k in range(3):
-        local_w[k].wait()
         if k == 0:
+            arrived(wbuf.at[:, span(LANE * mod, LANE)], l_w)
             arrived(ubuf.at[:, pl.ds(0, 3)], u_recv)
         arrived(wbuf.at[k, pl.ds(0, PAIR)], w_recv.at[k, 0])
         u_row = jnp.concatenate([ubuf[k, j] for j in range(4)], axis=1)
@@ -262,11 +261,11 @@
         return remote(acc.at[k, 1 - core], rbuf.at[k], d_send, d_recv.at[k], p_sib)
 
     def fd_copy(k):
-        return remote(fsend.at[k], frbuf.at[k], d_send, d_recv.at[4 + k], p_sib)
+        return remote(fsend.at[k], frbuf.at[k], d_send, d_recv.at[4], p_sib)
 
     def p_copy(k):
         part = pl.ds((PAIR, 0, LANE)[k], (8, LANE, LANE)[k])
-        return remote(p_own.at[part], p_other.at[part], d_send, d_recv.at[8 + k], p_y)
+        return remote(p_own.at[part], p_other.at[part], d_send, d_recv.at[5], p_y)
 
     s_copy = remote(sstat, rstat, d_send, d_recv.at[3], p_sib)
     fs_copy = remote(fsstat, frstat, d_send, d_recv.at[6], p_sib)
@@ -430,11 +429,10 @@
 
     g_copy.wait_recv()
     tot_out[PAIR:384, :] = g_own[...] + g_other[...]
-    for k in range(3):
-        p_copy(k).wait_recv()
+    arrived(p_other, d_recv.at[5])
+    arrived(frbuf, d_recv.at[4])
     for i, k in enumerate((1, 0)):
         part = slice(LANE * i, LANE * i + LANE)
-        fd_copy(k).wait_recv()
         tot_out[part, :] = (p_own[part, :] + p_other[part, :]) + ((facc[0, k, core] + facc[1, k, core]) + frbuf[k])
     fs_copy.wait_recv()
     tot_out[384:392, :] = (p_own[PAIR:264, :] + p_other[PAIR:264, :]) + (fsstat[...] + frstat[...])
@@ -527,9 +525,9 @@
                 vm((2, LAST, width), BF16), vm((2, LAST, LANE), BF16), vm((2, LAST, width), BF16),
                 vm((2, 8, LANE), F32), vm((6, 8, LANE), F32),
                 dma(()), dma((3, 3)), dma(()), dma(()),
-                dma(()), dma((N_PLAIN + N_SHARED,)), dma(()), dma(()), dma(()), dma(()), dma(()), dma((11,)),
+                dma(()), dma((N_PLAIN + N_SHARED,)), dma(()), dma(()), dma(()), dma(()), dma(()), dma((8,)),
                 dma(()), dma(()), dma(()), dma((N_SHARED,)), dma(()), dma((3,)), dma(()), dma((3,)),
-                dma((3,)), dma((3,)), dma(()), dma(()), dma(()),
+                dma(()), dma(()), dma(()), dma(()), dma(()),
             ],
             compiler_params=pltpu.CompilerParams(
                 collective_id=0, has_side_effects=True, vmem_limit_bytes=55 * 2**20),

time: 68.7 us -> 68.7 us (level)
  no operation moved by 1% of the time
where the time goes in v10:
time: 68.7 us; the launch traced here: 68.6 us
  Pallas kernels  67.9 us (99%)
    pallas_call x1, Pallas kernels, local_step(): pl.pallas_call(functools.partial(main_kernel, 1.0 / batch_total), out_sha...  64.3 us
    pallas_call x1, Pallas kernels, local_step(): pl.pallas_call(functools.partial(finish_kernel, 0.5 / batch_total), out_s...  3.67 us

profile of v10, /device:TPU:0, one launch (start us, length us, event | category | flops | bytes accessed | tf_op | source)
XLA Modules:
  0.0 68.6 jit_solution(14480675194856225490)
XLA Ops:
  0.6 64.3 %fused_step.1 = (bf16[8192,512]{1,0:T(8,128)(2,1)S(1)}, f32[392,512]{1,0:T(8,128)S(1)}, f32[16,512]{1,0:T(8,128)S(1)}) custom-call(bf16[8192,512]{1,0:T(8,128)(2,1)} %x_hbm.1, bf16[128,512]{1,0:T(8,128)(2,1)} %w0_hbm.1, bf16[128,512]{1,0:T(8,128)(2,1)} %w1_hbm.1, bf16[128,512]{1,0:T(8,128)(2,1)} %w2_hbm.1, f32[1,128]{1,0:T(1,128)} %bitcast.11, ...), custom_call_target="tpu_custom_call" | custom-call | tf_op jit(solution)/shard_map/fused_step/pallas_call | solution.py:505
  64.9 3.7 %finish.1 = (bf16[8192,512]{1,0:T(8,128)(2,1)}, f32[128,512]{1,0:T(8,128)}, f32[128,512]{1,0:T(8,128)}, f32[128,512]{1,0:T(8,128)}, f32[1,512]{1,0:T(1,128)}, /*...) custom-call(bf16[8192,512]{1,0:T(8,128)(2,1)S(1)} %get-tuple-element, ...), custom_call_target="tpu_custom_call" | custom-call | tf_op jit(solution)/shard_map/finish/pallas_call | solution.py:538

commit v11 on v10

--- a/solution.py
+++ b/solution.py
@@ -50,8 +50,8 @@
                 dx_out, tot_out, pack_out,
                 x1, x2, y0, y1, y2, tbuf, wbuf, ubuf, e2, e1, e0, xfor, acc, facc, rbuf, frbuf, fsend,
                 g_own, g_other, p_own, p_other, stat, fstat, sstat, rstat, fsstat, frstat, srow, sx, se, eq, xstat, xb,
-                w_send, w_recv, u_send, u_recv, t_send, t_recv, s_send, s_recv, e_send, e_recv, d_send, d_recv,
-                f_send, f_recv, h_send, h_recv, q_send, q_recv, x_send, x_recv, l_w, l_u, l_t, l_x, l_q):
+                w_send, w_recv, u_send, u_recv, t_recv, s_recv, e_recv, d_send, d_recv,
+                f_recv, h_recv, q_recv, x_send, x_recv, l_w, l_u, l_x, l_q):
     rep, dat, mod = lax.axis_index("replica"), lax.axis_index("data"), lax.axis_index("model")
     core = lax.rem(mod, 2)
     chip = mod // 2
@@ -107,7 +107,7 @@
     def t_copy(kind, idx, at, size):
         other_core = core if kind == 0 else 1 - core
         return remote(t_hbm.at[tile(other_core * rows_own + at, size)], tbuf.at[mod, tile(at, size)],
-                      t_send, t_recv.at[idx], p_cnt if kind == 0 else p_crs)
+                      w_send, t_recv.at[idx], p_cnt if kind == 0 else p_crs)
 
     def f_copy(kind):
         if kind == 0:
@@ -116,11 +116,11 @@
             other_core = core if kind == 1 else 1 - core
             src = t_hbm.at[tile(other_core * rows_own + shared_at, SHARED_ROWS)]
             dst, peer = tbuf.at[mod, tile(rows_own, SHARED_ROWS)], p_y if kind == 1 else p_ys
-        return remote(src, dst, f_send, f_recv, peer)
+        return remote(src, dst, w_send, f_recv, peer)
 
     def h_copy(kind, idx, at, size):
         ref = tbuf.at[mod if kind == 0 else sib, tile(at, size)]
-        return remote(ref, ref, h_send, h_recv.at[idx], p_cnt)
+        return remote(ref, ref, w_send, h_recv.at[idx], p_cnt)
 
     barrier = pltpu.get_barrier_semaphore()
     peers = (p_sib, p_cnt, p_crs, p_y, p_ys)
@@ -130,7 +130,7 @@
     local_u = [pltpu.make_async_copy(u_hbm[k], ubuf.at[k, mod], l_u) for k in range(3)]
     own_rows = span(row_base, rows_own)
     local_x = pltpu.make_async_copy(x_hbm.at[own_rows], dx_out.at[own_rows], l_x)
-    local_t = pltpu.make_async_copy(t_hbm.at[own_rows], tbuf.at[mod, pl.ds(0, rows_own)], l_t)
+    local_t = pltpu.make_async_copy(t_hbm.at[own_rows], tbuf.at[mod, pl.ds(0, rows_own)], s_recv)
     for k in range(3):
         local_w[k].start()
         local_u[k].start()
@@ -154,7 +154,7 @@
         t_copy(1, idx, at, size).start()
 
     each_chunk(PLAIN + SHARED, 0, 0, start_targets)
-    t_sib = remote(t_hbm.at[span((1 - core) * rows_own, rows_own)], tbuf.at[mod, pl.ds(0, rows_own)], s_send, s_recv, p_sib)
+    t_sib = remote(t_hbm.at[span((1 - core) * rows_own, rows_own)], tbuf.at[mod, pl.ds(0, rows_own)], w_send, s_recv, p_sib)
     t_sib.start()
     acc[...] = jnp.zeros_like(acc)
     facc[...] = jnp.zeros_like(facc)
@@ -179,7 +179,7 @@
             src, dst = x1.at[pl.ds(last_at, LAST)], sx.at[1]
         else:
             src, dst = eq.at[kind, :, span(LANE * sib, LANE)], se.at[kind]
-        return remote(src, dst, q_send, q_recv.at[kind], p_sib)
+        return remote(src, dst, w_send, q_recv.at[kind], p_sib)
 
     def fold(val):
         return jnp.sum(val.reshape(val.shape[0] // 8, 8, val.shape[1]), axis=0)
@@ -237,8 +237,7 @@
         if k == 0:
             local_x.wait()
         if k == 2:
-            local_t.wait()
-            t_sib.wait_recv()
+            arrived(tbuf.at[pl.ds(0, 2), pl.ds(0, rows_own)], s_recv)
 
         def forward(c, carry, k=k, inv=inv):
             rows = span(c * FWD_ROWS, FWD_ROWS)
@@ -273,7 +272,7 @@
 
     def dx_copy(at, size):
         ref = dx_out.at[tile(row_base + at, size)]
-        return remote(ref, ref, e_send, e_recv, p_sib)
+        return remote(ref, ref, d_send, e_recv, p_sib)
 
     def backward(at, size, sums, grads, idx=None, mid=None, split=False):
         rows = tile(at, size)
@@ -439,16 +438,11 @@
     x_copy(2).wait_recv()
     tot_out[384:392, :LANE] += xb[4] + xb[5]
 
-    arrived(x1.at[pl.ds(0, 3 * 384)], w_send)
+    sent_rows = 3 * 384 + 2 * SHARED_ROWS + 3 * LAST // 2 + 3 * rows_own // 4
+    arrived(dx_out.at[pl.ds(0, sent_rows)], w_send)
     arrived(ubuf.at[:, pl.ds(0, 3)], u_send)
-    arrived(t_hbm, t_send)
-    arrived(tbuf.at[mod, pl.ds(0, rows_own)], s_send)
-    arrived(x1.at[pl.ds(0, 3 * SHARED_ROWS // 2)], f_send)
-    arrived(tbuf.at[pl.ds(0, 2), pl.ds(rows_own, SHARED_ROWS)], h_send)
-    arrived(y0.at[pl.ds(0, 8 * LANE + 24)], d_send)
+    arrived(dx_out.at[pl.ds(0, rows_own + 2 * (8 * LANE + 24))], d_send)
     arrived(xb.at[pl.ds(0, 3)], x_send)
-    arrived(x1.at[pl.ds(0, 3 * LAST // 2)], q_send)
-    arrived(dx_out.at[own_rows], e_send)
     arrived(dx_out.at[own_rows], e_recv)
 
 
@@ -525,9 +519,9 @@
                 vm((2, LAST, width), BF16), vm((2, LAST, LANE), BF16), vm((2, LAST, width), BF16),
                 vm((2, 8, LANE), F32), vm((6, 8, LANE), F32),
                 dma(()), dma((3, 3)), dma(()), dma(()),
-                dma(()), dma((N_PLAIN + N_SHARED,)), dma(()), dma(()), dma(()), dma(()), dma(()), dma((8,)),
-                dma(()), dma(()), dma(()), dma((N_SHARED,)), dma(()), dma((3,)), dma(()), dma((3,)),
-                dma(()), dma(()), dma(()), dma(()), dma(()),
+                dma((N_PLAIN + N_SHARED,)), dma(()), dma(()), dma(()), dma((8,)),
+                dma(()), dma((N_SHARED,)), dma((3,)), dma(()), dma((3,)),
+                dma(()), dma(()), dma(()), dma(()),
             ],
             compiler_params=pltpu.CompilerParams(
                 collective_id=0, has_side_effects=True, vmem_limit_bytes=55 * 2**20),

time: 68.7 us -> 68.6 us (level)
  no operation moved by 1% of the time
where the time goes in v11:
time: 68.6 us; the launch traced here: 68.5 us
  Pallas kernels  67.9 us (99%)
    pallas_call x1, Pallas kernels, local_step(): pl.pallas_call(functools.partial(main_kernel, 1.0 / batch_total), out_sha...  64.2 us
    pallas_call x1, Pallas kernels, local_step(): pl.pallas_call(functools.partial(finish_kernel, 0.5 / batch_total), out_s...  3.67 us

profile of v11, /device:TPU:0, one launch (start us, length us, event | category | flops | bytes accessed | tf_op | source)
XLA Modules:
  0.0 68.5 jit_solution(1937685584601575820)
XLA Ops:
  0.6 64.2 %fused_step.1 = (bf16[8192,512]{1,0:T(8,128)(2,1)S(1)}, f32[392,512]{1,0:T(8,128)S(1)}, f32[16,512]{1,0:T(8,128)S(1)}) custom-call(bf16[8192,512]{1,0:T(8,128)(2,1)} %x_hbm.1, bf16[128,512]{1,0:T(8,128)(2,1)} %w0_hbm.1, bf16[128,512]{1,0:T(8,128)(2,1)} %w1_hbm.1, bf16[128,512]{1,0:T(8,128)(2,1)} %w2_hbm.1, f32[1,128]{1,0:T(1,128)} %bitcast.11, ...), custom_call_target="tpu_custom_call" | custom-call | tf_op jit(solution)/shard_map/fused_step/pallas_call | solution.py:499
  64.8 3.7 %finish.1 = (bf16[8192,512]{1,0:T(8,128)(2,1)}, f32[128,512]{1,0:T(8,128)}, f32[128,512]{1,0:T(8,128)}, f32[128,512]{1,0:T(8,128)}, f32[1,512]{1,0:T(1,128)}, /*...) custom-call(bf16[8192,512]{1,0:T(8,128)(2,1)S(1)} %get-tuple-element, ...), custom_call_target="tpu_custom_call" | custom-call | tf_op jit(solution)/shard_map/finish/pallas_call | solution.py:532

commit v12 on v11

--- a/solution.py
+++ b/solution.py
@@ -267,8 +267,8 @@
         return remote(p_own.at[part], p_other.at[part], d_send, d_recv.at[5], p_y)
 
     s_copy = remote(sstat, rstat, d_send, d_recv.at[3], p_sib)
-    fs_copy = remote(fsstat, frstat, d_send, d_recv.at[6], p_sib)
-    g_copy = remote(g_own, g_other, d_send, d_recv.at[7], p_y)
+    fs_copy = remote(fsstat, frstat, d_send, d_recv.at[4], p_sib)
+    g_copy = remote(g_own, g_other, d_send, d_recv.at[5], p_y)
 
     def dx_copy(at, size):
         ref = dx_out.at[tile(row_base + at, size)]
@@ -426,14 +426,12 @@
 
     each_chunk(SHARED, 0, rows_own, foreign_chunk)
 
-    g_copy.wait_recv()
+    arrived(y0.at[pl.ds(0, 392)], d_recv.at[5])
     tot_out[PAIR:384, :] = g_own[...] + g_other[...]
-    arrived(p_other, d_recv.at[5])
-    arrived(frbuf, d_recv.at[4])
+    arrived(y0.at[pl.ds(0, 264)], d_recv.at[4])
     for i, k in enumerate((1, 0)):
         part = slice(LANE * i, LANE * i + LANE)
         tot_out[part, :] = (p_own[part, :] + p_other[part, :]) + ((facc[0, k, core] + facc[1, k, core]) + frbuf[k])
-    fs_copy.wait_recv()
     tot_out[384:392, :] = (p_own[PAIR:264, :] + p_other[PAIR:264, :]) + (fsstat[...] + frstat[...])
     x_copy(2).wait_recv()
     tot_out[384:392, :LANE] += xb[4] + xb[5]
@@ -519,7 +517,7 @@
                 vm((2, LAST, width), BF16), vm((2, LAST, LANE), BF16), vm((2, LAST, width), BF16),
                 vm((2, 8, LANE), F32), vm((6, 8, LANE), F32),
                 dma(()), dma((3, 3)), dma(()), dma(()),
-                dma((N_PLAIN + N_SHARED,)), dma(()), dma(()), dma(()), dma((8,)),
+                dma((N_PLAIN + N_SHARED,)), dma(()), dma(()), dma(()), dma((6,)),
                 dma(()), dma((N_SHARED,)), dma((3,)), dma(()), dma((3,)),
                 dma(()), dma(()), dma(()), dma(()),
             ],

time: 68.6 us -> 68.6 us (level)
  no operation moved by 1% of the time
where the time goes in v12:
time: 68.6 us; the launch traced here: 68.5 us
  Pallas kernels  67.9 us (99%)
    pallas_call x1, Pallas kernels, local_step(): pl.pallas_call(functools.partial(main_kernel, 1.0 / batch_total), out_sha...  64.2 us
    pallas_call x1, Pallas kernels, local_step(): pl.pallas_call(functools.partial(finish_kernel, 0.5 / batch_total), out_s...  3.67 us

profile of v12, /device:TPU:0, one launch (start us, length us, event | category | flops | bytes accessed | tf_op | source)
XLA Modules:
  0.0 68.5 jit_solution(13352421555355555818)
XLA Ops:
  0.6 64.2 %fused_step.1 = (bf16[8192,512]{1,0:T(8,128)(2,1)S(1)}, f32[392,512]{1,0:T(8,128)S(1)}, f32[16,512]{1,0:T(8,128)S(1)}) custom-call(bf16[8192,512]{1,0:T(8,128)(2,1)} %x_hbm.1, bf16[128,512]{1,0:T(8,128)(2,1)} %w0_hbm.1, bf16[128,512]{1,0:T(8,128)(2,1)} %w1_hbm.1, bf16[128,512]{1,0:T(8,128)(2,1)} %w2_hbm.1, f32[1,128]{1,0:T(1,128)} %bitcast.11, ...), custom_call_target="tpu_custom_call" | custom-call | tf_op jit(solution)/shard_map/fused_step/pallas_call | solution.py:497
  64.8 3.7 %finish.1 = (bf16[8192,512]{1,0:T(8,128)(2,1)}, f32[128,512]{1,0:T(8,128)}, f32[128,512]{1,0:T(8,128)}, f32[128,512]{1,0:T(8,128)}, f32[1,512]{1,0:T(1,128)}, /*...) custom-call(bf16[8192,512]{1,0:T(8,128)(2,1)S(1)} %get-tuple-element, ...), custom_call_target="tpu_custom_call" | custom-call | tf_op jit(solution)/shard_map/finish/pallas_call | solution.py:530
